TPU v7x, 512 devices: a whole 4x8x8 slice. The times are simulated.
512 devices in a mesh: group: 16 (over z, core), panel: 32 (over x, y).
Axes of the slice: x: 4, y: 8, z: 8, core: 2. Of those that a mesh axis runs over, the one named last changes fastest.
Arguments:
- source_matrix_tiles: bfloat16 [2, 192, 4, 4096], P(None, 'group', None, 'panel'), may hold values from -6 to 6
- second_operand_encoded: bfloat16 [32, 4096, 2, 4096], P('group', None, None, 'panel'), may hold values from -0.5 to 0.5
- responding_nodes: int32 [19], replicated, may hold values from 0 to 31, as said below
Outputs:
- c_blocks: float32 [2, 192, 2, 4096], P(None, 'group', None, 'panel')
Inputs may be any that keep to these rules, and one draw needn't show every extreme that they name: `responding_nodes`: 19 distinct point indices in ascending order; of the points 2 j and 2 j + 1, at least one is listed.
All inputs are finite; a program needn't handle non-finite values.
Results may differ from a plain program's by a relative error of at most 0.0029.
Values may be sent and summed in bfloat16 or wider, within the bound.
No kernel may reach another device: no remote copies, remote signals or barrier semaphores. Data moves between devices by JAX's collectives and lax.ppermute only.
A program may use at most 64 MiB of HBM per device.

v0:
```python
import math

import jax
import jax.numpy as jnp
from jax import lax
from jax.sharding import Mesh
from jax.sharding import PartitionSpec as P

NODE_NUMBER = 32
PANEL = ("panel_0", "panel_1")


TWO_PI_RADIANS = 2.0 * math.pi


def joined_along(parts, dim):
    shape = list(parts.shape[1:])
    shape[dim] *= parts.shape[0]
    return jnp.moveaxis(parts, 0, dim).reshape(shape)


def gather_in_order(shard, axes, turns):
    parts = shard
    for k in turns:
        parts = lax.all_gather(parts, axes[k])
    done = turns[::-1]
    back = [done.index(k) for k in range(len(axes))]
    parts = parts.transpose(*back, *range(len(axes), parts.ndim))
    return parts.reshape(-1, *shard.shape)


def gather_axes(shard, axes, turns, dim):
    return joined_along(gather_in_order(shard, axes, turns), dim)


def point_trig(node_phases):
    exponent = (
        jnp.arange(4, dtype=jnp.float32)[None, :] + 8.0 * jnp.arange(2, dtype=jnp.float32)[:, None]
    )
    phase = node_phases[:, None, None] * exponent[None]
    return jnp.stack([jnp.cos(phase), jnp.sin(phase)], axis=1)


def recovery_coefficients(responding_nodes):
    responder_number = responding_nodes.shape[0]
    grid_index = jnp.arange(NODE_NUMBER, dtype=jnp.int32)
    grid_angle = TWO_PI_RADIANS * grid_index.astype(jnp.float32) / NODE_NUMBER
    node_angle = TWO_PI_RADIANS * responding_nodes.astype(jnp.float32) / NODE_NUMBER
    diff_real = jnp.cos(grid_angle)[None, :] - jnp.cos(node_angle)[:, None]
    diff_imag = jnp.sin(grid_angle)[None, :] - jnp.sin(node_angle)[:, None]
    ranks = jnp.arange(responder_number, dtype=jnp.int32)
    itself = (ranks[:, None] == ranks[None, :])[:, :, None]
    factor_real = jnp.where(itself, jnp.float32(1.0), diff_real[None])
    factor_imag = jnp.where(itself, jnp.float32(0.0), diff_imag[None])
    padded_width = 1 << (responder_number - 1).bit_length()
    extra = padded_width - responder_number
    factor_real = jnp.concatenate(
        [factor_real, jnp.ones((responder_number, extra, NODE_NUMBER), jnp.float32)], axis=1
    )
    factor_imag = jnp.concatenate(
        [factor_imag, jnp.zeros((responder_number, extra, NODE_NUMBER), jnp.float32)], axis=1
    )
    while factor_real.shape[1] > 1:
        middle = factor_real.shape[1] // 2
        left_real, right_real = (factor_real[:, :middle], factor_real[:, middle:])
        left_imag, right_imag = (factor_imag[:, :middle], factor_imag[:, middle:])
        factor_real = left_real * right_real - left_imag * right_imag
        factor_imag = left_real * right_imag + left_imag * right_real
    sample_real = factor_real[:, 0]
    sample_imag = factor_imag[:, 0]
    wanted = 3.0 + 4.0 * jnp.arange(4, dtype=jnp.float32)
    table_angle = -grid_angle[:, None] * wanted[None, :]
    table_cos = jnp.cos(table_angle)
    table_sin = jnp.sin(table_angle)
    highest = lax.Precision.HIGHEST
    numer_real = (
        jnp.dot(sample_real, table_cos, precision=highest)
        - jnp.dot(sample_imag, table_sin, precision=highest)
    ) / NODE_NUMBER
    numer_imag = (
        jnp.dot(sample_real, table_sin, precision=highest)
        + jnp.dot(sample_imag, table_cos, precision=highest)
    ) / NODE_NUMBER
    onehot = (responding_nodes[:, None] == grid_index[None, :]).astype(jnp.float32)
    denom_real = jnp.sum(onehot * sample_real, axis=1)
    denom_imag = jnp.sum(onehot * sample_imag, axis=1)
    magnitude = denom_real * denom_real + denom_imag * denom_imag
    coefficient_actual = (
        numer_real * denom_real[:, None] + numer_imag * denom_imag[:, None]
    ) / magnitude[:, None]
    coefficient_image = (
        numer_imag * denom_real[:, None] - numer_real * denom_imag[:, None]
    ) / magnitude[:, None]
    return (coefficient_actual, coefficient_image)


def weighted_slots(position_actual, position_image, real_part, imag_part):
    responder_number = position_actual.shape[0]
    output_matrix = jnp.einsum(
        "qil,qrn->irln",
        position_actual.reshape(responder_number, 2, 2),
        real_part,
        precision=lax.Precision.HIGHEST,
    )
    return output_matrix - jnp.einsum(
        "qil,qrn->irln",
        position_image.reshape(responder_number, 2, 2),
        imag_part,
        precision=lax.Precision.HIGHEST,
    )


def shards(source_matrix_tiles, second_operand_encoded, responding_nodes):
    coefficient_actual, coefficient_image = recovery_coefficients(responding_nodes)
    here = second_operand_encoded.shape[0]
    quarter = second_operand_encoded.shape[1]
    half_local = second_operand_encoded.shape[3]
    point_selector = (
        responding_nodes[:, None] == jnp.arange(NODE_NUMBER, dtype=jnp.int32)[None, :]
    ).astype(jnp.float32)
    every_real = jnp.dot(point_selector.T, coefficient_actual, precision=lax.Precision.HIGHEST)
    every_imag = jnp.dot(point_selector.T, coefficient_image, precision=lax.Precision.HIGHEST)
    shares_flat = second_operand_encoded.reshape(here, quarter, 2 * half_local)
    trig_every = point_trig(
        TWO_PI_RADIANS * jnp.arange(NODE_NUMBER, dtype=jnp.float32) / NODE_NUMBER
    )
    coded_every = jnp.einsum(
        "irkn,qcik->qcrn",
        source_matrix_tiles.astype(jnp.float32),
        trig_every,
        precision=lax.Precision.HIGHEST,
    ).astype(jnp.bfloat16)
    coded_here = lax.all_to_all(coded_every, "group", split_axis=0, concat_axis=2, tiled=True)
    products = jnp.einsum(
        "qcrk,qkn->qcrn",
        gather_axes(coded_here, PANEL, (0, 1), 3),
        shares_flat,
        preferred_element_type=jnp.float32,
    )
    real_part = products[:, 0, :, :half_local] - products[:, 1, :, half_local:]
    imag_part = products[:, 0, :, half_local:] + products[:, 1, :, :half_local]
    planes = jnp.stack([real_part, imag_part], axis=1)
    received = lax.all_to_all(planes, "group", split_axis=2, concat_axis=0, tiled=True)
    return weighted_slots(every_real, every_imag, received[:, 0], received[:, 1])


def solution(mesh):
    torus = Mesh(mesh.devices.reshape(mesh.shape["group"], 4, 8), ("group", "panel_0", "panel_1"))
    return jax.shard_map(
        shards,
        mesh=torus,
        in_specs=(P(None, "group", None, PANEL), P("group", None, None, PANEL), P()),
        out_specs=P(None, "group", None, PANEL),
        check_vma=False,
    )
```

profile of v0, /device:TPU:1, one launch (start us, length us, event | category | flops | bytes accessed | tf_op | source)
XLA Modules:
  0.0 156.1 jit_solution(15786603227173219415)
XLA Ops:
  6.8 1.1 fusion.4
  7.9 0.2 copy.42
  8.1 21.8 %all_to_all.33 = bf16[32,2,12,128]{3,1,2,0:T(2,128)(2,1)S(1)} all-to-all(bf16[32,2,12,128]{3,1,2,0:T(2,128)(2,1)S(1)} %copy.42), channel_id=1, replica_groups=mesh['group'=16,'panel_0'=4,'panel_1'=8] {'group'}, dimensions={0} | all-to-all | bytes 393216 | tf_op jit(solution)/shard_map/all_to_all | solution.py:133
  29.9 0.1 copy.43
  30.1 13.7 %all_gather.13 = bf16[4,2,2,192,128]{4,3,2,1,0:T(8,128)(2,1)} all-gather(bf16[1,2,2,192,128]{4,3,2,1,0:T(8,128)(2,1)S(1)} %copy.44), channel_id=1, replica_groups=mesh['group'=16,'panel_0'=4,'panel_1'=8] {'panel_0'}, dimensions={0}, use_global_device_ids=true | all-gather | bytes 983040 | tf_op jit(solution)/shard_map/all_gather | solution.py:25
  43.8 7.6 %reshape.157 = bf16[2,4096,256,1]{2,1,0,3:T(8,128)(2,1)} reshape(bf16[2,4096,2,128]{3,2,1,0:T(2,128)(2,1)} %param.4) | data formatting | bytes 8388608 | tf_op jit(solution)/shard_map/reshape | solution.py:123
  51.9 0.2 fusion.16
  52.1 0.3 fusion.10
  52.4 0.3 fusion.9
  52.8 0.3 convolution_subtract_fusion.1
  53.1 65.1 %all-gather.3.cloned.1.call-done = bf16[32,2,2,192,128]{4,3,2,1,0:T(8,128)(2,1)} async-done(((bf16[4,2,2,192,128]{4,3,2,1,0:T(8,128)(2,1)}), bf16[32,2,2,192,128]{4,3,2,1,0:T(8,128)(2,1)}) %all-gather.3.cloned.1.call-update) | async-done | bytes 6291472 | tf_op jit(solution)/shard_map/all_gather | solution.py:25
  118.3 3.4 %copy.45 = bf16[4,8,2,2,192,128]{5,4,3,2,1,0:T(8,128)(2,1)S(1)} copy(bf16[4,8,2,2,192,128]{5,4,3,2,0,1:T(8,128)(2,1)} %bitcast.72) | data formatting | bytes 12582912 | tf_op jit(solution)/shard_map/transpose | solution.py:28
  121.7 0.6 copy-done
  122.3 1.8 %fusion = f32[2,2,192,256]{3,2,1,0:T(8,128)S(1)} fusion(bf16[32,2,2,24,8,128]{5,4,3,2,1,0:T(8,128)(2,1)S(1)} %bitcast.73, bf16[2,4096,256,1]{2,1,0,3:T(8,128)(2,1)S(1)} %copy-done), kind=kOutput, calls=%fused_computation | convolution fusion | flops 1610612736 | bytes 11272192 | tf_op jit(solution)/shard_map/qcrk,qkn->qcrn/dot_general | solution.py:134
  124.1 1.0 copy.47
  125.2 8.2 %all-to-all-start.1 = ((f32[2,2,192,128]{3,1,0,2:T(2,128)}), f32[2,2,192,128]{3,1,0,2:T(2,128)S(1)}, u32[]{:S(2)}, u32[]{:S(2)}) async-start(f32[2,2,192,128]{3,1,0,2:T(2,128)} %copy.47), calls=%async_computation.1 | async-start | bytes 786432 | tf_op jit(solution)/shard_map/all_to_all | solution.py:143
  133.4 0.3 convolution_add_fusion
  133.7 0.2 fusion.17
  133.9 0.2 fusion.18
  134.1 13.8 %all-to-all-done.1 = f32[2,2,192,128]{3,1,0,2:T(2,128)S(1)} async-done(((f32[2,2,192,128]{3,1,0,2:T(2,128)}), f32[2,2,192,128]{3,1,0,2:T(2,128)S(1)}, u32[]{:S(2)}, u32[]{:S(2)}) %all-to-all-start.1) | async-done | bytes 393248 | tf_op jit(solution)/shard_map/all_to_all | solution.py:143
  147.9 0.2 copy.49
  148.1 0.2 fusion.6
  148.4 0.2 fusion.5
  148.6 0.6 copy.50
  (25 shorter events, 0.8 us)
Async XLA Ops:
  6.5 45.0 %copy-start.1 = (s32[19]{0:T(128)S(1)}, s32[19]{0:T(128)}, u32[]{:S(2)}) copy-start(s32[19]{0:T(128)} %param.5) | copy-start | bytes 232
  6.5 111.7 %all-gather.3.cloned.1.call-start = ((), (), s32[]{:S(2)}) async-start(), calls=%async_computation.2 | async-start | bytes 7077888 | tf_op jit(solution)/shard_map/all_gather | solution.py:25
  118.3 4.0 %copy-start = (bf16[2,4096,256,1]{2,1,0,3:T(8,128)(2,1)S(1)}, bf16[2,4096,256,1]{2,1,0,3:T(8,128)(2,1)}, u32[]{:S(2)}) copy-start(bf16[2,4096,256,1]{2,1,0,3:T(8,128)(2,1)} %reshape.157) | copy-start | bytes 12582916
  125.2 22.7 %all-to-all-start.1 = ((f32[2,2,192,128]{3,1,0,2:T(2,128)}), f32[2,2,192,128]{3,1,0,2:T(2,128)S(1)}, u32[]{:S(2)}, u32[]{:S(2)}) async-start(f32[2,2,192,128]{3,1,0,2:T(2,128)} %copy.47), calls=%async_computation.1 | async-start | bytes 786432 | tf_op jit(solution)/shard_map/all_to_all | solution.py:143
Sparse Core Ops, SparseCore 0:
  43.9 74.2 all-gather.2
where the time goes:
time: 157 us; the launch traced here: 156 us
  waiting for transfers between devices  78.9 us (50%)
  blocking collectives  35.5 us (23%)
  local copies, waits for them, and re-layouts  13.8 us (9%)
  between operations  13.5 us (9%)
  starting transfers between devices  8.23 us (5%)
  matrix products  5.12 us (3%)
    all_gather x1, waiting for transfers between devices, gather_in_order(): parts = lax.all_gather(parts, axes[k])  65.1 us
    all_to_all x1, blocking collectives, shards(): lax.all_to_all(coded_every, 'group', split_axis=0, concat_axis=2, tiled=T...  21.8 us
    all_to_all x1, waiting for transfers between devices, shards(): lax.all_to_all(planes, 'group', split_axis=2, concat_axis=0, tiled=True)  13.8 us
    all_gather x1, blocking collectives, gather_in_order(): parts = lax.all_gather(parts, axes[k])  13.7 us
    all_to_all x1, starting transfers between devices, shards(): lax.all_to_all(planes, 'group', split_axis=2, concat_axis=0, tiled=True)  8.23 us
    reshape x1, local copies, waits for them, and re-layouts, shards(): shares_flat = second_operand_encoded.reshape(here, quarter, 2 * half_local)  7.61 us
    transpose x1, local copies, waits for them, and re-layouts, gather_in_order(): parts = parts.transpose(*back, *range(len(axes), parts.ndim))  3.39 us
  transfers between devices with their start and end apart: 2, of which 2 were waited for; matrix products, arithmetic and copies ran while one was open for 6% of the time, Pallas kernels for 0%

commit v1 on v0

v1 whole, which is shorter than its diff:
```python
import math

import jax
import jax.numpy as jnp
import numpy as np
from jax import lax
from jax.experimental import pallas as pl
from jax.experimental.pallas import tpu as pltpu
from jax.sharding import Mesh
from jax.sharding import PartitionSpec as P


NODE_NUMBER = 32
PAIRS = 16
EXTRAS = 3
XS = 4
YS = 8
PANELS = XS * YS
ROWS = 384
CHUNK_ROWS = 464
INTERPRET = False

TWO_PI_RADIANS = 2.0 * math.pi


def trig_table():
    exponent = np.arange(4, dtype=np.float32)[None, :] + 8 * np.arange(2, dtype=np.float32)[:, None]
    point = np.arange(NODE_NUMBER, dtype=np.float32)
    phase = np.float32(TWO_PI_RADIANS) * point / np.float32(NODE_NUMBER)
    angle = (phase[:, None, None] * exponent[None]).astype(np.float64)
    table = np.stack([np.cos(angle), np.sin(angle)], axis=1)
    return table.reshape(NODE_NUMBER, 16).astype(np.float32)


def recovery_coefficients(responding_nodes):
    responder_number = responding_nodes.shape[0]
    grid_index = jnp.arange(NODE_NUMBER, dtype=jnp.int32)
    grid_angle = TWO_PI_RADIANS * grid_index.astype(jnp.float32) / NODE_NUMBER
    node_angle = TWO_PI_RADIANS * responding_nodes.astype(jnp.float32) / NODE_NUMBER
    diff_real = jnp.cos(grid_angle)[None, :] - jnp.cos(node_angle)[:, None]
    diff_imag = jnp.sin(grid_angle)[None, :] - jnp.sin(node_angle)[:, None]
    ranks = jnp.arange(responder_number, dtype=jnp.int32)
    itself = (ranks[:, None] == ranks[None, :])[:, :, None]
    factor_real = jnp.where(itself, jnp.float32(1.0), diff_real[None])
    factor_imag = jnp.where(itself, jnp.float32(0.0), diff_imag[None])
    padded_width = 1 << (responder_number - 1).bit_length()
    extra = padded_width - responder_number
    factor_real = jnp.concatenate(
        [factor_real, jnp.ones((responder_number, extra, NODE_NUMBER), jnp.float32)], axis=1
    )
    factor_imag = jnp.concatenate(
        [factor_imag, jnp.zeros((responder_number, extra, NODE_NUMBER), jnp.float32)], axis=1
    )
    while factor_real.shape[1] > 1:
        middle = factor_real.shape[1] // 2
        left_real, right_real = (factor_real[:, :middle], factor_real[:, middle:])
        left_imag, right_imag = (factor_imag[:, :middle], factor_imag[:, middle:])
        factor_real = left_real * right_real - left_imag * right_imag
        factor_imag = left_real * right_imag + left_imag * right_real
    sample_real = factor_real[:, 0]
    sample_imag = factor_imag[:, 0]
    wanted = 3.0 + 4.0 * jnp.arange(4, dtype=jnp.float32)
    table_angle = -grid_angle[:, None] * wanted[None, :]
    table_cos = jnp.cos(table_angle)
    table_sin = jnp.sin(table_angle)
    highest = lax.Precision.HIGHEST
    numer_real = (
        jnp.dot(sample_real, table_cos, precision=highest)
        - jnp.dot(sample_imag, table_sin, precision=highest)
    ) / NODE_NUMBER
    numer_imag = (
        jnp.dot(sample_real, table_sin, precision=highest)
        + jnp.dot(sample_imag, table_cos, precision=highest)
    ) / NODE_NUMBER
    onehot = (responding_nodes[:, None] == grid_index[None, :]).astype(jnp.float32)
    denom_real = jnp.sum(onehot * sample_real, axis=1)
    denom_imag = jnp.sum(onehot * sample_imag, axis=1)
    magnitude = denom_real * denom_real + denom_imag * denom_imag
    coefficient_actual = (
        numer_real * denom_real[:, None] + numer_imag * denom_imag[:, None]
    ) / magnitude[:, None]
    coefficient_image = (
        numer_imag * denom_real[:, None] - numer_real * denom_imag[:, None]
    ) / magnitude[:, None]
    return (coefficient_actual, coefficient_image)


def encode_kernel(main_trig, extra_trig, tiles, out, stack):
    upper = lax.broadcasted_iota(jnp.int32, (8, 128), 0) < 4

    def block(trig, at):
        top_r = trig[at] * tiles[0, :8, :]
        top_i = trig[at + 8] * tiles[0, :8, :]
        low_r = trig[at] * tiles[0, 8:, :]
        low_i = trig[at + 8] * tiles[0, 8:, :]
        for b in range(1, 8):
            top_r += trig[at + b] * tiles[b, :8, :]
            top_i += trig[at + 8 + b] * tiles[b, :8, :]
            low_r += trig[at + b] * tiles[b, 8:, :]
            low_i += trig[at + 8 + b] * tiles[b, 8:, :]
        return top_r, top_i, jnp.where(upper, low_r, low_i)

    stack[...] = jnp.zeros_like(stack)
    for e in range(EXTRAS):
        for v, tile in enumerate(block(extra_trig, 16 * e)):
            stack[24 * e + 8 * v : 24 * e + 8 * v + 8, :] = tile
    turned = stack[...].T
    for t in range(PAIRS):
        parts = list(block(main_trig, 16 * t)) + [turned[8 * t : 8 * t + 8, :]]
        out[t] = jnp.concatenate(parts, axis=0).astype(jnp.bfloat16)


def encode(main_trig, extra_trig, tiles):
    return pl.pallas_call(
        encode_kernel,
        out_shape=jax.ShapeDtypeStruct((PAIRS, 32, 128), jnp.bfloat16),
        in_specs=[
            pl.BlockSpec(memory_space=pltpu.SMEM),
            pl.BlockSpec(memory_space=pltpu.SMEM),
            pl.BlockSpec(memory_space=pltpu.VMEM),
        ],
        out_specs=pl.BlockSpec(memory_space=pltpu.VMEM),
        scratch_shapes=[pltpu.VMEM((128, 128), jnp.float32)],
        name="encode",
        interpret=INTERPRET,
    )(main_trig, extra_trig, tiles)


def compact_kernel(got, out, rows):
    lane = lax.broadcasted_iota(jnp.int32, (8, 128), 1)
    pieces = []
    for g in range(PAIRS):
        block = got[g].astype(jnp.float32)
        rows[24 * g : 24 * g + 24, :] = block[:24]
        pieces.append(block[24:])
    for e in range(EXTRAS):
        for v in range(3):
            tile = jnp.zeros((8, 128), jnp.float32)
            for g in range(PAIRS):
                start = 24 * g - 128 * v
                if start + 24 <= 0 or start >= 128:
                    continue
                moved = pltpu.roll(pieces[g], (start - 24 * e) % 128, 1)
                tile = jnp.where((lane >= start) & (lane < start + 24), moved, tile)
            at = ROWS + 8 * (3 * e + v)
            rows[at : at + 8, :] = tile
    rows[ROWS + 72 :, :] = jnp.zeros((8, 128), jnp.float32)
    out[...] = rows[...].astype(jnp.bfloat16)


def compact(got):
    return pl.pallas_call(
        compact_kernel,
        out_shape=jax.ShapeDtypeStruct((CHUNK_ROWS, 128), jnp.bfloat16),
        in_specs=[pl.BlockSpec(memory_space=pltpu.VMEM)],
        out_specs=pl.BlockSpec(memory_space=pltpu.VMEM),
        scratch_shapes=[pltpu.VMEM((CHUNK_ROWS, 128), jnp.float32)],
        name="compact",
        interpret=INTERPRET,
    )(got)


def split_pairs(pairs, scratch):
    count = pairs.shape[0] // 2
    scratch[: 2 * count, :] = pairs.astype(jnp.float32)
    real = scratch[pl.ds(0, count, stride=2), :]
    imag = scratch[pl.ds(1, count, stride=2), :]
    return jnp.concatenate([real, imag], axis=1).astype(jnp.bfloat16)


def share_kernel(picks, share, own, out, scratch):
    out[0] = split_pairs(share[0], scratch)


def split_share(picks, share, own):
    return pl.pallas_call(
        share_kernel,
        out_shape=jax.ShapeDtypeStruct((XS, 1024, 256), jnp.bfloat16),
        grid_spec=pltpu.PrefetchScalarGridSpec(
            num_scalar_prefetch=1,
            grid=(XS,),
            in_specs=[
                pl.BlockSpec((1, 2048, 128), lambda k, picks: (picks[0], k, 0)),
                pl.BlockSpec(memory_space=pl.ANY),
            ],
            out_specs=pl.BlockSpec((1, 1024, 256), lambda k, picks: (k, 0, 0)),
            scratch_shapes=[pltpu.VMEM((2048, 128), jnp.float32)],
        ),
        name="split_share",
        cost_estimate=pl.CostEstimate(flops=400_000_000, bytes_accessed=4_200_000, transcendentals=0),
        interpret=INTERPRET,
    )(picks, share, own)


def wide(chunk, first, count):
    return jnp.concatenate([chunk[first + y, :ROWS, :] for y in range(count)], axis=1)


def product_kernel(
    picks, weights, share, spread, own, right, left, far_a, far_b, out, acc, extra, acc_extra, scratch
):
    def dot(a, b):
        return jnp.dot(a, b, preferred_element_type=jnp.float32)

    acc[...] = dot(wide(own, 0, YS), share[picks[1]])
    acc[...] += dot(wide(right, 0, YS), share[picks[2]])
    acc[...] += dot(wide(left, 0, YS), share[picks[3]])
    acc[...] += dot(wide(far_a, 0, YS // 2), share[picks[4], :512, :])
    acc[...] += dot(wide(far_b, 0, YS // 2), share[picks[4], 512:, :])

    def place(chunk, count, panel):
        for y in range(count):
            rows = chunk[y, ROWS:, :].astype(jnp.float32)
            at = pl.multiple_of(8 * (panel + y), 8)
            for v in range(9):
                extra[pl.ds(at, 8), 128 * v : 128 * v + 128] = rows[8 * v : 8 * v + 8]

    place(own, YS, YS * picks[1])
    place(right, YS, YS * picks[2])
    place(left, YS, YS * picks[3])
    place(far_a, YS // 2, YS * picks[4])
    place(far_b, YS // 2, YS * picks[4] + YS // 2)
    for e in range(EXTRAS):
        slices = split_pairs(spread[picks[5 + e]], scratch)
        turned = extra[:, ROWS * e : ROWS * e + ROWS].astype(jnp.bfloat16)
        acc_extra[e] = lax.dot_general(
            turned, slices, (((0,), (0,)), ((), ())), preferred_element_type=jnp.float32
        )

    upper = lax.broadcasted_iota(jnp.int32, (8, 128), 0) < 4

    def decode(g, carry):
        top = [jnp.zeros((8, 128), jnp.float32)] * 4
        low = [jnp.zeros((8, 128), jnp.float32)] * 4
        at = pl.multiple_of(24 * g, 8)
        for s in range(1 + EXTRAS):
            tiles = [
                acc[pl.ds(at + 8 * v, 8), :] if s == 0 else acc_extra[s - 1, pl.ds(at + 8 * v, 8), :]
                for v in range(3)
            ]
            top_r = tiles[0][:, :128] - tiles[1][:, 128:]
            top_i = tiles[0][:, 128:] + tiles[1][:, :128]
            low_r = tiles[2][:, :128] - pltpu.roll(tiles[2][:, 128:], 4, 0)
            low_i = tiles[2][:, 128:] + pltpu.roll(tiles[2][:, :128], 4, 0)
            for b in range(4):
                w_r = weights[8 * s + b]
                w_i = weights[8 * s + 4 + b]
                top[b] = top[b] + (w_r * top_r - w_i * top_i)
                low[b] = low[b] + (w_r * low_r - w_i * low_i)
        low_a = jnp.where(upper, low[0], pltpu.roll(low[1], 4, 0))
        low_b = jnp.where(upper, low[2], pltpu.roll(low[3], 4, 0))
        out[g] = jnp.concatenate(top + [low_a, low_b], axis=0)
        return carry

    lax.fori_loop(0, PAIRS, decode, 0)


def product(picks, weights, share, spread, own, right, left, far_a, far_b):
    return pl.pallas_call(
        product_kernel,
        out_shape=jax.ShapeDtypeStruct((PAIRS, 48, 128), jnp.float32),
        in_specs=[pl.BlockSpec(memory_space=pltpu.SMEM)] * 2 + [pl.BlockSpec(memory_space=pltpu.VMEM)] * 7,
        out_specs=pl.BlockSpec(memory_space=pltpu.VMEM),
        scratch_shapes=[
            pltpu.VMEM((ROWS, 256), jnp.float32),
            pltpu.VMEM((256, 1152), jnp.float32),
            pltpu.VMEM((EXTRAS, ROWS, 256), jnp.float32),
            pltpu.VMEM((512, 128), jnp.float32),
        ],
        name="product",
        interpret=INTERPRET,
    )(picks, weights, share, spread, own, right, left, far_a, far_b)


def choose(responding_nodes):
    listed = jnp.any(
        responding_nodes[:, None] == jnp.arange(NODE_NUMBER, dtype=jnp.int32)[None, :], axis=0
    ).reshape(PAIRS, 2)
    both = listed[:, 0] & listed[:, 1]
    index = jnp.arange(PAIRS, dtype=jnp.int32)
    before = jnp.sum((index[None, :] < index[:, None]) & both[None, :], axis=1)
    extra_pair = both[None, :] & (before[None, :] == jnp.arange(EXTRAS, dtype=jnp.int32)[:, None])
    return listed[:, 0], extra_pair


def source_tiles(source):
    blocks = source.astype(jnp.float32).transpose(0, 2, 1, 3).reshape(8, 12, 128)
    return jnp.concatenate([blocks, blocks[:, 8:]], axis=1)


def summed(received):
    total = jnp.sum(received, axis=0)
    top = total[:32].reshape(2, 2, 8, 128)
    low = total[32:].reshape(2, 2, 4, 128)
    return jnp.concatenate([top, low], axis=2).transpose(0, 2, 1, 3)


def shards(source_matrix_tiles, second_operand_encoded, responding_nodes):
    table = jnp.asarray(trig_table())
    even_listed, extra_pair = choose(responding_nodes)
    pair_table = table.reshape(PAIRS, 2, 16)
    main_trig = jnp.where(even_listed[:, None], pair_table[:, 0], pair_table[:, 1])
    extra_trig = jnp.sum(jnp.where(extra_pair[:, :, None], pair_table[None, :, 1], 0.0), axis=1)
    sent = encode(main_trig.reshape(-1), extra_trig.reshape(-1), source_tiles(source_matrix_tiles))
    got = lax.all_to_all(sent, "group", split_axis=0, concat_axis=0, tiled=True)

    odd = second_operand_encoded[1].reshape(PANELS, PAIRS, 8, 2, 128).transpose(1, 0, 2, 3, 4)
    odd, got = lax.optimization_barrier((odd, got))
    spread = lax.all_to_all(odd, "group", split_axis=0, concat_axis=0, tiled=True)
    own = lax.all_gather(compact(got), "y")

    responding_nodes, own = lax.optimization_barrier((responding_nodes, own))
    right = lax.ppermute(own, "x", [(i, (i + 1) % XS) for i in range(XS)])
    left = lax.ppermute(own, "x", [(i, (i - 1) % XS) for i in range(XS)])
    far_a = lax.ppermute(right[: YS // 2], "x", [(i, (i + 1) % XS) for i in range(XS)])
    far_b = lax.ppermute(left[YS // 2 :], "x", [(i, (i - 1) % XS) for i in range(XS)])

    coefficient_actual, coefficient_image = recovery_coefficients(responding_nodes)
    even_listed, extra_pair = choose(responding_nodes)
    group = lax.axis_index("group")
    x = lax.axis_index("x")
    second = jnp.where(even_listed[group], 0, 1).astype(jnp.int32)
    extra_group = jnp.sum(
        jnp.where(extra_pair, jnp.arange(PAIRS, dtype=jnp.int32)[None, :], 0), axis=1
    ).astype(jnp.int32)
    used = jnp.concatenate([(2 * group + second)[None], 2 * extra_group + 1])
    point_selector = (used[:, None] == responding_nodes[None, :])[:, :, None]
    weights = jnp.concatenate(
        [
            jnp.sum(jnp.where(point_selector, coefficient_actual[None], 0.0), axis=1),
            jnp.sum(jnp.where(point_selector, coefficient_image[None], 0.0), axis=1),
        ],
        axis=1,
    ).reshape(-1)
    panels = jnp.stack([x, (x - 1) % XS, (x + 1) % XS, (x + 2) % XS]).astype(jnp.int32)
    picks = jnp.concatenate([second[None], panels, extra_group])

    share = split_share(picks, second_operand_encoded.reshape(2, 8192, 128), own)
    partial = product(
        picks, weights, share, spread.reshape(PAIRS, 512, 128), own, right, left, far_a, far_b
    )
    received = lax.all_to_all(partial, "group", split_axis=0, concat_axis=0, tiled=True)
    return summed(received)


def solution(mesh):
    torus = Mesh(mesh.devices.reshape(mesh.shape["group"], XS, YS), ("group", "x", "y"))
    return jax.shard_map(
        shards,
        mesh=torus,
        in_specs=(P(None, "group", None, ("x", "y")), P("group", None, None, ("x", "y")), P()),
        out_specs=P(None, "group", None, ("x", "y")),
        check_vma=False,
    )
```

time: 157 us -> 146 us (0.930)
  waiting for transfers between devices: 78.9 us -> 32.9 us
  starting transfers between devices: 8.23 us -> 34.6 us
  Pallas kernels: 0 us -> 13.7 us
  between operations: 13.5 us -> 0.9 us
  blocking collectives: 35.5 us -> 42.4 us
  other arithmetic: 0.91 us -> 5.87 us
  matrix products: 5.12 us -> 1.34 us
    all_gather x1 -> x0, waiting for transfers between devices: 65.1 us -> none  [gather_in_order(): parts = lax.all_gather(parts, axes[k])]
    all_to_all x1 -> x2, waiting for transfers between devices: 13.8 us -> 30.2 us  [the longest x1 26.5 us: shards(): lax.all_to_all(odd, 'group', split_axis=0, concat_axis=0, tiled=True)]
    ppermute x0 -> x4, starting transfers between devices: none -> 13.8 us  [the longest x1 5.43 us: shards(): lax.ppermute(left[YS // 2:], 'x', [(i, (i - 1) % XS) for i in range(XS)])]
    pallas_call x0 -> x4, Pallas kernels: none -> 13.7 us  [the longest x1 5.75 us: product(): pl.pallas_call(product_kernel, out_shape=jax.ShapeDtypeStruct((PAIRS, 48,...]
    all_to_all x1 -> x2, starting transfers between devices: 8.23 us -> 20.9 us  [the longest x1 11.8 us: shards(): got = lax.all_to_all(sent, 'group', split_axis=0, concat_axis=0, tiled=True)]
    all_gather x1, blocking collectives: 13.7 us -> 23.1 us  [shards(): own = lax.all_gather(compact(got), 'y')]
    reshape x1 -> x5, local copies, waits for them, and re-layouts: 7.61 us -> 1.44 us  [the longest x1 0.63 us: shards(): extra_trig.reshape(-1)]
    slice x0 -> x8, local copies, waits for them, and re-layouts: none -> 3.9 us  [the longest x2 1.59 us: shards(): second_operand_encoded[1].reshape(PANELS, PAIRS, 8, 2, 128)]
  transfers between devices with their start and end apart: 2 -> 6, of which waited for: 2 -> 4; matrix products, arithmetic and copies ran while one was open for 6% -> 7% of each run, Pallas kernels for 0% -> 3%
where the time goes in v1:
time: 146 us; the launch traced here: 145 us
  blocking collectives  42.4 us (29%)
  starting transfers between devices  34.6 us (24%)
  waiting for transfers between devices  32.9 us (23%)
  Pallas kernels  13.7 us (9%)
  local copies, waits for them, and re-layouts  13.2 us (9%)
  other arithmetic  5.87 us (4%)
    all_to_all x1, waiting for transfers between devices, shards(): lax.all_to_all(odd, 'group', split_axis=0, concat_axis=0, tiled=True)  26.5 us
    all_gather x1, blocking collectives, shards(): own = lax.all_gather(compact(got), 'y')  23.1 us
    all_to_all x1, blocking collectives, shards(): lax.all_to_all(partial, 'group', split_axis=0, concat_axis=0, tiled=True)  19.3 us
    all_to_all x1, starting transfers between devices, shards(): got = lax.all_to_all(sent, 'group', split_axis=0, concat_axis=0, tiled=True)  11.8 us
    all_to_all x1, starting transfers between devices, shards(): lax.all_to_all(odd, 'group', split_axis=0, concat_axis=0, tiled=True)  9.03 us
    pallas_call x1, Pallas kernels, product(): pl.pallas_call(product_kernel, out_shape=jax.ShapeDtypeStruct((PAIRS, 48,...  5.75 us
    ppermute x1, starting transfers between devices, shards(): lax.ppermute(left[YS // 2:], 'x', [(i, (i - 1) % XS) for i in range(XS)])  5.43 us
    pallas_call x1, Pallas kernels, split_share(): pl.pallas_call(share_kernel, out_shape=jax.ShapeDtypeStruct((XS, 1024, 25...  4.63 us
  transfers between devices with their start and end apart: 6, of which 4 were waited for; matrix products, arithmetic and copies ran while one was open for 7% of the time, Pallas kernels for 3%

profile of v1, /device:TPU:1, one launch (start us, length us, event | category | flops | bytes accessed | tf_op | source)
XLA Modules:
  0.0 145.0 jit_solution(14055283068356235143)
XLA Ops:
  0.0 0.7 fusion.9
  1.2 0.8 select_reduce_fusion
  2.6 0.8 broadcast_select_fusion.2
  5.4 1.7 %encode.1 = bf16[16,32,128]{2,1,0:T(8,128)(2,1)} custom-call(f32[256]{0:T(256)} %reshape.233.main_trig, f32[48]{0:T(128)} %reshape.222.extra_trig, f32[8,16,128]{2,1,0:T(8,128)} %pad_maximum_fusion.tiles), custom_call_target="tpu_custom_call" | custom-call | tf_op jit(solution)/shard_map/encode/pallas_call | solution.py:114
  7.1 11.8 %all-to-all-start = ((bf16[16,32,128]{2,1,0:T(8,128)(2,1)}), bf16[16,32,128]{2,1,0:T(8,128)(2,1)S(1)}, u32[]{:S(2)}, u32[]{:S(2)}) async-start(bf16[16,32,128]{2,1,0:T(8,128)(2,1)} %encode.1), calls=%async_computation | async-start | bytes 262144 | tf_op jit(solution)/shard_map/all_to_all | solution.py:305
  19.1 1.6 %slice-done = bf16[1,4096,2,128]{3,2,1,0:T(2,128)(2,1)S(1)} async-done(((bf16[2,4096,2,128]{3,2,1,0:T(2,128)(2,1)}), bf16[1,4096,2,128]{3,2,1,0:T(2,128)(2,1)S(1)}, s32[]{:S(2)}) %slice-start) | async-done | bytes 2097176 | tf_op jit(solution)/shard_map/slice | solution.py:307
  20.6 3.4 %copy.18 = bf16[32,16,8,2,128]{4,3,2,0,1:T(2,128)(2,1)} copy(bf16[32,16,8,2,128]{4,3,2,1,0:T(2,128)(2,1)S(1)} %bitcast.40) | data formatting | bytes 4194304 | tf_op jit(solution)/shard_map/reshape;squeeze | solution.py:307
  24.1 3.8 %all-to-all-done.got = bf16[16,32,128]{2,1,0:T(8,128)(2,1)S(1)} async-done(((bf16[16,32,128]{2,1,0:T(8,128)(2,1)}), bf16[16,32,128]{2,1,0:T(8,128)(2,1)S(1)}, u32[]{:S(2)}, u32[]{:S(2)}) %all-to-all-start) | async-done | bytes 131104 | tf_op jit(solution)/shard_map/all_to_all | solution.py:305
  28.5 1.6 %compact.1 = bf16[464,128]{1,0:T(8,128)(2,1)} custom-call(bf16[16,32,128]{2,1,0:T(8,128)(2,1)} %copy-done.2), custom_call_target="tpu_custom_call" | custom-call | tf_op jit(solution)/shard_map/compact/pallas_call | solution.py:152
  30.1 23.1 %all-gather = bf16[3712,128]{1,0:T(8,128)(2,1)S(1)} all-gather(bf16[464,128]{1,0:T(8,128)(2,1)} %compact.1), channel_id=2, replica_groups=mesh['group'=16,'x'=4,'y'=8] {'y'}, dimensions={0}, use_global_device_ids=true | all-gather | bytes 1069056 | tf_op jit(solution)/shard_map/all_gather | solution.py:310
  53.3 4.5 %collective-permute-start.1 = (bf16[8,464,128]{2,1,0:T(8,128)(2,1)S(1)}, bf16[8,464,128]{2,1,0:T(8,128)(2,1)}, u32[]{:S(2)}, u32[]{:S(2)}) collective-permute-start(bf16[8,464,128]{2,1,0:T(8,128)(2,1)S(1)} %bitcast.41), channel_id=1, source_target_pairs={{0,24},{8,0},{16,8},{24,16},{1,25},{9,1},{17,9},{25,17},{2,26},{10... | collective-permute-start | bytes 2850824 | tf_op jit(solution)/shard_map/ppermute | solution.py:314
  57.8 1.9 %collective-permute-start = (bf16[8,464,128]{2,1,0:T(8,128)(2,1)S(1)}, bf16[8,464,128]{2,1,0:T(8,128)(2,1)}, u32[]{:S(2)}, u32[]{:S(2)}) collective-permute-start(bf16[8,464,128]{2,1,0:T(8,128)(2,1)S(1)} %bitcast.42), channel_id=1, source_target_pairs={{0,8},{8,16},{16,24},{24,0},{1,9},{9,17},{17,25},{25,1},{2,10},{10... | collective-permute-start | bytes 2850824 | tf_op jit(solution)/shard_map/ppermute | solution.py:313
  59.7 9.0 %all-to-all-start.1 = ((bf16[16,32,8,2,128]{4,3,2,1,0:T(2,128)(2,1)}), bf16[16,32,8,2,128]{4,3,2,1,0:T(2,128)(2,1)S(1)}, u32[]{:S(2)}, u32[]{:S(2)}) async-start(bf16[16,32,8,2,128]{4,3,2,1,0:T(2,128)(2,1)} %bitcast.46), calls=%async_computation.1 | async-start | bytes 4194304 | tf_op jit(solution)/shard_map/all_to_all | solution.py:309
  72.9 1.1 slice.155
  74.0 5.4 %collective-permute-start.3 = (bf16[4,464,128]{2,1,0:T(8,128)(2,1)S(1)}, bf16[4,464,128]{2,1,0:T(8,128)(2,1)}, u32[]{:S(2)}, u32[]{:S(2)}) collective-permute-start(bf16[4,464,128]{2,1,0:T(8,128)(2,1)S(1)} %slice.155), channel_id=1, source_target_pairs={{0,24},{8,0},{16,8},{24,16},{1,25},{9,1},{17,9},{25,17},{2,26},{10... | collective-permute-start | bytes 1425416 | tf_op jit(solution)/shard_map/ppermute | solution.py:316
  79.4 1.1 slice.154
  80.5 1.9 %collective-permute-start.2 = (bf16[4,464,128]{2,1,0:T(8,128)(2,1)S(1)}, bf16[4,464,128]{2,1,0:T(8,128)(2,1)S(1)}, u32[]{:S(2)}, u32[]{:S(2)}) collective-permute-start(bf16[4,464,128]{2,1,0:T(8,128)(2,1)S(1)} %slice.154), channel_id=1, source_target_pairs={{0,8},{8,16},{16,24},{24,0},{1,9},{9,17},{17,25},{25,1},{2,10},{10... | collective-permute-start | bytes 1425416 | tf_op jit(solution)/shard_map/ppermute | solution.py:315
  83.3 1.2 concatenate.22.picks
  84.5 4.6 %split_share.1.share = bf16[4,1024,256]{2,1,0:T(8,128)(2,1)} custom-call(s32[8]{0:T(128)} %concatenate.22.picks, bf16[2,8192,128]{2,1,0:T(8,128)(2,1)} %bitcast.39, bf16[8,464,128]{2,1,0:T(8,128)(2,1)} %bitcast.43), custom_call_target="tpu_custom_call" | custom-call | flops 400000000 | bytes 4200000 | tf_op jit(solution)/shard_map/split_share/pallas_call | solution.py:176
  89.1 2.3 %collective-permute-done.2.far_a = bf16[4,464,128]{2,1,0:T(8,128)(2,1)S(1)} collective-permute-done((bf16[4,464,128]{2,1,0:T(8,128)(2,1)S(1)}, bf16[4,464,128]{2,1,0:T(8,128)(2,1)S(1)}, u32[]{:S(2)}, u32[]{:S(2)}) %collective-permute-start.2) | collective-permute-done | bytes 475168 | tf_op jit(solution)/shard_map/ppermute | solution.py:315
  91.4 26.5 %all-to-all-done.1 = bf16[16,32,8,2,128]{4,3,2,1,0:T(2,128)(2,1)S(1)} async-done(((bf16[16,32,8,2,128]{4,3,2,1,0:T(2,128)(2,1)}), bf16[16,32,8,2,128]{4,3,2,1,0:T(2,128)(2,1)S(1)}, u32[]{:S(2)}, u32[]{:S(2)}) %all-to-all-start.1) | async-done | bytes 2097184 | tf_op jit(solution)/shard_map/all_to_all | solution.py:309
  117.9 1.3 copy-done.1
  119.2 5.7 %product.1 = f32[16,48,128]{2,1,0:T(8,128)} custom-call(s32[8]{0:T(128)} %concatenate.22.picks, f32[32]{0:T(128)} %reshape.226.weights, bf16[4,1024,256]{2,1,0:T(8,128)(2,1)} %split_share.1.share, bf16[16,512,128]{2,1,0:T(8,128)(2,1)} %bitcast.45, bf16[8,464,128]{2,1,0:T(8,128)(2,1)} %bitcast.44, bf16[8,464,128]{2,1,0:T(8,128)(2,1)} %collective-permute-done.right, ...), custom_call_target="tpu_custom_call" | custom-call | tf_op jit(solution)/shard_map/product/pallas_call | solution.py:259
  125.0 19.3 %all_to_all.15 = f32[16,48,128]{2,1,0:T(8,128)S(1)} all-to-all(f32[16,48,128]{2,1,0:T(8,128)} %product.1), channel_id=1, replica_groups=mesh['group'=16,'x'=4,'y'=8] {'group'}, dimensions={0} | all-to-all | bytes 786432 | tf_op jit(solution)/shard_map/all_to_all | solution.py:342
  (59 shorter events, 8.8 us)
Async XLA Ops:
  7.1 20.7 %all-to-all-start = ((bf16[16,32,128]{2,1,0:T(8,128)(2,1)}), bf16[16,32,128]{2,1,0:T(8,128)(2,1)S(1)}, u32[]{:S(2)}, u32[]{:S(2)}) async-start(bf16[16,32,128]{2,1,0:T(8,128)(2,1)} %encode.1), calls=%async_computation | async-start | bytes 262144 | tf_op jit(solution)/shard_map/all_to_all | solution.py:305
  19.0 1.6 %slice-start = ((bf16[2,4096,2,128]{3,2,1,0:T(2,128)(2,1)}), bf16[1,4096,2,128]{3,2,1,0:T(2,128)(2,1)S(1)}, s32[]{:S(2)}) async-start(bf16[2,4096,2,128]{3,2,1,0:T(2,128)(2,1)} %param.5), calls=%async_computation.3 | async-start | bytes 4194304 | tf_op jit(solution)/shard_map/slice | solution.py:307
  27.8 0.7 copy-start.2
  53.3 6.5 %copy-start = (bf16[3712,128]{1,0:T(8,128)(2,1)}, bf16[3712,128]{1,0:T(8,128)(2,1)S(1)}, u32[]{:S(2)}) copy-start(bf16[3712,128]{1,0:T(8,128)(2,1)S(1)} %all-gather) | copy-start | bytes 2850820
  53.3 15.5 %copy-start.4 = (s32[19]{0:T(128)S(1)}, s32[19]{0:T(128)}, u32[]{:S(2)}) copy-start(s32[19]{0:T(128)} %param.6) | copy-start | bytes 232
  53.3 19.7 %collective-permute-start.1 = (bf16[8,464,128]{2,1,0:T(8,128)(2,1)S(1)}, bf16[8,464,128]{2,1,0:T(8,128)(2,1)}, u32[]{:S(2)}, u32[]{:S(2)}) collective-permute-start(bf16[8,464,128]{2,1,0:T(8,128)(2,1)S(1)} %bitcast.41), channel_id=1, source_target_pairs={{0,24},{8,0},{16,8},{24,16},{1,25},{9,1},{17,9},{25,17},{2,26},{10... | collective-permute-start | bytes 2850824 | tf_op jit(solution)/shard_map/ppermute | solution.py:314
  57.8 21.6 %collective-permute-start = (bf16[8,464,128]{2,1,0:T(8,128)(2,1)S(1)}, bf16[8,464,128]{2,1,0:T(8,128)(2,1)}, u32[]{:S(2)}, u32[]{:S(2)}) collective-permute-start(bf16[8,464,128]{2,1,0:T(8,128)(2,1)S(1)} %bitcast.42), channel_id=1, source_target_pairs={{0,8},{8,16},{16,24},{24,0},{1,9},{9,17},{17,25},{25,1},{2,10},{10... | collective-permute-start | bytes 2850824 | tf_op jit(solution)/shard_map/ppermute | solution.py:313
  59.7 58.1 %all-to-all-start.1 = ((bf16[16,32,8,2,128]{4,3,2,1,0:T(2,128)(2,1)}), bf16[16,32,8,2,128]{4,3,2,1,0:T(2,128)(2,1)S(1)}, u32[]{:S(2)}, u32[]{:S(2)}) async-start(bf16[16,32,8,2,128]{4,3,2,1,0:T(2,128)(2,1)} %bitcast.46), calls=%async_computation.1 | async-start | bytes 4194304 | tf_op jit(solution)/shard_map/all_to_all | solution.py:309
  74.0 15.1 %collective-permute-start.3 = (bf16[4,464,128]{2,1,0:T(8,128)(2,1)S(1)}, bf16[4,464,128]{2,1,0:T(8,128)(2,1)}, u32[]{:S(2)}, u32[]{:S(2)}) collective-permute-start(bf16[4,464,128]{2,1,0:T(8,128)(2,1)S(1)} %slice.155), channel_id=1, source_target_pairs={{0,24},{8,0},{16,8},{24,16},{1,25},{9,1},{17,9},{25,17},{2,26},{10... | collective-permute-start | bytes 1425416 | tf_op jit(solution)/shard_map/ppermute | solution.py:316
  80.5 10.9 %collective-permute-start.2 = (bf16[4,464,128]{2,1,0:T(8,128)(2,1)S(1)}, bf16[4,464,128]{2,1,0:T(8,128)(2,1)S(1)}, u32[]{:S(2)}, u32[]{:S(2)}) collective-permute-start(bf16[4,464,128]{2,1,0:T(8,128)(2,1)S(1)} %slice.154), channel_id=1, source_target_pairs={{0,8},{8,16},{16,24},{24,0},{1,9},{9,17},{17,25},{25,1},{2,10},{10... | collective-permute-start | bytes 1425416 | tf_op jit(solution)/shard_map/ppermute | solution.py:315
  91.4 26.5 %copy-start.3 = (bf16[4,464,128]{2,1,0:T(8,128)(2,1)}, bf16[4,464,128]{2,1,0:T(8,128)(2,1)S(1)}, u32[]{:S(2)}) copy-start(bf16[4,464,128]{2,1,0:T(8,128)(2,1)S(1)} %collective-permute-done.2.far_a) | copy-start | bytes 1425412
  117.9 1.4 copy-start.1

commit v2 on v1

v2 whole, which is shorter than its diff:
```python
import math

import jax
import jax.numpy as jnp
import numpy as np
from jax import lax
from jax.experimental import pallas as pl
from jax.experimental.pallas import tpu as pltpu
from jax.sharding import Mesh
from jax.sharding import PartitionSpec as P


NODE_NUMBER = 32
PAIRS = 16
EXTRAS = 3
XS = 4
YS = 8
QUADS = YS // 2
PANELS = XS * YS
ROWS = 384
CHUNK_ROWS = 464
INTERPRET = False

TWO_PI_RADIANS = 2.0 * math.pi


def trig_table():
    exponent = np.arange(4, dtype=np.float32)[None, :] + 8 * np.arange(2, dtype=np.float32)[:, None]
    point = np.arange(NODE_NUMBER, dtype=np.float32)
    phase = np.float32(TWO_PI_RADIANS) * point / np.float32(NODE_NUMBER)
    angle = (phase[:, None, None] * exponent[None]).astype(np.float64)
    table = np.stack([np.cos(angle), np.sin(angle)], axis=1)
    return table.reshape(NODE_NUMBER, 16).astype(np.float32)


def recovery_coefficients(responding_nodes):
    responder_number = responding_nodes.shape[0]
    grid_index = jnp.arange(NODE_NUMBER, dtype=jnp.int32)
    grid_angle = TWO_PI_RADIANS * grid_index.astype(jnp.float32) / NODE_NUMBER
    node_angle = TWO_PI_RADIANS * responding_nodes.astype(jnp.float32) / NODE_NUMBER
    diff_real = jnp.cos(grid_angle)[None, :] - jnp.cos(node_angle)[:, None]
    diff_imag = jnp.sin(grid_angle)[None, :] - jnp.sin(node_angle)[:, None]
    ranks = jnp.arange(responder_number, dtype=jnp.int32)
    itself = (ranks[:, None] == ranks[None, :])[:, :, None]
    factor_real = jnp.where(itself, jnp.float32(1.0), diff_real[None])
    factor_imag = jnp.where(itself, jnp.float32(0.0), diff_imag[None])
    padded_width = 1 << (responder_number - 1).bit_length()
    extra = padded_width - responder_number
    factor_real = jnp.concatenate(
        [factor_real, jnp.ones((responder_number, extra, NODE_NUMBER), jnp.float32)], axis=1
    )
    factor_imag = jnp.concatenate(
        [factor_imag, jnp.zeros((responder_number, extra, NODE_NUMBER), jnp.float32)], axis=1
    )
    while factor_real.shape[1] > 1:
        middle = factor_real.shape[1] // 2
        left_real, right_real = (factor_real[:, :middle], factor_real[:, middle:])
        left_imag, right_imag = (factor_imag[:, :middle], factor_imag[:, middle:])
        factor_real = left_real * right_real - left_imag * right_imag
        factor_imag = left_real * right_imag + left_imag * right_real
    sample_real = factor_real[:, 0]
    sample_imag = factor_imag[:, 0]
    wanted = 3.0 + 4.0 * jnp.arange(4, dtype=jnp.float32)
    table_angle = -grid_angle[:, None] * wanted[None, :]
    table_cos = jnp.cos(table_angle)
    table_sin = jnp.sin(table_angle)
    highest = lax.Precision.HIGHEST
    numer_real = (
        jnp.dot(sample_real, table_cos, precision=highest)
        - jnp.dot(sample_imag, table_sin, precision=highest)
    ) / NODE_NUMBER
    numer_imag = (
        jnp.dot(sample_real, table_sin, precision=highest)
        + jnp.dot(sample_imag, table_cos, precision=highest)
    ) / NODE_NUMBER
    onehot = (responding_nodes[:, None] == grid_index[None, :]).astype(jnp.float32)
    denom_real = jnp.sum(onehot * sample_real, axis=1)
    denom_imag = jnp.sum(onehot * sample_imag, axis=1)
    magnitude = denom_real * denom_real + denom_imag * denom_imag
    coefficient_actual = (
        numer_real * denom_real[:, None] + numer_imag * denom_imag[:, None]
    ) / magnitude[:, None]
    coefficient_image = (
        numer_imag * denom_real[:, None] - numer_real * denom_imag[:, None]
    ) / magnitude[:, None]
    return (coefficient_actual, coefficient_image)


def encode_kernel(nodes, table, source, out, flags, extra_points, rows, stack):
    for j in range(NODE_NUMBER):
        flags[j] = 0
    for s in range(nodes.shape[0]):
        flags[nodes[s]] = 1
    found = jnp.int32(0)
    for g in range(PAIRS):
        extra_points[found] = 2 * g + 1
        found = found + flags[2 * g] * flags[2 * g + 1]

    rows[...] = source[...].astype(jnp.float32)
    tops = []
    lows = []
    for b in range(8):
        at = 48 * (b // 4) + b % 4
        tops.append(rows[pl.ds(at, 8, stride=4), :])
        low = rows[pl.ds(at + 32, 4, stride=4), :]
        lows.append(jnp.concatenate([low, low], axis=0))
    upper = lax.broadcasted_iota(jnp.int32, (8, 128), 0) < 4

    def block(point):
        at = 16 * point
        real = [table[at + b] for b in range(8)]
        imag = [table[at + 8 + b] for b in range(8)]
        top_r = sum(real[b] * tops[b] for b in range(8))
        top_i = sum(imag[b] * tops[b] for b in range(8))
        low = sum(jnp.where(upper, real[b], imag[b]) * lows[b] for b in range(8))
        return [top_r, top_i, low]

    stack[...] = jnp.zeros_like(stack)
    for e in range(EXTRAS):
        for v, tile in enumerate(block(extra_points[e])):
            stack[24 * e + 8 * v : 24 * e + 8 * v + 8, :] = tile
    stack[...] = stack[...].T

    def main(t, carry):
        parts = block(2 * t + 1 - flags[2 * t])
        parts.append(stack[pl.ds(pl.multiple_of(8 * t, 8), 8), :])
        value = jnp.concatenate(parts, axis=0).astype(jnp.bfloat16)
        for q in range(QUADS):
            out[t, q] = value
        return carry

    lax.fori_loop(0, PAIRS, main, 0)


def encode(nodes, table, source):
    return pl.pallas_call(
        encode_kernel,
        out_shape=jax.ShapeDtypeStruct((PAIRS, QUADS, 32, 128), jnp.bfloat16),
        in_specs=[
            pl.BlockSpec(memory_space=pltpu.SMEM),
            pl.BlockSpec(memory_space=pltpu.SMEM),
            pl.BlockSpec(memory_space=pltpu.VMEM),
        ],
        out_specs=pl.BlockSpec(memory_space=pltpu.VMEM),
        scratch_shapes=[
            pltpu.SMEM((NODE_NUMBER,), jnp.int32),
            pltpu.SMEM((PAIRS,), jnp.int32),
            pltpu.VMEM((96, 128), jnp.float32),
            pltpu.VMEM((128, 128), jnp.float32),
        ],
        name="encode",
        interpret=INTERPRET,
    )(nodes, table, source)


def compact_kernel(got, out, rows):
    lane = lax.broadcasted_iota(jnp.int32, (8, 128), 1)
    rows[ROWS + 72 :, :] = jnp.zeros((8, 128), jnp.float32)

    def one(q, carry):
        pieces = []
        for g in range(PAIRS):
            block = got[QUADS * g + q].astype(jnp.float32)
            rows[24 * g : 24 * g + 24, :] = block[:24]
            pieces.append(block[24:])
        for e in range(EXTRAS):
            for v in range(3):
                tile = jnp.zeros((8, 128), jnp.float32)
                for g in range(PAIRS):
                    start = 24 * g - 128 * v
                    if start + 24 <= 0 or start >= 128:
                        continue
                    moved = pltpu.roll(pieces[g], (start - 24 * e) % 128, 1)
                    tile = jnp.where((lane >= start) & (lane < start + 24), moved, tile)
                at = ROWS + 8 * (3 * e + v)
                rows[at : at + 8, :] = tile
        out[q] = rows[...].astype(jnp.bfloat16)
        return carry

    lax.fori_loop(0, QUADS, one, 0)


def compact(got):
    return pl.pallas_call(
        compact_kernel,
        out_shape=jax.ShapeDtypeStruct((QUADS, CHUNK_ROWS, 128), jnp.bfloat16),
        in_specs=[pl.BlockSpec(memory_space=pltpu.VMEM)],
        out_specs=pl.BlockSpec(memory_space=pltpu.VMEM),
        scratch_shapes=[pltpu.VMEM((CHUNK_ROWS, 128), jnp.float32)],
        name="compact",
        interpret=INTERPRET,
    )(got)


def split_pairs(pairs, scratch):
    count = pairs.shape[0] // 2
    scratch[: 2 * count, :] = pairs.astype(jnp.float32)
    real = scratch[pl.ds(0, count, stride=2), :]
    imag = scratch[pl.ds(1, count, stride=2), :]
    return jnp.concatenate([real, imag], axis=1).astype(jnp.bfloat16)


def share_kernel(picks, share, out, scratch):
    for y in range(YS):
        piece = split_pairs(share[0, 256 * y : 256 * y + 256, :], scratch)
        out[0, y % 2, 128 * (y // 2) : 128 * (y // 2) + 128, :] = piece


def split_share(picks, share):
    return pl.pallas_call(
        share_kernel,
        out_shape=jax.ShapeDtypeStruct((XS, 2, 512, 256), jnp.bfloat16),
        grid_spec=pltpu.PrefetchScalarGridSpec(
            num_scalar_prefetch=1,
            grid=(XS,),
            in_specs=[pl.BlockSpec((1, 2048, 128), lambda k, picks: (picks[0], k, 0))],
            out_specs=pl.BlockSpec((1, 2, 512, 256), lambda k, picks: (k, 0, 0, 0)),
            scratch_shapes=[pltpu.VMEM((256, 128), jnp.float32)],
        ),
        name="split_share",
        cost_estimate=pl.CostEstimate(flops=400_000_000, bytes_accessed=4_200_000, transcendentals=0),
        interpret=INTERPRET,
    )(picks, share)


def wide(chunk):
    return jnp.concatenate([chunk[q, :ROWS, :] for q in range(QUADS)], axis=1)


def dot(a, b):
    return jnp.dot(a, b, preferred_element_type=jnp.float32)


EARLY = ((0, True), (0, False), (-1, True), (1, True))
LATE = ((-1, False), (1, False), (2, True), (2, False))


def block_of(picks, kind):
    offset, same = kind
    x = (picks[1] + offset + XS) % XS
    return x, picks[2] if same else 1 - picks[2]


def early_kernel(picks, share, a, b, right_a, left_a, acc):
    for n, (chunk, kind) in enumerate(zip((a, b, right_a, left_a), EARLY)):
        x, parity = block_of(picks, kind)
        term = dot(wide(chunk), share[x, parity])
        if n == 0:
            acc[...] = term
        else:
            acc[...] += term


def early_product(picks, share, chunks):
    return pl.pallas_call(
        early_kernel,
        out_shape=jax.ShapeDtypeStruct((ROWS, 256), jnp.float32),
        in_specs=[pl.BlockSpec(memory_space=pltpu.SMEM)] + [pl.BlockSpec(memory_space=pltpu.VMEM)] * 5,
        out_specs=pl.BlockSpec(memory_space=pltpu.VMEM),
        name="early_product",
        cost_estimate=pl.CostEstimate(flops=400_000_000, bytes_accessed=4_200_000, transcendentals=0),
        interpret=INTERPRET,
    )(picks, share, *chunks)


def late_kernel(
    picks, weights, share, spread, before, c0, c1, c2, c3, c4, c5, c6, c7, out,
    acc, blocks, small, ends, late, extra, acc_extra, scratch, sems,
):
    early = (c0, c1, c2, c3)
    chunks = (c4, c5, c6, c7)
    copies = []

    def start(source, target):
        copy = pltpu.make_async_copy(source, target, sems.at[len(copies)])
        copy.start()
        copies.append(copy)

    start(spread, small)
    for n in range(4):
        start(early[n].at[:, pl.ds(ROWS, 80), :], ends.at[n])
    for n in range(4):
        x, parity = block_of(picks, LATE[n])
        start(chunks[n], late.at[n])
        start(share.at[x, parity], blocks.at[n])
    start(before, acc)

    def place(rows_of, kind):
        x, parity = block_of(picks, kind)
        for q in range(QUADS):
            rows = rows_of(q)
            at = pl.multiple_of(8 * (YS * x + 2 * q + parity), 8)
            for v in range(9):
                extra[pl.ds(at, 8), 128 * v : 128 * v + 128] = rows[8 * v : 8 * v + 8]

    for copy in copies[:5]:
        copy.wait()
    for n in range(4):
        place(lambda q: ends[n, q].astype(jnp.float32), EARLY[n])
    slices = [split_pairs(small[e], scratch) for e in range(EXTRAS)]
    for n in range(4):
        copies[5 + 2 * n].wait()
        place(lambda q: late[n, q, ROWS:, :].astype(jnp.float32), LATE[n])
    for e in range(EXTRAS):
        turned = extra[:, ROWS * e : ROWS * e + ROWS].astype(jnp.bfloat16)
        acc_extra[e] = lax.dot_general(
            turned, slices[e], (((0,), (0,)), ((), ())), preferred_element_type=jnp.float32
        )
    copies[13].wait()
    for n in range(4):
        copies[6 + 2 * n].wait()
        acc[...] += dot(wide(late.at[n]), blocks[n])

    upper = lax.broadcasted_iota(jnp.int32, (8, 128), 0) < 4

    def decode(g, carry):
        top = [jnp.zeros((8, 128), jnp.float32)] * 4
        low = [jnp.zeros((8, 128), jnp.float32)] * 4
        at = pl.multiple_of(24 * g, 8)
        for s in range(1 + EXTRAS):
            tiles = [
                acc[pl.ds(at + 8 * v, 8), :] if s == 0 else acc_extra[s - 1, pl.ds(at + 8 * v, 8), :]
                for v in range(3)
            ]
            top_r = tiles[0][:, :128] - tiles[1][:, 128:]
            top_i = tiles[0][:, 128:] + tiles[1][:, :128]
            low_r = tiles[2][:, :128] - pltpu.roll(tiles[2][:, 128:], 4, 0)
            low_i = tiles[2][:, 128:] + pltpu.roll(tiles[2][:, :128], 4, 0)
            for b in range(4):
                w_r = weights[8 * s + b]
                w_i = weights[8 * s + 4 + b]
                top[b] = top[b] + (w_r * top_r - w_i * top_i)
                low[b] = low[b] + (w_r * low_r - w_i * low_i)
        low_a = jnp.where(upper, low[0], pltpu.roll(low[1], 4, 0))
        low_b = jnp.where(upper, low[2], pltpu.roll(low[3], 4, 0))
        out[g] = jnp.concatenate(top + [low_a, low_b], axis=0)
        return carry

    lax.fori_loop(0, PAIRS, decode, 0)


def late_product(picks, weights, share, spread, before, early, late):
    return pl.pallas_call(
        late_kernel,
        out_shape=jax.ShapeDtypeStruct((PAIRS, 48, 128), jnp.float32),
        in_specs=[pl.BlockSpec(memory_space=pltpu.SMEM)] * 2 + [pl.BlockSpec(memory_space=pl.ANY)] * 11,
        out_specs=pl.BlockSpec(memory_space=pltpu.VMEM),
        scratch_shapes=[
            pltpu.VMEM((ROWS, 256), jnp.float32),
            pltpu.VMEM((4, 512, 256), jnp.bfloat16),
            pltpu.VMEM((EXTRAS, 512, 128), jnp.bfloat16),
            pltpu.VMEM((4, QUADS, 80, 128), jnp.bfloat16),
            pltpu.VMEM((4, QUADS, CHUNK_ROWS, 128), jnp.bfloat16),
            pltpu.VMEM((256, 1152), jnp.float32),
            pltpu.VMEM((EXTRAS, ROWS, 256), jnp.float32),
            pltpu.VMEM((512, 128), jnp.float32),
            pltpu.SemaphoreType.DMA((14,)),
        ],
        name="late_product",
        interpret=INTERPRET,
    )(picks, weights, share, spread, before, *early, *late)


def choose(responding_nodes):
    listed = jnp.any(
        responding_nodes[:, None] == jnp.arange(NODE_NUMBER, dtype=jnp.int32)[None, :], axis=0
    ).reshape(PAIRS, 2)
    both = listed[:, 0] & listed[:, 1]
    index = jnp.arange(PAIRS, dtype=jnp.int32)
    before = jnp.sum((index[None, :] < index[:, None]) & both[None, :], axis=1)
    extra_pair = both[None, :] & (before[None, :] == jnp.arange(EXTRAS, dtype=jnp.int32)[:, None])
    return listed[:, 0], extra_pair


def summed(received):
    total = jnp.sum(received, axis=0)
    top = total[:32].reshape(2, 2, 8, 128)
    low = total[32:].reshape(2, 2, 4, 128)
    return jnp.concatenate([top, low], axis=2).transpose(0, 2, 1, 3)


def shards(source_matrix_tiles, second_operand_encoded, responding_nodes):
    sent = encode(
        responding_nodes, jnp.asarray(trig_table().reshape(-1)), source_matrix_tiles.reshape(96, 128)
    ).reshape(PAIRS * QUADS, 32, 128)
    got = lax.all_to_all(sent, ("group", "quad"), split_axis=0, concat_axis=0, tiled=True)

    odd = second_operand_encoded[1].reshape(PANELS, PAIRS, 8, 2, 128).transpose(1, 0, 2, 3, 4)
    spread = lax.all_to_all(odd, "group", split_axis=0, concat_axis=0, tiled=True)
    even_listed, _ = choose(responding_nodes)
    group = lax.axis_index("group")
    second = jnp.where(even_listed[group], 0, 1).astype(jnp.int32)
    picks = jnp.stack([second, lax.axis_index("x"), lax.axis_index("parity")]).astype(jnp.int32)
    share = split_share(picks, second_operand_encoded.reshape(2, 8192, 128))
    a = compact(got)

    def shift(chunk, by):
        return lax.ppermute(chunk, "x", [(i, (i + by) % XS) for i in range(XS)])

    responding_nodes, a = lax.optimization_barrier((responding_nodes, a))
    b = lax.ppermute(a, "parity", [(0, 1), (1, 0)])
    right_a, left_a = shift(a, 1), shift(a, -1)
    right_b, left_b = shift(b, 1), shift(b, -1)
    far_a, far_b = shift(right_a, 1), shift(left_b, -1)

    coefficient_actual, coefficient_image = recovery_coefficients(responding_nodes)
    _, extra_pair = choose(responding_nodes)
    extra_group = jnp.sum(
        jnp.where(extra_pair, jnp.arange(PAIRS, dtype=jnp.int32)[None, :], 0), axis=1
    ).astype(jnp.int32)
    used = jnp.concatenate([(2 * group + second)[None], 2 * extra_group + 1])
    point_selector = (used[:, None] == responding_nodes[None, :])[:, :, None]
    weights = jnp.concatenate(
        [
            jnp.sum(jnp.where(point_selector, coefficient_actual[None], 0.0), axis=1),
            jnp.sum(jnp.where(point_selector, coefficient_image[None], 0.0), axis=1),
        ],
        axis=1,
    ).reshape(-1)

    early = (a, b, right_a, left_a)
    before = early_product(picks, share, early)
    three = jnp.stack(
        [lax.dynamic_index_in_dim(spread, extra_group[e], 0, keepdims=False) for e in range(EXTRAS)]
    ).reshape(EXTRAS, 512, 128)
    partial = late_product(
        picks, weights, share, three, before, early, (right_b, left_b, far_a, far_b)
    )
    received = lax.all_to_all(partial, "group", split_axis=0, concat_axis=0, tiled=True)
    return summed(received)


def solution(mesh):
    torus = Mesh(
        mesh.devices.reshape(mesh.shape["group"], XS, QUADS, 2), ("group", "x", "quad", "parity")
    )
    panel = ("x", "quad", "parity")
    return jax.shard_map(
        shards,
        mesh=torus,
        in_specs=(P(None, "group", None, panel), P("group", None, None, panel), P()),
        out_specs=P(None, "group", None, panel),
        check_vma=False,
    )
```

time: 146 us -> 127 us (0.87)
  blocking collectives: 42.4 us -> 23.4 us
  waiting for transfers between devices: 32.9 us -> 14.8 us
  starting transfers between devices: 34.6 us -> 43.4 us
  between operations: 0.9 us -> 6.65 us
  Pallas kernels: 13.7 us -> 18.1 us
  local copies, waits for them, and re-layouts: 13.2 us -> 8.89 us
  matrix products: 1.34 us -> 5.23 us
    all_gather x1 -> x0, blocking collectives: 23.1 us -> none  [shards(): own = lax.all_gather(compact(got), 'y')]
    all_to_all x1, waiting for transfers between devices: 26.5 us -> 6.41 us  [shards(): lax.all_to_all(odd, 'group', split_axis=0, concat_axis=0, tiled=True)]
    ppermute x4 -> x7, starting transfers between devices: 13.8 us -> 20.9 us  [the longest x6 19 us: shift(): return lax.ppermute(chunk, 'x', [(i, (i + by) % XS) for i in range(XS)])]
    all_to_all x1, starting transfers between devices: 11.8 us -> 17.6 us  [shards(): lax.all_to_all(sent, ('group', 'quad'), split_axis=0, concat_axis=0, tile...]
    pallas_call x4 -> x5, Pallas kernels: 13.7 us -> 18.1 us  [the longest x1 5.66 us: late_product(): pl.pallas_call(late_kernel, out_shape=jax.ShapeDtypeStruct((PAIRS, 48, 12...]
    all_to_all x1, starting transfers between devices: 9.03 us -> 4.85 us  [shards(): lax.all_to_all(odd, 'group', split_axis=0, concat_axis=0, tiled=True)]
    all_to_all x1, blocking collectives: 19.3 us -> 23.4 us  [shards(): lax.all_to_all(partial, 'group', split_axis=0, concat_axis=0, tiled=True)]
    all_to_all x1, waiting for transfers between devices: 3.76 us -> 6.81 us  [shards(): lax.all_to_all(sent, ('group', 'quad'), split_axis=0, concat_axis=0, tile...]
  transfers between devices with their start and end apart: 6 -> 9, of which waited for: 4 -> 5; matrix products, arithmetic and copies ran while one was open for 7% -> 13% of each run, Pallas kernels for 3% -> 8%
where the time goes in v2:
time: 127 us; the launch traced here: 126 us
  starting transfers between devices  43.4 us (34%)
  blocking collectives  23.4 us (18%)
  Pallas kernels  18.1 us (14%)
  waiting for transfers between devices  14.8 us (12%)
  local copies, waits for them, and re-layouts  8.89 us (7%)
  between operations  6.65 us (5%)
  other arithmetic  5.9 us (5%)
  matrix products  5.23 us (4%)
    all_to_all x1, blocking collectives, shards(): lax.all_to_all(partial, 'group', split_axis=0, concat_axis=0, tiled=True)  23.4 us
    ppermute x6, starting transfers between devices, shift(): return lax.ppermute(chunk, 'x', [(i, (i + by) % XS) for i in range(XS)])  19 us
    all_to_all x1, starting transfers between devices, shards(): lax.all_to_all(sent, ('group', 'quad'), split_axis=0, concat_axis=0, tile...  17.6 us
    all_to_all x1, waiting for transfers between devices, shards(): lax.all_to_all(sent, ('group', 'quad'), split_axis=0, concat_axis=0, tile...  6.81 us
    all_to_all x1, waiting for transfers between devices, shards(): lax.all_to_all(odd, 'group', split_axis=0, concat_axis=0, tiled=True)  6.41 us
    pallas_call x1, Pallas kernels, late_product(): pl.pallas_call(late_kernel, out_shape=jax.ShapeDtypeStruct((PAIRS, 48, 12...  5.66 us
    all_to_all x1, starting transfers between devices, shards(): lax.all_to_all(odd, 'group', split_axis=0, concat_axis=0, tiled=True)  4.85 us
    pallas_call x1, Pallas kernels, split_share(): pl.pallas_call(share_kernel, out_shape=jax.ShapeDtypeStruct((XS, 2, 512,...  4.66 us
  transfers between devices with their start and end apart: 9, of which 5 were waited for; matrix products, arithmetic and copies ran while one was open for 13% of the time, Pallas kernels for 8%

profile of v2, /device:TPU:1, one launch (start us, length us, event | category | flops | bytes accessed | tf_op | source)
XLA Modules:
  0.0 126.5 jit_solution(16601507314724796490)
XLA Ops:
  0.0 2.1 %encode.1 = bf16[16,4,32,128]{3,2,1,0:T(8,128)(2,1)} custom-call(s32[19]{0:T(128)} %nodes.1, f32[512]{0:T(512)} %constant.67.clone.table, bf16[96,128]{1,0:T(8,128)(2,1)} %bitcast.45), custom_call_target="tpu_custom_call" | custom-call | tf_op jit(solution)/shard_map/encode/pallas_call | solution.py:136
  2.1 17.6 %all-to-all-start = ((bf16[64,32,128]{2,1,0:T(8,128)(2,1)}), bf16[64,32,128]{2,1,0:T(8,128)(2,1)S(1)}, u32[]{:S(2)}, u32[]{:S(2)}) async-start(bf16[64,32,128]{2,1,0:T(8,128)(2,1)} %bitcast.41), calls=%async_computation | async-start | bytes 1048576 | tf_op jit(solution)/shard_map/all_to_all | solution.py:386
  19.8 1.6 %slice-done = bf16[1,4096,2,128]{3,2,1,0:T(2,128)(2,1)S(1)} async-done(((bf16[2,4096,2,128]{3,2,1,0:T(2,128)(2,1)}), bf16[1,4096,2,128]{3,2,1,0:T(2,128)(2,1)S(1)}, s32[]{:S(2)}) %slice-start) | async-done | bytes 2097176 | tf_op jit(solution)/shard_map/slice | solution.py:388
  21.4 3.4 %copy.15 = bf16[32,16,8,2,128]{4,3,2,0,1:T(2,128)(2,1)} copy(bf16[32,16,8,2,128]{4,3,2,1,0:T(2,128)(2,1)S(1)} %bitcast.40) | data formatting | bytes 4194304 | tf_op jit(solution)/shard_map/reshape;squeeze | solution.py:388
  26.1 1.2 pad_add_fusion.picks
  27.3 4.7 %split_share.1.share = bf16[4,2,512,256]{3,2,1,0:T(8,128)(2,1)} custom-call(s32[3]{0:T(128)} %pad_add_fusion.picks, bf16[2,8192,128]{2,1,0:T(8,128)(2,1)} %bitcast.39), custom_call_target="tpu_custom_call" | custom-call | flops 400000000 | bytes 4200000 | tf_op jit(solution)/shard_map/split_share/pallas_call | solution.py:210
  33.2 6.8 %all-to-all-done.got = bf16[64,32,128]{2,1,0:T(8,128)(2,1)S(1)} async-done(((bf16[64,32,128]{2,1,0:T(8,128)(2,1)}), bf16[64,32,128]{2,1,0:T(8,128)(2,1)S(1)}, u32[]{:S(2)}, u32[]{:S(2)}) %all-to-all-start) | async-done | bytes 524320 | tf_op jit(solution)/shard_map/all_to_all | solution.py:386
  40.8 4.8 %all-to-all-start.1 = ((bf16[16,32,8,2,128]{4,3,2,1,0:T(2,128)(2,1)}), bf16[16,32,8,2,128]{4,3,2,1,0:T(2,128)(2,1)S(1)}, u32[]{:S(2)}, u32[]{:S(2)}) async-start(bf16[16,32,8,2,128]{4,3,2,1,0:T(2,128)(2,1)} %bitcast.37), calls=%async_computation.1 | async-start | bytes 4194304 | tf_op jit(solution)/shard_map/all_to_all | solution.py:389
  45.7 2.2 %compact.1.a.c0 = bf16[4,464,128]{2,1,0:T(8,128)(2,1)} custom-call(bf16[64,32,128]{2,1,0:T(8,128)(2,1)} %copy-done), custom_call_target="tpu_custom_call" | custom-call | tf_op jit(solution)/shard_map/compact/pallas_call | solution.py:184
  47.9 1.9 %collective-permute-start = (bf16[4,464,128]{2,1,0:T(8,128)(2,1)}, bf16[4,464,128]{2,1,0:T(8,128)(2,1)S(1)}, u32[]{:S(2)}, u32[]{:S(2)}) collective-permute-start(bf16[4,464,128]{2,1,0:T(8,128)(2,1)} %compact.1.a.c0), channel_id=1, source_target_pairs={{0,1},{1,0},{2,3},{3,2},{4,5},{5,4},{6,7},{7,6},{8,9},{9,8},{10,11... | collective-permute-start | bytes 1425416 | tf_op jit(solution)/shard_map/ppermute | solution.py:401
  49.8 3.1 %collective-permute-start.1 = (bf16[4,464,128]{2,1,0:T(8,128)(2,1)}, bf16[4,464,128]{2,1,0:T(8,128)(2,1)S(1)}, u32[]{:S(2)}, u32[]{:S(2)}) collective-permute-start(bf16[4,464,128]{2,1,0:T(8,128)(2,1)} %compact.1.a.c0), channel_id=1, source_target_pairs={{0,8},{8,16},{16,24},{24,0},{1,9},{9,17},{17,25},{25,1},{2,10},{10... | collective-permute-start | bytes 1425416 | tf_op jit(solution)/shard_map/ppermute | solution.py:398
  53.0 3.4 %collective-permute-start.2 = (bf16[4,464,128]{2,1,0:T(8,128)(2,1)}, bf16[4,464,128]{2,1,0:T(8,128)(2,1)S(1)}, u32[]{:S(2)}, u32[]{:S(2)}) collective-permute-start(bf16[4,464,128]{2,1,0:T(8,128)(2,1)} %compact.1.a.c0), channel_id=1, source_target_pairs={{0,24},{8,0},{16,8},{24,16},{1,25},{9,1},{17,9},{25,17},{2,26},{10... | collective-permute-start | bytes 1425416 | tf_op jit(solution)/shard_map/ppermute | solution.py:398
  58.6 1.6 %fusion = f32[19,4]{0,1:T(4,128)} fusion(f32[19,1,32]{2,0,1:T(8,128)S(1)} %get-tuple-element.14, f32[4]{0:T(128)} %multiply_add_fusion.6, f32[32]{0:T(128)} %fusion.21), kind=kOutput, calls=%fused_computation.19 | convolution fusion | flops 29312 | bytes 2880 | tf_op jit(solution)/shard_map/dot_general | solution.py:69
  60.2 1.6 %convolution_add_fusion = f32[19,4]{0,1:T(4,128)} fusion(f32[19,4]{0,1:T(4,128)S(1)} %fusion.1, f32[19,1,32]{2,0,1:T(8,128)S(1)} %get-tuple-element.13, f32[4]{0:T(128)} %multiply_add_fusion.6, f32[32]{0:T(128)} %fusion.21), kind=kOutput, calls=%fused_computation.1 | convolution fusion | flops 29388 | bytes 3184 | tf_op jit(solution)/shard_map/dot_general | solution.py:74
  62.2 4.4 %collective-permute-start.4 = (bf16[4,464,128]{2,1,0:T(8,128)(2,1)S(1)}, bf16[4,464,128]{2,1,0:T(8,128)(2,1)}, u32[]{:S(2)}, u32[]{:S(2)}) collective-permute-start(bf16[4,464,128]{2,1,0:T(8,128)(2,1)S(1)} %collective-permute-done.b.c1), channel_id=1, source_target_pairs={{0,24},{8,0},{16,8},{24,16},{1,25},{9,1},{17,9},{25,17},{2,26},{10... | collective-permute-start | bytes 1425416 | tf_op jit(solution)/shard_map/ppermute | solution.py:398
  71.2 1.0 subtract_divide_fusion
  72.2 1.9 %collective-permute-start.3 = (bf16[4,464,128]{2,1,0:T(8,128)(2,1)S(1)}, bf16[4,464,128]{2,1,0:T(8,128)(2,1)}, u32[]{:S(2)}, u32[]{:S(2)}) collective-permute-start(bf16[4,464,128]{2,1,0:T(8,128)(2,1)S(1)} %collective-permute-done.b.c1), channel_id=1, source_target_pairs={{0,8},{8,16},{16,24},{24,0},{1,9},{9,17},{17,25},{25,1},{2,10},{10... | collective-permute-start | bytes 1425416 | tf_op jit(solution)/shard_map/ppermute | solution.py:398
  74.2 2.1 %collective-permute-start.5 = (bf16[4,464,128]{2,1,0:T(8,128)(2,1)S(1)}, bf16[4,464,128]{2,1,0:T(8,128)(2,1)}, u32[]{:S(2)}, u32[]{:S(2)}) collective-permute-start(bf16[4,464,128]{2,1,0:T(8,128)(2,1)S(1)} %collective-permute-done.1.right_a.c2), channel_id=1, source_target_pairs={{0,8},{8,16},{16,24},{24,0},{1,9},{9,17},{17,25},{25,1},{2,10},{10... | collective-permute-start | bytes 1425416 | tf_op jit(solution)/shard_map/ppermute | solution.py:398
  77.3 4.1 %collective-permute-start.6 = (bf16[4,464,128]{2,1,0:T(8,128)(2,1)}, bf16[4,464,128]{2,1,0:T(8,128)(2,1)}, u32[]{:S(2)}, u32[]{:S(2)}) collective-permute-start(bf16[4,464,128]{2,1,0:T(8,128)(2,1)} %collective-permute-done.4.c5), channel_id=1, source_target_pairs={{0,24},{8,0},{16,8},{24,16},{1,25},{9,1},{17,9},{25,17},{2,26},{10... | collective-permute-start | bytes 1425416 | tf_op jit(solution)/shard_map/ppermute | solution.py:398
  84.9 3.5 %early_product.1.before = f32[384,256]{1,0:T(8,128)} custom-call(s32[3]{0:T(128)} %pad_add_fusion.picks, bf16[4,2,512,256]{3,2,1,0:T(8,128)(2,1)} %split_share.1.share, bf16[4,464,128]{2,1,0:T(8,128)(2,1)} %compact.1.a.c0, bf16[4,464,128]{2,1,0:T(8,128)(2,1)} %copy-done.1, bf16[4,464,128]{2,1,0:T(8,128)(2,1)} %copy-done.2, bf16[4,464,128]{2,1,0:T(8,128)(2,1)} %copy-done.3), custom_call_target="tpu_custom_call" | custom-call | flops 400000000 | bytes 4200000 | tf_op jit(solution)/shard_map/early_product/pallas_call | solution.py:255
  88.4 6.4 %all-to-all-done.1 = bf16[16,32,8,2,128]{4,3,2,1,0:T(2,128)(2,1)S(1)} async-done(((bf16[16,32,8,2,128]{4,3,2,1,0:T(2,128)(2,1)}), bf16[16,32,8,2,128]{4,3,2,1,0:T(2,128)(2,1)S(1)}, u32[]{:S(2)}, u32[]{:S(2)}) %all-to-all-start.1) | async-done | bytes 2097184 | tf_op jit(solution)/shard_map/all_to_all | solution.py:389
  95.1 1.4 %pad_maximum_fusion = bf16[3,32,8,2,128]{4,3,2,1,0:T(2,128)(2,1)} fusion(bf16[1,32,8,2,128]{4,3,2,1,0:T(2,128)(2,1)S(1)} %get-tuple-element.16, bf16[1,32,8,2,128]{4,3,2,1,0:T(2,128)(2,1)S(1)} %get-tuple-element.17, bf16[1,32,8,2,128]{4,3,2,1,0:T(2,128)(2,1)S(1)} %get-tuple-element.15), kind=kLoop, calls=%fused_computation.3 | loop fusion | flops 393216 | bytes 786432 | tf_op jit(solution)/shard_map/stack | solution.py:423
  96.7 5.7 %late_product.1 = f32[16,48,128]{2,1,0:T(8,128)} custom-call(s32[3]{0:T(128)} %pad_add_fusion.picks, f32[32]{0:T(128)} %reshape.173.weights, bf16[4,2,512,256]{3,2,1,0:T(8,128)(2,1)} %split_share.1.share, bf16[3,512,128]{2,1,0:T(8,128)(2,1)} %bitcast.42, f32[384,256]{1,0:T(8,128)} %early_product.1.before, bf16[4,464,128]{2,1,0:T(8,128)(2,1)} %compact.1.a.c0, ...), custom_call_target="tpu_custom_call" | custom-call | tf_op jit(solution)/shard_map/late_product/pallas_call | solution.py:343
  102.3 23.4 %all_to_all.15 = f32[16,48,128]{2,1,0:T(8,128)S(1)} all-to-all(f32[16,48,128]{2,1,0:T(8,128)} %late_product.1), channel_id=1, replica_groups=mesh['group'=16,'x'=4,'quad'=4,'parity'=2] {'group'}, dimensions={0} | all-to-all | bytes 786432 | tf_op jit(solution)/shard_map/all_to_all | solution.py:429
  (54 shorter events, 9.8 us)
Async XLA Ops:
  2.1 37.9 %all-to-all-start = ((bf16[64,32,128]{2,1,0:T(8,128)(2,1)}), bf16[64,32,128]{2,1,0:T(8,128)(2,1)S(1)}, u32[]{:S(2)}, u32[]{:S(2)}) async-start(bf16[64,32,128]{2,1,0:T(8,128)(2,1)} %bitcast.41), calls=%async_computation | async-start | bytes 1048576 | tf_op jit(solution)/shard_map/all_to_all | solution.py:386
  19.8 1.6 %slice-start = ((bf16[2,4096,2,128]{3,2,1,0:T(2,128)(2,1)}), bf16[1,4096,2,128]{3,2,1,0:T(2,128)(2,1)S(1)}, s32[]{:S(2)}) async-start(bf16[2,4096,2,128]{3,2,1,0:T(2,128)(2,1)} %param.5), calls=%async_computation.3 | async-start | bytes 4194304 | tf_op jit(solution)/shard_map/slice | solution.py:388
  21.4 3.4 %copy-start.4 = (s32[19]{0:T(128)S(1)}, s32[19]{0:T(128)}, u32[]{:S(2)}) copy-start(s32[19]{0:T(128)} %nodes.1) | copy-start | bytes 232
  40.0 0.8 copy-start
  40.8 54.0 %all-to-all-start.1 = ((bf16[16,32,8,2,128]{4,3,2,1,0:T(2,128)(2,1)}), bf16[16,32,8,2,128]{4,3,2,1,0:T(2,128)(2,1)S(1)}, u32[]{:S(2)}, u32[]{:S(2)}) async-start(bf16[16,32,8,2,128]{4,3,2,1,0:T(2,128)(2,1)} %bitcast.37), calls=%async_computation.1 | async-start | bytes 4194304 | tf_op jit(solution)/shard_map/all_to_all | solution.py:389
  47.9 14.3 %collective-permute-start = (bf16[4,464,128]{2,1,0:T(8,128)(2,1)}, bf16[4,464,128]{2,1,0:T(8,128)(2,1)S(1)}, u32[]{:S(2)}, u32[]{:S(2)}) collective-permute-start(bf16[4,464,128]{2,1,0:T(8,128)(2,1)} %compact.1.a.c0), channel_id=1, source_target_pairs={{0,1},{1,0},{2,3},{3,2},{4,5},{5,4},{6,7},{7,6},{8,9},{9,8},{10,11... | collective-permute-start | bytes 1425416 | tf_op jit(solution)/shard_map/ppermute | solution.py:401
  49.8 24.3 %collective-permute-start.1 = (bf16[4,464,128]{2,1,0:T(8,128)(2,1)}, bf16[4,464,128]{2,1,0:T(8,128)(2,1)S(1)}, u32[]{:S(2)}, u32[]{:S(2)}) collective-permute-start(bf16[4,464,128]{2,1,0:T(8,128)(2,1)} %compact.1.a.c0), channel_id=1, source_target_pairs={{0,8},{8,16},{16,24},{24,0},{1,9},{9,17},{17,25},{25,1},{2,10},{10... | collective-permute-start | bytes 1425416 | tf_op jit(solution)/shard_map/ppermute | solution.py:398
  53.0 31.1 %collective-permute-start.2 = (bf16[4,464,128]{2,1,0:T(8,128)(2,1)}, bf16[4,464,128]{2,1,0:T(8,128)(2,1)S(1)}, u32[]{:S(2)}, u32[]{:S(2)}) collective-permute-start(bf16[4,464,128]{2,1,0:T(8,128)(2,1)} %compact.1.a.c0), channel_id=1, source_target_pairs={{0,24},{8,0},{16,8},{24,16},{1,25},{9,1},{17,9},{25,17},{2,26},{10... | collective-permute-start | bytes 1425416 | tf_op jit(solution)/shard_map/ppermute | solution.py:398
  62.2 21.9 %copy-start.1 = (bf16[4,464,128]{2,1,0:T(8,128)(2,1)}, bf16[4,464,128]{2,1,0:T(8,128)(2,1)S(1)}, u32[]{:S(2)}) copy-start(bf16[4,464,128]{2,1,0:T(8,128)(2,1)S(1)} %collective-permute-done.b.c1) | copy-start | bytes 1425412
  62.2 15.1 %collective-permute-start.4 = (bf16[4,464,128]{2,1,0:T(8,128)(2,1)S(1)}, bf16[4,464,128]{2,1,0:T(8,128)(2,1)}, u32[]{:S(2)}, u32[]{:S(2)}) collective-permute-start(bf16[4,464,128]{2,1,0:T(8,128)(2,1)S(1)} %collective-permute-done.b.c1), channel_id=1, source_target_pairs={{0,24},{8,0},{16,8},{24,16},{1,25},{9,1},{17,9},{25,17},{2,26},{10... | collective-permute-start | bytes 1425416 | tf_op jit(solution)/shard_map/ppermute | solution.py:398
  72.2 24.3 %collective-permute-start.3 = (bf16[4,464,128]{2,1,0:T(8,128)(2,1)S(1)}, bf16[4,464,128]{2,1,0:T(8,128)(2,1)}, u32[]{:S(2)}, u32[]{:S(2)}) collective-permute-start(bf16[4,464,128]{2,1,0:T(8,128)(2,1)S(1)} %collective-permute-done.b.c1), channel_id=1, source_target_pairs={{0,8},{8,16},{16,24},{24,0},{1,9},{9,17},{17,25},{25,1},{2,10},{10... | collective-permute-start | bytes 1425416 | tf_op jit(solution)/shard_map/ppermute | solution.py:398
  74.1 10.0 %copy-start.2 = (bf16[4,464,128]{2,1,0:T(8,128)(2,1)}, bf16[4,464,128]{2,1,0:T(8,128)(2,1)S(1)}, u32[]{:S(2)}) copy-start(bf16[4,464,128]{2,1,0:T(8,128)(2,1)S(1)} %collective-permute-done.1.right_a.c2) | copy-start | bytes 1425412
  74.2 22.5 %collective-permute-start.5 = (bf16[4,464,128]{2,1,0:T(8,128)(2,1)S(1)}, bf16[4,464,128]{2,1,0:T(8,128)(2,1)}, u32[]{:S(2)}, u32[]{:S(2)}) collective-permute-start(bf16[4,464,128]{2,1,0:T(8,128)(2,1)S(1)} %collective-permute-done.1.right_a.c2), channel_id=1, source_target_pairs={{0,8},{8,16},{16,24},{24,0},{1,9},{9,17},{17,25},{25,1},{2,10},{10... | collective-permute-start | bytes 1425416 | tf_op jit(solution)/shard_map/ppermute | solution.py:398
  77.3 19.4 %collective-permute-start.6 = (bf16[4,464,128]{2,1,0:T(8,128)(2,1)}, bf16[4,464,128]{2,1,0:T(8,128)(2,1)}, u32[]{:S(2)}, u32[]{:S(2)}) collective-permute-start(bf16[4,464,128]{2,1,0:T(8,128)(2,1)} %collective-permute-done.4.c5), channel_id=1, source_target_pairs={{0,24},{8,0},{16,8},{24,16},{1,25},{9,1},{17,9},{25,17},{2,26},{10... | collective-permute-start | bytes 1425416 | tf_op jit(solution)/shard_map/ppermute | solution.py:398
  84.1 0.8 copy-start.3

commit v3 on v2

--- a/solution.py
+++ b/solution.py
@@ -125,8 +125,7 @@
         parts = block(2 * t + 1 - flags[2 * t])
         parts.append(stack[pl.ds(pl.multiple_of(8 * t, 8), 8), :])
         value = jnp.concatenate(parts, axis=0).astype(jnp.bfloat16)
-        for q in range(QUADS):
-            out[t, q] = value
+        out[t] = value
         return carry
 
     lax.fori_loop(0, PAIRS, main, 0)
@@ -135,7 +134,7 @@
 def encode(nodes, table, source):
     return pl.pallas_call(
         encode_kernel,
-        out_shape=jax.ShapeDtypeStruct((PAIRS, QUADS, 32, 128), jnp.bfloat16),
+        out_shape=jax.ShapeDtypeStruct((PAIRS, 32, 128), jnp.bfloat16),
         in_specs=[
             pl.BlockSpec(memory_space=pltpu.SMEM),
             pl.BlockSpec(memory_space=pltpu.SMEM),
@@ -156,34 +155,29 @@
 def compact_kernel(got, out, rows):
     lane = lax.broadcasted_iota(jnp.int32, (8, 128), 1)
     rows[ROWS + 72 :, :] = jnp.zeros((8, 128), jnp.float32)
-
-    def one(q, carry):
-        pieces = []
-        for g in range(PAIRS):
-            block = got[QUADS * g + q].astype(jnp.float32)
-            rows[24 * g : 24 * g + 24, :] = block[:24]
-            pieces.append(block[24:])
-        for e in range(EXTRAS):
-            for v in range(3):
-                tile = jnp.zeros((8, 128), jnp.float32)
-                for g in range(PAIRS):
-                    start = 24 * g - 128 * v
-                    if start + 24 <= 0 or start >= 128:
-                        continue
-                    moved = pltpu.roll(pieces[g], (start - 24 * e) % 128, 1)
-                    tile = jnp.where((lane >= start) & (lane < start + 24), moved, tile)
-                at = ROWS + 8 * (3 * e + v)
-                rows[at : at + 8, :] = tile
-        out[q] = rows[...].astype(jnp.bfloat16)
-        return carry
-
-    lax.fori_loop(0, QUADS, one, 0)
+    pieces = []
+    for g in range(PAIRS):
+        block = got[g].astype(jnp.float32)
+        rows[24 * g : 24 * g + 24, :] = block[:24]
+        pieces.append(block[24:])
+    for e in range(EXTRAS):
+        for v in range(3):
+            tile = jnp.zeros((8, 128), jnp.float32)
+            for g in range(PAIRS):
+                start = 24 * g - 128 * v
+                if start + 24 <= 0 or start >= 128:
+                    continue
+                moved = pltpu.roll(pieces[g], (start - 24 * e) % 128, 1)
+                tile = jnp.where((lane >= start) & (lane < start + 24), moved, tile)
+            at = ROWS + 8 * (3 * e + v)
+            rows[at : at + 8, :] = tile
+    out[...] = rows[...].astype(jnp.bfloat16)
 
 
 def compact(got):
     return pl.pallas_call(
         compact_kernel,
-        out_shape=jax.ShapeDtypeStruct((QUADS, CHUNK_ROWS, 128), jnp.bfloat16),
+        out_shape=jax.ShapeDtypeStruct((CHUNK_ROWS, 128), jnp.bfloat16),
         in_specs=[pl.BlockSpec(memory_space=pltpu.VMEM)],
         out_specs=pl.BlockSpec(memory_space=pltpu.VMEM),
         scratch_shapes=[pltpu.VMEM((CHUNK_ROWS, 128), jnp.float32)],
@@ -231,8 +225,8 @@
     return jnp.dot(a, b, preferred_element_type=jnp.float32)
 
 
-EARLY = ((0, True), (0, False), (-1, True), (1, True))
-LATE = ((-1, False), (1, False), (2, True), (2, False))
+EARLY = ((0, True), (0, False), (-1, True), (1, True), (-1, False), (1, False))
+LATE = ((2, True), (2, False))
 
 
 def block_of(picks, kind):
@@ -241,8 +235,8 @@
     return x, picks[2] if same else 1 - picks[2]
 
 
-def early_kernel(picks, share, a, b, right_a, left_a, acc):
-    for n, (chunk, kind) in enumerate(zip((a, b, right_a, left_a), EARLY)):
+def early_kernel(picks, share, c0, c1, c2, c3, c4, c5, acc):
+    for n, (chunk, kind) in enumerate(zip((c0, c1, c2, c3, c4, c5), EARLY)):
         x, parity = block_of(picks, kind)
         term = dot(wide(chunk), share[x, parity])
         if n == 0:
@@ -255,7 +249,7 @@
     return pl.pallas_call(
         early_kernel,
         out_shape=jax.ShapeDtypeStruct((ROWS, 256), jnp.float32),
-        in_specs=[pl.BlockSpec(memory_space=pltpu.SMEM)] + [pl.BlockSpec(memory_space=pltpu.VMEM)] * 5,
+        in_specs=[pl.BlockSpec(memory_space=pltpu.SMEM)] + [pl.BlockSpec(memory_space=pltpu.VMEM)] * 7,
         out_specs=pl.BlockSpec(memory_space=pltpu.VMEM),
         name="early_product",
         cost_estimate=pl.CostEstimate(flops=400_000_000, bytes_accessed=4_200_000, transcendentals=0),
@@ -267,8 +261,8 @@
     picks, weights, share, spread, before, c0, c1, c2, c3, c4, c5, c6, c7, out,
     acc, blocks, small, ends, late, extra, acc_extra, scratch, sems,
 ):
-    early = (c0, c1, c2, c3)
-    chunks = (c4, c5, c6, c7)
+    early = (c0, c1, c2, c3, c4, c5)
+    chunks = (c6, c7)
     copies = []
 
     def start(source, target):
@@ -277,9 +271,9 @@
         copies.append(copy)
 
     start(spread, small)
-    for n in range(4):
+    for n in range(6):
         start(early[n].at[:, pl.ds(ROWS, 80), :], ends.at[n])
-    for n in range(4):
+    for n in range(2):
         x, parity = block_of(picks, LATE[n])
         start(chunks[n], late.at[n])
         start(share.at[x, parity], blocks.at[n])
@@ -293,22 +287,22 @@
             for v in range(9):
                 extra[pl.ds(at, 8), 128 * v : 128 * v + 128] = rows[8 * v : 8 * v + 8]
 
-    for copy in copies[:5]:
+    for copy in copies[:7]:
         copy.wait()
-    for n in range(4):
+    for n in range(6):
         place(lambda q: ends[n, q].astype(jnp.float32), EARLY[n])
     slices = [split_pairs(small[e], scratch) for e in range(EXTRAS)]
-    for n in range(4):
-        copies[5 + 2 * n].wait()
+    for n in range(2):
+        copies[7 + 2 * n].wait()
         place(lambda q: late[n, q, ROWS:, :].astype(jnp.float32), LATE[n])
     for e in range(EXTRAS):
         turned = extra[:, ROWS * e : ROWS * e + ROWS].astype(jnp.bfloat16)
         acc_extra[e] = lax.dot_general(
             turned, slices[e], (((0,), (0,)), ((), ())), preferred_element_type=jnp.float32
         )
-    copies[13].wait()
-    for n in range(4):
-        copies[6 + 2 * n].wait()
+    copies[11].wait()
+    for n in range(2):
+        copies[8 + 2 * n].wait()
         acc[...] += dot(wide(late.at[n]), blocks[n])
 
     upper = lax.broadcasted_iota(jnp.int32, (8, 128), 0) < 4
@@ -347,14 +341,14 @@
         out_specs=pl.BlockSpec(memory_space=pltpu.VMEM),
         scratch_shapes=[
             pltpu.VMEM((ROWS, 256), jnp.float32),
-            pltpu.VMEM((4, 512, 256), jnp.bfloat16),
+            pltpu.VMEM((2, 512, 256), jnp.bfloat16),
             pltpu.VMEM((EXTRAS, 512, 128), jnp.bfloat16),
-            pltpu.VMEM((4, QUADS, 80, 128), jnp.bfloat16),
-            pltpu.VMEM((4, QUADS, CHUNK_ROWS, 128), jnp.bfloat16),
+            pltpu.VMEM((6, QUADS, 80, 128), jnp.bfloat16),
+            pltpu.VMEM((2, QUADS, CHUNK_ROWS, 128), jnp.bfloat16),
             pltpu.VMEM((256, 1152), jnp.float32),
             pltpu.VMEM((EXTRAS, ROWS, 256), jnp.float32),
             pltpu.VMEM((512, 128), jnp.float32),
-            pltpu.SemaphoreType.DMA((14,)),
+            pltpu.SemaphoreType.DMA((12,)),
         ],
         name="late_product",
         interpret=INTERPRET,
@@ -379,37 +373,14 @@
     return jnp.concatenate([top, low], axis=2).transpose(0, 2, 1, 3)
 
 
-def shards(source_matrix_tiles, second_operand_encoded, responding_nodes):
-    sent = encode(
-        responding_nodes, jnp.asarray(trig_table().reshape(-1)), source_matrix_tiles.reshape(96, 128)
-    ).reshape(PAIRS * QUADS, 32, 128)
-    got = lax.all_to_all(sent, ("group", "quad"), split_axis=0, concat_axis=0, tiled=True)
-
-    odd = second_operand_encoded[1].reshape(PANELS, PAIRS, 8, 2, 128).transpose(1, 0, 2, 3, 4)
-    spread = lax.all_to_all(odd, "group", split_axis=0, concat_axis=0, tiled=True)
-    even_listed, _ = choose(responding_nodes)
-    group = lax.axis_index("group")
-    second = jnp.where(even_listed[group], 0, 1).astype(jnp.int32)
-    picks = jnp.stack([second, lax.axis_index("x"), lax.axis_index("parity")]).astype(jnp.int32)
-    share = split_share(picks, second_operand_encoded.reshape(2, 8192, 128))
-    a = compact(got)
-
-    def shift(chunk, by):
-        return lax.ppermute(chunk, "x", [(i, (i + by) % XS) for i in range(XS)])
-
-    responding_nodes, a = lax.optimization_barrier((responding_nodes, a))
-    b = lax.ppermute(a, "parity", [(0, 1), (1, 0)])
-    right_a, left_a = shift(a, 1), shift(a, -1)
-    right_b, left_b = shift(b, 1), shift(b, -1)
-    far_a, far_b = shift(right_a, 1), shift(left_b, -1)
-
-    coefficient_actual, coefficient_image = recovery_coefficients(responding_nodes)
-    _, extra_pair = choose(responding_nodes)
+def decode_weights(nodes, group, second):
+    coefficient_actual, coefficient_image = recovery_coefficients(nodes)
+    _, extra_pair = choose(nodes)
     extra_group = jnp.sum(
         jnp.where(extra_pair, jnp.arange(PAIRS, dtype=jnp.int32)[None, :], 0), axis=1
     ).astype(jnp.int32)
     used = jnp.concatenate([(2 * group + second)[None], 2 * extra_group + 1])
-    point_selector = (used[:, None] == responding_nodes[None, :])[:, :, None]
+    point_selector = (used[:, None] == nodes[None, :])[:, :, None]
     weights = jnp.concatenate(
         [
             jnp.sum(jnp.where(point_selector, coefficient_actual[None], 0.0), axis=1),
@@ -417,15 +388,45 @@
         ],
         axis=1,
     ).reshape(-1)
-
-    early = (a, b, right_a, left_a)
+    return weights, extra_group
+
+
+def shards(source_matrix_tiles, second_operand_encoded, responding_nodes):
+    sent = encode(
+        responding_nodes, jnp.asarray(trig_table().reshape(-1)), source_matrix_tiles.reshape(96, 128)
+    )
+    got = lax.all_to_all(sent, "group", split_axis=0, concat_axis=0, tiled=True)
+
+    odd = second_operand_encoded[1].reshape(PANELS, PAIRS, 8, 2, 128).transpose(1, 0, 2, 3, 4)
+    odd, got = lax.optimization_barrier((odd, got))
+    spread = lax.all_to_all(odd, "group", split_axis=0, concat_axis=0, tiled=True)
+    even_listed, _ = choose(responding_nodes)
+    group = lax.axis_index("group")
+    second = jnp.where(even_listed[group], 0, 1).astype(jnp.int32)
+    picks = jnp.stack([second, lax.axis_index("x"), lax.axis_index("parity")]).astype(jnp.int32)
+    a = lax.all_gather(compact(got), "quad")
+
+    def hop(chunk, axis, size, by):
+        return lax.ppermute(chunk, axis, [(i, (i + by) % size) for i in range(size)])
+
+    y_axes = ("quad", "parity")
+    nodes, whole, a = lax.optimization_barrier((responding_nodes, second_operand_encoded, a))
+    right_a = hop(a, "x", XS, 1)
+    left_a = hop(a, "x", XS, -1)
+    b = hop(a, y_axes, YS, -1)
+    right_b = hop(right_a, y_axes, YS, 1)
+    left_b = hop(left_a, y_axes, YS, -1)
+    far_a = hop(right_a, "x", XS, 1)
+    far_b = hop(left_b, "x", XS, -1)
+    share = split_share(picks, whole.reshape(2, 8192, 128))
+
+    weights, extra_group = decode_weights(nodes, group, second)
+    early = (a, b, right_a, left_a, right_b, left_b)
     before = early_product(picks, share, early)
     three = jnp.stack(
         [lax.dynamic_index_in_dim(spread, extra_group[e], 0, keepdims=False) for e in range(EXTRAS)]
     ).reshape(EXTRAS, 512, 128)
-    partial = late_product(
-        picks, weights, share, three, before, early, (right_b, left_b, far_a, far_b)
-    )
+    partial = late_product(picks, weights, share, three, before, early, (far_a, far_b))
     received = lax.all_to_all(partial, "group", split_axis=0, concat_axis=0, tiled=True)
     return summed(received)
 

time: 127 us -> 137 us (1.079)
  blocking collectives: 23.4 us -> 36.2 us
  matrix products: 5.23 us -> 1.34 us
  waiting for transfers between devices: 14.8 us -> 17.4 us
    all_gather x0 -> x1, blocking collectives: none -> 16.8 us  [shards(): a = lax.all_gather(compact(got), 'quad')]
    all_to_all x1, waiting for transfers between devices: 6.81 us -> 0.01 us  [shards(): got = lax.all_to_all(sent, 'group', split_axis=0, concat_axis=0, tiled=True)]
    all_to_all x1, starting transfers between devices: 17.6 us -> 11.8 us  [shards(): got = lax.all_to_all(sent, 'group', split_axis=0, concat_axis=0, tiled=True)]
    all_to_all x1, starting transfers between devices: 4.85 us -> 9.95 us  [shards(): lax.all_to_all(odd, 'group', split_axis=0, concat_axis=0, tiled=True)]
    ppermute x7, waiting for transfers between devices: 1.61 us -> 6.5 us  [hop(): lax.ppermute(chunk, axis, [(i, (i + by) % size) for i in range(size)])]
    all_to_all x1, waiting for transfers between devices: 6.41 us -> 10.9 us  [shards(): lax.all_to_all(odd, 'group', split_axis=0, concat_axis=0, tiled=True)]
    all_to_all x1, blocking collectives: 23.4 us -> 19.3 us  [shards(): lax.all_to_all(partial, 'group', split_axis=0, concat_axis=0, tiled=True)]
  transfers between devices with their start and end apart: 9 -> 9, of which waited for: 5 -> 2; matrix products, arithmetic and copies ran while one was open for 13% -> 9% of each run, Pallas kernels for 8% -> 6%
where the time goes in v3:
time: 137 us; the launch traced here: 136 us
  starting transfers between devices  43 us (31%)
  blocking collectives  36.2 us (26%)
  waiting for transfers between devices  17.4 us (13%)
  Pallas kernels  16.9 us (12%)
  local copies, waits for them, and re-layouts  8.09 us (6%)
  between operations  6.61 us (5%)
  other arithmetic  6.33 us (5%)
    ppermute x7, starting transfers between devices, hop(): lax.ppermute(chunk, axis, [(i, (i + by) % size) for i in range(size)])  21.2 us
    all_to_all x1, blocking collectives, shards(): lax.all_to_all(partial, 'group', split_axis=0, concat_axis=0, tiled=True)  19.3 us
    all_gather x1, blocking collectives, shards(): a = lax.all_gather(compact(got), 'quad')  16.8 us
    all_to_all x1, starting transfers between devices, shards(): got = lax.all_to_all(sent, 'group', split_axis=0, concat_axis=0, tiled=True)  11.8 us
    all_to_all x1, waiting for transfers between devices, shards(): lax.all_to_all(odd, 'group', split_axis=0, concat_axis=0, tiled=True)  10.9 us
    all_to_all x1, starting transfers between devices, shards(): lax.all_to_all(odd, 'group', split_axis=0, concat_axis=0, tiled=True)  9.95 us
    ppermute x7, waiting for transfers between devices, hop(): lax.ppermute(chunk, axis, [(i, (i + by) % size) for i in range(size)])  6.5 us
    pallas_call x1, Pallas kernels, late_product(): pl.pallas_call(late_kernel, out_shape=jax.ShapeDtypeStruct((PAIRS, 48, 12...  4.67 us
  transfers between devices with their start and end apart: 9, of which 2 were waited for; matrix products, arithmetic and copies ran while one was open for 9% of the time, Pallas kernels for 6%

profile of v3, /device:TPU:1, one launch (start us, length us, event | category | flops | bytes accessed | tf_op | source)
XLA Modules:
  0.0 135.9 jit_solution(10975161450551794543)
XLA Ops:
  0.0 2.0 %encode.1 = bf16[16,32,128]{2,1,0:T(8,128)(2,1)} custom-call(s32[19]{0:T(128)} %nodes.1, f32[512]{0:T(512)} %constant.67.clone.table, bf16[96,128]{1,0:T(8,128)(2,1)} %bitcast.50), custom_call_target="tpu_custom_call" | custom-call | tf_op jit(solution)/shard_map/encode/pallas_call | solution.py:135
  2.0 11.8 %all-to-all-start = ((bf16[16,32,128]{2,1,0:T(8,128)(2,1)}), bf16[16,32,128]{2,1,0:T(8,128)(2,1)S(1)}, u32[]{:S(2)}, u32[]{:S(2)}) async-start(bf16[16,32,128]{2,1,0:T(8,128)(2,1)} %encode.1), calls=%async_computation | async-start | bytes 262144 | tf_op jit(solution)/shard_map/all_to_all | solution.py:398
  14.9 0.7 fusion.9
  15.8 1.6 %slice-done = bf16[1,4096,2,128]{3,2,1,0:T(2,128)(2,1)S(1)} async-done(((bf16[2,4096,2,128]{3,2,1,0:T(2,128)(2,1)}), bf16[1,4096,2,128]{3,2,1,0:T(2,128)(2,1)S(1)}, s32[]{:S(2)}) %slice-start) | async-done | bytes 2097176 | tf_op jit(solution)/shard_map/slice | solution.py:400
  17.4 3.4 %copy.15 = bf16[32,16,8,2,128]{4,3,2,0,1:T(2,128)(2,1)} copy(bf16[32,16,8,2,128]{4,3,2,1,0:T(2,128)(2,1)S(1)} %bitcast.40) | data formatting | bytes 4194304 | tf_op jit(solution)/shard_map/reshape;squeeze | solution.py:400
  21.8 1.1 pad_add_fusion.picks
  23.6 1.6 %compact.1 = bf16[464,128]{1,0:T(8,128)(2,1)} custom-call(bf16[16,32,128]{2,1,0:T(8,128)(2,1)} %copy-done.3), custom_call_target="tpu_custom_call" | custom-call | tf_op jit(solution)/shard_map/compact/pallas_call | solution.py:178
  25.2 16.8 %all-gather = bf16[1856,128]{1,0:T(8,128)(2,1)S(1)} all-gather(bf16[464,128]{1,0:T(8,128)(2,1)} %compact.1), channel_id=2, replica_groups=mesh['group'=16,'x'=4,'quad'=4,'parity'=2] {'quad'}, dimensions={0}, use_global_device_ids=true | all-gather | bytes 593920 | tf_op jit(solution)/shard_map/all_gather | solution.py:407
  42.2 4.4 %collective-permute-start.2 = (bf16[4,464,128]{2,1,0:T(8,128)(2,1)S(1)}, bf16[4,464,128]{2,1,0:T(8,128)(2,1)S(1)}, u32[]{:S(2)}, u32[]{:S(2)}) collective-permute-start(bf16[4,464,128]{2,1,0:T(8,128)(2,1)S(1)} %bitcast.42), channel_id=1, source_target_pairs={{0,24},{8,0},{16,8},{24,16},{1,25},{9,1},{17,9},{25,17},{2,26},{10... | collective-permute-start | bytes 1425416 | tf_op jit(solution)/shard_map/ppermute | solution.py:410
  46.6 1.9 %collective-permute-start.1 = (bf16[4,464,128]{2,1,0:T(8,128)(2,1)S(1)}, bf16[4,464,128]{2,1,0:T(8,128)(2,1)S(1)}, u32[]{:S(2)}, u32[]{:S(2)}) collective-permute-start(bf16[4,464,128]{2,1,0:T(8,128)(2,1)S(1)} %bitcast.43), channel_id=1, source_target_pairs={{0,8},{8,16},{16,24},{24,0},{1,9},{9,17},{17,25},{25,1},{2,10},{10... | collective-permute-start | bytes 1425416 | tf_op jit(solution)/shard_map/ppermute | solution.py:410
  48.5 1.9 %collective-permute-start = (bf16[4,464,128]{2,1,0:T(8,128)(2,1)S(1)}, bf16[4,464,128]{2,1,0:T(8,128)(2,1)}, u32[]{:S(2)}, u32[]{:S(2)}) collective-permute-start(bf16[4,464,128]{2,1,0:T(8,128)(2,1)S(1)} %bitcast.44), channel_id=1, source_target_pairs={{0,7},{1,0},{2,1},{3,2},{4,3},{5,4},{6,5},{7,6},{8,15},{9,8},{10,9... | collective-permute-start | bytes 1425416 | tf_op jit(solution)/shard_map/ppermute | solution.py:410
  50.5 10.0 %all-to-all-start.1 = ((bf16[16,32,8,2,128]{4,3,2,1,0:T(2,128)(2,1)}), bf16[16,32,8,2,128]{4,3,2,1,0:T(2,128)(2,1)S(1)}, u32[]{:S(2)}, u32[]{:S(2)}) async-start(bf16[16,32,8,2,128]{4,3,2,1,0:T(2,128)(2,1)} %bitcast.41), calls=%async_computation.1 | async-start | bytes 4194304 | tf_op jit(solution)/shard_map/all_to_all | solution.py:402
  63.0 3.8 %collective-permute-start.4 = (bf16[4,464,128]{2,1,0:T(8,128)(2,1)S(1)}, bf16[4,464,128]{2,1,0:T(8,128)(2,1)}, u32[]{:S(2)}, u32[]{:S(2)}) collective-permute-start(bf16[4,464,128]{2,1,0:T(8,128)(2,1)S(1)} %collective-permute-done.2.c3), channel_id=1, source_target_pairs={{0,7},{1,0},{2,1},{3,2},{4,3},{5,4},{6,5},{7,6},{8,15},{9,8},{10,9... | collective-permute-start | bytes 1425416 | tf_op jit(solution)/shard_map/ppermute | solution.py:410
  66.9 1.9 %collective-permute-start.3 = (bf16[4,464,128]{2,1,0:T(8,128)(2,1)S(1)}, bf16[4,464,128]{2,1,0:T(8,128)(2,1)}, u32[]{:S(2)}, u32[]{:S(2)}) collective-permute-start(bf16[4,464,128]{2,1,0:T(8,128)(2,1)S(1)} %collective-permute-done.1.c2), channel_id=1, source_target_pairs={{0,1},{1,2},{2,3},{3,4},{4,5},{5,6},{6,7},{7,0},{8,9},{9,10},{10,1... | collective-permute-start | bytes 1425416 | tf_op jit(solution)/shard_map/ppermute | solution.py:410
  69.0 2.4 %collective-permute-start.5 = (bf16[4,464,128]{2,1,0:T(8,128)(2,1)S(1)}, bf16[4,464,128]{2,1,0:T(8,128)(2,1)}, u32[]{:S(2)}, u32[]{:S(2)}) collective-permute-start(bf16[4,464,128]{2,1,0:T(8,128)(2,1)S(1)} %collective-permute-done.1.c2), channel_id=1, source_target_pairs={{0,8},{8,16},{16,24},{24,0},{1,9},{9,17},{17,25},{25,1},{2,10},{10... | collective-permute-start | bytes 1425416 | tf_op jit(solution)/shard_map/ppermute | solution.py:410
  71.4 6.5 %collective-permute-done.4.c5 = bf16[4,464,128]{2,1,0:T(8,128)(2,1)} collective-permute-done((bf16[4,464,128]{2,1,0:T(8,128)(2,1)S(1)}, bf16[4,464,128]{2,1,0:T(8,128)(2,1)}, u32[]{:S(2)}, u32[]{:S(2)}) %collective-permute-start.4) | collective-permute-done | bytes 475168 | tf_op jit(solution)/shard_map/ppermute | solution.py:410
  77.9 4.8 %collective-permute-start.6 = (bf16[4,464,128]{2,1,0:T(8,128)(2,1)}, bf16[4,464,128]{2,1,0:T(8,128)(2,1)}, u32[]{:S(2)}, u32[]{:S(2)}) collective-permute-start(bf16[4,464,128]{2,1,0:T(8,128)(2,1)} %collective-permute-done.4.c5), channel_id=1, source_target_pairs={{0,24},{8,0},{16,8},{24,16},{1,25},{9,1},{17,9},{25,17},{2,26},{10... | collective-permute-start | bytes 1425416 | tf_op jit(solution)/shard_map/ppermute | solution.py:410
  82.7 0.7 fusion.26
  89.9 4.7 %split_share.1.share = bf16[4,2,512,256]{3,2,1,0:T(8,128)(2,1)} custom-call(s32[3]{0:T(128)} %pad_add_fusion.picks, bf16[2,8192,128]{2,1,0:T(8,128)(2,1)} %bitcast.39), custom_call_target="tpu_custom_call" | custom-call | flops 400000000 | bytes 4200000 | tf_op jit(solution)/shard_map/split_share/pallas_call | solution.py:204
  94.6 4.0 %early_product.1.before = f32[384,256]{1,0:T(8,128)} custom-call(s32[3]{0:T(128)} %pad_add_fusion.picks, bf16[4,2,512,256]{3,2,1,0:T(8,128)(2,1)} %split_share.1.share, bf16[4,464,128]{2,1,0:T(8,128)(2,1)} %bitcast.45, bf16[4,464,128]{2,1,0:T(8,128)(2,1)} %collective-permute-done.c1, bf16[4,464,128]{2,1,0:T(8,128)(2,1)} %copy-done.2, ...), custom_call_target="tpu_custom_call" | custom-call | flops 400000000 | bytes 4200000 | tf_op jit(solution)/shard_map/early_product/pallas_call | solution.py:249
  98.5 10.9 %all-to-all-done.1 = bf16[16,32,8,2,128]{4,3,2,1,0:T(2,128)(2,1)S(1)} async-done(((bf16[16,32,8,2,128]{4,3,2,1,0:T(2,128)(2,1)}), bf16[16,32,8,2,128]{4,3,2,1,0:T(2,128)(2,1)S(1)}, u32[]{:S(2)}, u32[]{:S(2)}) %all-to-all-start.1) | async-done | bytes 2097184 | tf_op jit(solution)/shard_map/all_to_all | solution.py:402
  109.7 1.4 %pad_maximum_fusion = bf16[3,32,8,2,128]{4,3,2,1,0:T(2,128)(2,1)} fusion(bf16[1,32,8,2,128]{4,3,2,1,0:T(2,128)(2,1)S(1)} %get-tuple-element.22, bf16[1,32,8,2,128]{4,3,2,1,0:T(2,128)(2,1)S(1)} %get-tuple-element.23, bf16[1,32,8,2,128]{4,3,2,1,0:T(2,128)(2,1)S(1)} %get-tuple-element.21), kind=kLoop, calls=%fused_computation.3 | loop fusion | flops 393216 | bytes 786432 | tf_op jit(solution)/shard_map/stack | solution.py:426
  111.2 4.7 %late_product.1 = f32[16,48,128]{2,1,0:T(8,128)} custom-call(s32[3]{0:T(128)} %pad_add_fusion.picks, f32[32]{0:T(128)} %reshape.169.weights, bf16[4,2,512,256]{3,2,1,0:T(8,128)(2,1)} %split_share.1.share, bf16[3,512,128]{2,1,0:T(8,128)(2,1)} %bitcast.47, f32[384,256]{1,0:T(8,128)} %early_product.1.before, bf16[4,464,128]{2,1,0:T(8,128)(2,1)} %bitcast.46, ...), custom_call_target="tpu_custom_call" | custom-call | tf_op jit(solution)/shard_map/late_product/pallas_call | solution.py:337
  115.8 19.3 %all_to_all.15 = f32[16,48,128]{2,1,0:T(8,128)S(1)} all-to-all(f32[16,48,128]{2,1,0:T(8,128)} %late_product.1), channel_id=1, replica_groups=mesh['group'=16,'x'=4,'quad'=4,'parity'=2] {'group'}, dimensions={0} | all-to-all | bytes 786432 | tf_op jit(solution)/shard_map/all_to_all | solution.py:430
  (59 shorter events, 6.9 us)
Async XLA Ops:
  2.0 21.0 %all-to-all-start = ((bf16[16,32,128]{2,1,0:T(8,128)(2,1)}), bf16[16,32,128]{2,1,0:T(8,128)(2,1)S(1)}, u32[]{:S(2)}, u32[]{:S(2)}) async-start(bf16[16,32,128]{2,1,0:T(8,128)(2,1)} %encode.1), calls=%async_computation | async-start | bytes 262144 | tf_op jit(solution)/shard_map/all_to_all | solution.py:398
  15.8 1.6 %slice-start = ((bf16[2,4096,2,128]{3,2,1,0:T(2,128)(2,1)}), bf16[1,4096,2,128]{3,2,1,0:T(2,128)(2,1)S(1)}, s32[]{:S(2)}) async-start(bf16[2,4096,2,128]{3,2,1,0:T(2,128)(2,1)} %param.5), calls=%async_computation.3 | async-start | bytes 4194304 | tf_op jit(solution)/shard_map/slice | solution.py:400
  17.4 24.6 %copy-start.4 = (s32[19]{0:T(128)S(1)}, s32[19]{0:T(128)}, u32[]{:S(2)}) copy-start(s32[19]{0:T(128)} %nodes.1) | copy-start | bytes 232
  22.9 0.6 copy-start.3
  42.1 8.4 %copy-start = (bf16[1856,128]{1,0:T(8,128)(2,1)}, bf16[1856,128]{1,0:T(8,128)(2,1)S(1)}, u32[]{:S(2)}) copy-start(bf16[1856,128]{1,0:T(8,128)(2,1)S(1)} %all-gather) | copy-start | bytes 1425412
  42.2 20.8 %collective-permute-start.2 = (bf16[4,464,128]{2,1,0:T(8,128)(2,1)S(1)}, bf16[4,464,128]{2,1,0:T(8,128)(2,1)S(1)}, u32[]{:S(2)}, u32[]{:S(2)}) collective-permute-start(bf16[4,464,128]{2,1,0:T(8,128)(2,1)S(1)} %bitcast.42), channel_id=1, source_target_pairs={{0,24},{8,0},{16,8},{24,16},{1,25},{9,1},{17,9},{25,17},{2,26},{10... | collective-permute-start | bytes 1425416 | tf_op jit(solution)/shard_map/ppermute | solution.py:410
  46.6 20.3 %collective-permute-start.1 = (bf16[4,464,128]{2,1,0:T(8,128)(2,1)S(1)}, bf16[4,464,128]{2,1,0:T(8,128)(2,1)S(1)}, u32[]{:S(2)}, u32[]{:S(2)}) collective-permute-start(bf16[4,464,128]{2,1,0:T(8,128)(2,1)S(1)} %bitcast.43), channel_id=1, source_target_pairs={{0,8},{8,16},{16,24},{24,0},{1,9},{9,17},{17,25},{25,1},{2,10},{10... | collective-permute-start | bytes 1425416 | tf_op jit(solution)/shard_map/ppermute | solution.py:410
  48.5 46.0 %collective-permute-start = (bf16[4,464,128]{2,1,0:T(8,128)(2,1)S(1)}, bf16[4,464,128]{2,1,0:T(8,128)(2,1)}, u32[]{:S(2)}, u32[]{:S(2)}) collective-permute-start(bf16[4,464,128]{2,1,0:T(8,128)(2,1)S(1)} %bitcast.44), channel_id=1, source_target_pairs={{0,7},{1,0},{2,1},{3,2},{4,3},{5,4},{6,5},{7,6},{8,15},{9,8},{10,9... | collective-permute-start | bytes 1425416 | tf_op jit(solution)/shard_map/ppermute | solution.py:410
  50.5 59.0 %all-to-all-start.1 = ((bf16[16,32,8,2,128]{4,3,2,1,0:T(2,128)(2,1)}), bf16[16,32,8,2,128]{4,3,2,1,0:T(2,128)(2,1)S(1)}, u32[]{:S(2)}, u32[]{:S(2)}) async-start(bf16[16,32,8,2,128]{4,3,2,1,0:T(2,128)(2,1)} %bitcast.41), calls=%async_computation.1 | async-start | bytes 4194304 | tf_op jit(solution)/shard_map/all_to_all | solution.py:402
  60.5 0.6 copy-start.5
  60.5 0.7 copy-start.6
  63.0 31.6 %copy-start.1 = (bf16[4,464,128]{2,1,0:T(8,128)(2,1)}, bf16[4,464,128]{2,1,0:T(8,128)(2,1)S(1)}, u32[]{:S(2)}) copy-start(bf16[4,464,128]{2,1,0:T(8,128)(2,1)S(1)} %collective-permute-done.2.c3) | copy-start | bytes 1425412
  63.0 14.9 %collective-permute-start.4 = (bf16[4,464,128]{2,1,0:T(8,128)(2,1)S(1)}, bf16[4,464,128]{2,1,0:T(8,128)(2,1)}, u32[]{:S(2)}, u32[]{:S(2)}) collective-permute-start(bf16[4,464,128]{2,1,0:T(8,128)(2,1)S(1)} %collective-permute-done.2.c3), channel_id=1, source_target_pairs={{0,7},{1,0},{2,1},{3,2},{4,3},{5,4},{6,5},{7,6},{8,15},{9,8},{10,9... | collective-permute-start | bytes 1425416 | tf_op jit(solution)/shard_map/ppermute | solution.py:410
  66.9 27.6 %copy-start.2 = (bf16[4,464,128]{2,1,0:T(8,128)(2,1)}, bf16[4,464,128]{2,1,0:T(8,128)(2,1)S(1)}, u32[]{:S(2)}) copy-start(bf16[4,464,128]{2,1,0:T(8,128)(2,1)S(1)} %collective-permute-done.1.c2) | copy-start | bytes 1425412
  66.9 27.6 %collective-permute-start.3 = (bf16[4,464,128]{2,1,0:T(8,128)(2,1)S(1)}, bf16[4,464,128]{2,1,0:T(8,128)(2,1)}, u32[]{:S(2)}, u32[]{:S(2)}) collective-permute-start(bf16[4,464,128]{2,1,0:T(8,128)(2,1)S(1)} %collective-permute-done.1.c2), channel_id=1, source_target_pairs={{0,1},{1,2},{2,3},{3,4},{4,5},{5,6},{6,7},{7,0},{8,9},{9,10},{10,1... | collective-permute-start | bytes 1425416 | tf_op jit(solution)/shard_map/ppermute | solution.py:410
  69.0 42.1 %collective-permute-start.5 = (bf16[4,464,128]{2,1,0:T(8,128)(2,1)S(1)}, bf16[4,464,128]{2,1,0:T(8,128)(2,1)}, u32[]{:S(2)}, u32[]{:S(2)}) collective-permute-start(bf16[4,464,128]{2,1,0:T(8,128)(2,1)S(1)} %collective-permute-done.1.c2), channel_id=1, source_target_pairs={{0,8},{8,16},{16,24},{24,0},{1,9},{9,17},{17,25},{25,1},{2,10},{10... | collective-permute-start | bytes 1425416 | tf_op jit(solution)/shard_map/ppermute | solution.py:410
  77.9 33.3 %collective-permute-start.6 = (bf16[4,464,128]{2,1,0:T(8,128)(2,1)}, bf16[4,464,128]{2,1,0:T(8,128)(2,1)}, u32[]{:S(2)}, u32[]{:S(2)}) collective-permute-start(bf16[4,464,128]{2,1,0:T(8,128)(2,1)} %collective-permute-done.4.c5), channel_id=1, source_target_pairs={{0,24},{8,0},{16,8},{24,16},{1,25},{9,1},{17,9},{25,17},{2,26},{10... | collective-permute-start | bytes 1425416 | tf_op jit(solution)/shard_map/ppermute | solution.py:410

commit v4 on v3

--- a/solution.py
+++ b/solution.py
@@ -33,60 +33,71 @@
     return table.reshape(NODE_NUMBER, 16).astype(np.float32)
 
 
-def recovery_coefficients(responding_nodes):
-    responder_number = responding_nodes.shape[0]
-    grid_index = jnp.arange(NODE_NUMBER, dtype=jnp.int32)
-    grid_angle = TWO_PI_RADIANS * grid_index.astype(jnp.float32) / NODE_NUMBER
-    node_angle = TWO_PI_RADIANS * responding_nodes.astype(jnp.float32) / NODE_NUMBER
-    diff_real = jnp.cos(grid_angle)[None, :] - jnp.cos(node_angle)[:, None]
-    diff_imag = jnp.sin(grid_angle)[None, :] - jnp.sin(node_angle)[:, None]
-    ranks = jnp.arange(responder_number, dtype=jnp.int32)
-    itself = (ranks[:, None] == ranks[None, :])[:, :, None]
-    factor_real = jnp.where(itself, jnp.float32(1.0), diff_real[None])
-    factor_imag = jnp.where(itself, jnp.float32(0.0), diff_imag[None])
-    padded_width = 1 << (responder_number - 1).bit_length()
-    extra = padded_width - responder_number
-    factor_real = jnp.concatenate(
-        [factor_real, jnp.ones((responder_number, extra, NODE_NUMBER), jnp.float32)], axis=1
-    )
-    factor_imag = jnp.concatenate(
-        [factor_imag, jnp.zeros((responder_number, extra, NODE_NUMBER), jnp.float32)], axis=1
-    )
-    while factor_real.shape[1] > 1:
-        middle = factor_real.shape[1] // 2
-        left_real, right_real = (factor_real[:, :middle], factor_real[:, middle:])
-        left_imag, right_imag = (factor_imag[:, :middle], factor_imag[:, middle:])
-        factor_real = left_real * right_real - left_imag * right_imag
-        factor_imag = left_real * right_imag + left_imag * right_real
-    sample_real = factor_real[:, 0]
-    sample_imag = factor_imag[:, 0]
-    wanted = 3.0 + 4.0 * jnp.arange(4, dtype=jnp.float32)
-    table_angle = -grid_angle[:, None] * wanted[None, :]
-    table_cos = jnp.cos(table_angle)
-    table_sin = jnp.sin(table_angle)
-    highest = lax.Precision.HIGHEST
-    numer_real = (
-        jnp.dot(sample_real, table_cos, precision=highest)
-        - jnp.dot(sample_imag, table_sin, precision=highest)
-    ) / NODE_NUMBER
-    numer_imag = (
-        jnp.dot(sample_real, table_sin, precision=highest)
-        + jnp.dot(sample_imag, table_cos, precision=highest)
-    ) / NODE_NUMBER
-    onehot = (responding_nodes[:, None] == grid_index[None, :]).astype(jnp.float32)
-    denom_real = jnp.sum(onehot * sample_real, axis=1)
-    denom_imag = jnp.sum(onehot * sample_imag, axis=1)
-    magnitude = denom_real * denom_real + denom_imag * denom_imag
-    coefficient_actual = (
-        numer_real * denom_real[:, None] + numer_imag * denom_imag[:, None]
-    ) / magnitude[:, None]
-    coefficient_image = (
-        numer_imag * denom_real[:, None] - numer_real * denom_imag[:, None]
-    ) / magnitude[:, None]
-    return (coefficient_actual, coefficient_image)
-
-
-def encode_kernel(nodes, table, source, out, flags, extra_points, rows, stack):
+def grid_table():
+    grid = np.float32(TWO_PI_RADIANS) * np.arange(NODE_NUMBER, dtype=np.float32) / np.float32(NODE_NUMBER)
+    wanted = (3 + 4 * np.arange(4)).astype(np.float32)
+    turns = (-grid[None, :] * wanted[:, None]).astype(np.float64)
+    grid = grid.astype(np.float64)
+    rows = np.zeros((16, 128), np.float32)
+    rows[0, :NODE_NUMBER] = np.cos(grid)
+    rows[1, :NODE_NUMBER] = np.sin(grid)
+    rows[2:6, :NODE_NUMBER] = np.cos(turns)
+    rows[6:10, :NODE_NUMBER] = np.sin(turns)
+    return rows
+
+
+def weights_kernel(nodes, picks, points, grid, out):
+    number = nodes.shape[0]
+    shape = (24, 128)
+    row = lax.broadcasted_iota(jnp.int32, shape, 0)
+    lane = lax.broadcasted_iota(jnp.int32, shape, 1)
+    real = jnp.ones(shape, jnp.float32)
+    imag = jnp.zeros(shape, jnp.float32)
+    node = jnp.full(shape, -1, jnp.int32)
+    for t in range(number):
+        mine = row == t
+        node = jnp.where(mine, nodes[t], node)
+        step_r = jnp.where(mine, 1.0, grid[0:1, :] - points[nodes[t]])
+        step_i = jnp.where(mine, 0.0, grid[1:2, :] - points[NODE_NUMBER + nodes[t]])
+        real, imag = real * step_r - imag * step_i, real * step_i + imag * step_r
+
+    def across(value):
+        return jnp.sum(value, axis=1, keepdims=True)
+
+    here = node == lane
+    denom_r = across(jnp.where(here, real, 0.0))
+    denom_i = across(jnp.where(here, imag, 0.0))
+    magnitude = denom_r * denom_r + denom_i * denom_i
+    for e in range(4):
+        cos, sin = grid[2 + e : 3 + e, :], grid[6 + e : 7 + e, :]
+        numer_r = across(real * cos - imag * sin) / NODE_NUMBER
+        numer_i = across(real * sin + imag * cos) / NODE_NUMBER
+        weight_r = (numer_r * denom_r + numer_i * denom_i) / magnitude
+        weight_i = (numer_i * denom_r - numer_r * denom_i) / magnitude
+        for c in range(1 + EXTRAS):
+            chosen = node == picks[8 + c]
+            out[8 * c + e : 8 * c + e + 1, :] = jnp.sum(
+                jnp.where(chosen, weight_r, 0.0), axis=0, keepdims=True
+            )
+            out[8 * c + 4 + e : 8 * c + 5 + e, :] = jnp.sum(
+                jnp.where(chosen, weight_i, 0.0), axis=0, keepdims=True
+            )
+
+
+def decode_weights(nodes, picks):
+    grid = grid_table()
+    points = grid[:2, :NODE_NUMBER].reshape(-1)
+    return pl.pallas_call(
+        weights_kernel,
+        out_shape=jax.ShapeDtypeStruct((32, 128), jnp.float32),
+        in_specs=[pl.BlockSpec(memory_space=pltpu.SMEM)] * 3 + [pl.BlockSpec(memory_space=pltpu.VMEM)],
+        out_specs=pl.BlockSpec(memory_space=pltpu.VMEM),
+        name="weights",
+        interpret=INTERPRET,
+    )(nodes, picks, jnp.asarray(points), jnp.asarray(grid))
+
+
+def encode_kernel(place, nodes, table, source, out, picks, flags, extra_points, rows, stack):
     for j in range(NODE_NUMBER):
         flags[j] = 0
     for s in range(nodes.shape[0]):
@@ -95,6 +106,15 @@
     for g in range(PAIRS):
         extra_points[found] = 2 * g + 1
         found = found + flags[2 * g] * flags[2 * g + 1]
+    second = 1 - flags[2 * place[0]]
+    picks[0] = second
+    picks[1] = place[1]
+    picks[2] = place[2]
+    picks[3] = place[0] % 2
+    picks[8] = 2 * place[0] + second
+    for e in range(EXTRAS):
+        picks[4 + e] = (extra_points[e] - 1) // 2
+        picks[9 + e] = extra_points[e]
 
     rows[...] = source[...].astype(jnp.float32)
     tops = []
@@ -131,16 +151,15 @@
     lax.fori_loop(0, PAIRS, main, 0)
 
 
-def encode(nodes, table, source):
+def encode(place, nodes, table, source):
     return pl.pallas_call(
         encode_kernel,
-        out_shape=jax.ShapeDtypeStruct((PAIRS, 32, 128), jnp.bfloat16),
-        in_specs=[
-            pl.BlockSpec(memory_space=pltpu.SMEM),
-            pl.BlockSpec(memory_space=pltpu.SMEM),
-            pl.BlockSpec(memory_space=pltpu.VMEM),
-        ],
-        out_specs=pl.BlockSpec(memory_space=pltpu.VMEM),
+        out_shape=(
+            jax.ShapeDtypeStruct((PAIRS, 32, 128), jnp.bfloat16),
+            jax.ShapeDtypeStruct((16,), jnp.int32),
+        ),
+        in_specs=[pl.BlockSpec(memory_space=pltpu.SMEM)] * 3 + [pl.BlockSpec(memory_space=pltpu.VMEM)],
+        out_specs=(pl.BlockSpec(memory_space=pltpu.VMEM), pl.BlockSpec(memory_space=pltpu.SMEM)),
         scratch_shapes=[
             pltpu.SMEM((NODE_NUMBER,), jnp.int32),
             pltpu.SMEM((PAIRS,), jnp.int32),
@@ -149,7 +168,7 @@
         ],
         name="encode",
         interpret=INTERPRET,
-    )(nodes, table, source)
+    )(place, nodes, table, source)
 
 
 def compact_kernel(got, out, rows):
@@ -258,7 +277,7 @@
 
 
 def late_kernel(
-    picks, weights, share, spread, before, c0, c1, c2, c3, c4, c5, c6, c7, out,
+    picks, weights, share, s0, s1, s2, before, c0, c1, c2, c3, c4, c5, c6, c7, kept, sent,
     acc, blocks, small, ends, late, extra, acc_extra, scratch, sems,
 ):
     early = (c0, c1, c2, c3, c4, c5)
@@ -270,7 +289,8 @@
         copy.start()
         copies.append(copy)
 
-    start(spread, small)
+    for e, part in enumerate((s0, s1, s2)):
+        start(part, small.at[e])
     for n in range(6):
         start(early[n].at[:, pl.ds(ROWS, 80), :], ends.at[n])
     for n in range(2):
@@ -287,27 +307,27 @@
             for v in range(9):
                 extra[pl.ds(at, 8), 128 * v : 128 * v + 128] = rows[8 * v : 8 * v + 8]
 
-    for copy in copies[:7]:
+    for copy in copies[:9]:
         copy.wait()
     for n in range(6):
         place(lambda q: ends[n, q].astype(jnp.float32), EARLY[n])
     slices = [split_pairs(small[e], scratch) for e in range(EXTRAS)]
     for n in range(2):
-        copies[7 + 2 * n].wait()
+        copies[9 + 2 * n].wait()
         place(lambda q: late[n, q, ROWS:, :].astype(jnp.float32), LATE[n])
     for e in range(EXTRAS):
         turned = extra[:, ROWS * e : ROWS * e + ROWS].astype(jnp.bfloat16)
         acc_extra[e] = lax.dot_general(
             turned, slices[e], (((0,), (0,)), ((), ())), preferred_element_type=jnp.float32
         )
-    copies[11].wait()
+    copies[13].wait()
     for n in range(2):
-        copies[8 + 2 * n].wait()
+        copies[10 + 2 * n].wait()
         acc[...] += dot(wide(late.at[n]), blocks[n])
 
     upper = lax.broadcasted_iota(jnp.int32, (8, 128), 0) < 4
 
-    def decode(g, carry):
+    def decode(g):
         top = [jnp.zeros((8, 128), jnp.float32)] * 4
         low = [jnp.zeros((8, 128), jnp.float32)] * 4
         at = pl.multiple_of(24 * g, 8)
@@ -321,24 +341,31 @@
             low_r = tiles[2][:, :128] - pltpu.roll(tiles[2][:, 128:], 4, 0)
             low_i = tiles[2][:, 128:] + pltpu.roll(tiles[2][:, :128], 4, 0)
             for b in range(4):
-                w_r = weights[8 * s + b]
-                w_i = weights[8 * s + 4 + b]
+                w_r = weights[8 * s + b : 8 * s + b + 1, :]
+                w_i = weights[8 * s + 4 + b : 8 * s + 5 + b, :]
                 top[b] = top[b] + (w_r * top_r - w_i * top_i)
                 low[b] = low[b] + (w_r * low_r - w_i * low_i)
         low_a = jnp.where(upper, low[0], pltpu.roll(low[1], 4, 0))
         low_b = jnp.where(upper, low[2], pltpu.roll(low[3], 4, 0))
-        out[g] = jnp.concatenate(top + [low_a, low_b], axis=0)
+        return jnp.concatenate(top + [low_a, low_b], axis=0)
+
+    core = picks[3]
+
+    def both(z, carry):
+        kept[z] = decode(2 * z + core)
+        sent[z] = decode(2 * z + 1 - core)
         return carry
 
-    lax.fori_loop(0, PAIRS, decode, 0)
+    lax.fori_loop(0, PAIRS // 2, both, 0)
 
 
 def late_product(picks, weights, share, spread, before, early, late):
     return pl.pallas_call(
         late_kernel,
-        out_shape=jax.ShapeDtypeStruct((PAIRS, 48, 128), jnp.float32),
-        in_specs=[pl.BlockSpec(memory_space=pltpu.SMEM)] * 2 + [pl.BlockSpec(memory_space=pl.ANY)] * 11,
-        out_specs=pl.BlockSpec(memory_space=pltpu.VMEM),
+        out_shape=(jax.ShapeDtypeStruct((PAIRS // 2, 48, 128), jnp.float32),) * 2,
+        in_specs=[pl.BlockSpec(memory_space=pltpu.SMEM), pl.BlockSpec(memory_space=pltpu.VMEM)]
+        + [pl.BlockSpec(memory_space=pl.ANY)] * 13,
+        out_specs=(pl.BlockSpec(memory_space=pltpu.VMEM),) * 2,
         scratch_shapes=[
             pltpu.VMEM((ROWS, 256), jnp.float32),
             pltpu.VMEM((2, 512, 256), jnp.bfloat16),
@@ -348,22 +375,11 @@
             pltpu.VMEM((256, 1152), jnp.float32),
             pltpu.VMEM((EXTRAS, ROWS, 256), jnp.float32),
             pltpu.VMEM((512, 128), jnp.float32),
-            pltpu.SemaphoreType.DMA((12,)),
+            pltpu.SemaphoreType.DMA((14,)),
         ],
         name="late_product",
         interpret=INTERPRET,
-    )(picks, weights, share, spread, before, *early, *late)
-
-
-def choose(responding_nodes):
-    listed = jnp.any(
-        responding_nodes[:, None] == jnp.arange(NODE_NUMBER, dtype=jnp.int32)[None, :], axis=0
-    ).reshape(PAIRS, 2)
-    both = listed[:, 0] & listed[:, 1]
-    index = jnp.arange(PAIRS, dtype=jnp.int32)
-    before = jnp.sum((index[None, :] < index[:, None]) & both[None, :], axis=1)
-    extra_pair = both[None, :] & (before[None, :] == jnp.arange(EXTRAS, dtype=jnp.int32)[:, None])
-    return listed[:, 0], extra_pair
+    )(picks, weights, share, *spread, before, *early, *late)
 
 
 def summed(received):
@@ -373,37 +389,20 @@
     return jnp.concatenate([top, low], axis=2).transpose(0, 2, 1, 3)
 
 
-def decode_weights(nodes, group, second):
-    coefficient_actual, coefficient_image = recovery_coefficients(nodes)
-    _, extra_pair = choose(nodes)
-    extra_group = jnp.sum(
-        jnp.where(extra_pair, jnp.arange(PAIRS, dtype=jnp.int32)[None, :], 0), axis=1
-    ).astype(jnp.int32)
-    used = jnp.concatenate([(2 * group + second)[None], 2 * extra_group + 1])
-    point_selector = (used[:, None] == nodes[None, :])[:, :, None]
-    weights = jnp.concatenate(
-        [
-            jnp.sum(jnp.where(point_selector, coefficient_actual[None], 0.0), axis=1),
-            jnp.sum(jnp.where(point_selector, coefficient_image[None], 0.0), axis=1),
-        ],
-        axis=1,
-    ).reshape(-1)
-    return weights, extra_group
-
-
 def shards(source_matrix_tiles, second_operand_encoded, responding_nodes):
-    sent = encode(
-        responding_nodes, jnp.asarray(trig_table().reshape(-1)), source_matrix_tiles.reshape(96, 128)
+    group = ("z", "core")
+    place = jnp.stack([lax.axis_index(group), lax.axis_index("x"), lax.axis_index("parity")])
+    sent, picks = encode(
+        place.astype(jnp.int32),
+        responding_nodes,
+        jnp.asarray(trig_table().reshape(-1)),
+        source_matrix_tiles.reshape(96, 128),
     )
-    got = lax.all_to_all(sent, "group", split_axis=0, concat_axis=0, tiled=True)
+    got = lax.all_to_all(sent, group, split_axis=0, concat_axis=0, tiled=True)
 
     odd = second_operand_encoded[1].reshape(PANELS, PAIRS, 8, 2, 128).transpose(1, 0, 2, 3, 4)
     odd, got = lax.optimization_barrier((odd, got))
-    spread = lax.all_to_all(odd, "group", split_axis=0, concat_axis=0, tiled=True)
-    even_listed, _ = choose(responding_nodes)
-    group = lax.axis_index("group")
-    second = jnp.where(even_listed[group], 0, 1).astype(jnp.int32)
-    picks = jnp.stack([second, lax.axis_index("x"), lax.axis_index("parity")]).astype(jnp.int32)
+    spread = lax.all_to_all(odd, group, split_axis=0, concat_axis=0, tiled=True)
     a = lax.all_gather(compact(got), "quad")
 
     def hop(chunk, axis, size, by):
@@ -419,27 +418,29 @@
     far_a = hop(right_a, "x", XS, 1)
     far_b = hop(left_b, "x", XS, -1)
     share = split_share(picks, whole.reshape(2, 8192, 128))
-
-    weights, extra_group = decode_weights(nodes, group, second)
+    weights = decode_weights(nodes, picks)
     early = (a, b, right_a, left_a, right_b, left_b)
     before = early_product(picks, share, early)
-    three = jnp.stack(
-        [lax.dynamic_index_in_dim(spread, extra_group[e], 0, keepdims=False) for e in range(EXTRAS)]
-    ).reshape(EXTRAS, 512, 128)
-    partial = late_product(picks, weights, share, three, before, early, (far_a, far_b))
-    received = lax.all_to_all(partial, "group", split_axis=0, concat_axis=0, tiled=True)
+    three = [
+        lax.dynamic_index_in_dim(spread, picks[4 + e], 0, keepdims=False).reshape(512, 128)
+        for e in range(EXTRAS)
+    ]
+    kept, passed = late_product(picks, weights, share, three, before, early, (far_a, far_b))
+    kept = kept + lax.ppermute(passed, "core", [(0, 1), (1, 0)])
+    received = lax.all_to_all(kept, "z", split_axis=0, concat_axis=0, tiled=True)
     return summed(received)
 
 
 def solution(mesh):
     torus = Mesh(
-        mesh.devices.reshape(mesh.shape["group"], XS, QUADS, 2), ("group", "x", "quad", "parity")
+        mesh.devices.reshape(PAIRS // 2, 2, XS, QUADS, 2), ("z", "core", "x", "quad", "parity")
     )
+    group = ("z", "core")
     panel = ("x", "quad", "parity")
     return jax.shard_map(
         shards,
         mesh=torus,
-        in_specs=(P(None, "group", None, panel), P("group", None, None, panel), P()),
-        out_specs=P(None, "group", None, panel),
+        in_specs=(P(None, group, None, panel), P(group, None, None, panel), P()),
+        out_specs=P(None, group, None, panel),
         check_vma=False,
     )

time: 137 us -> 126 us (0.920)
  other arithmetic: 6.33 us -> 1.56 us
  blocking collectives: 36.2 us -> 31.6 us
  waiting for transfers between devices: 17.4 us -> 14 us
  starting transfers between devices: 43 us -> 45.2 us
  Pallas kernels: 16.9 us -> 18.5 us
    ppermute x0 -> x1, starting transfers between devices: none -> 7.51 us  [shards(): kept = kept + lax.ppermute(passed, 'core', [(0, 1), (1, 0)])]
    all_to_all x2, waiting for transfers between devices: 10.9 us -> 3.94 us  [the longest x1 3.93 us: shards(): got = lax.all_to_all(sent, group, split_axis=0, concat_axis=0, tiled=True)]
    all_to_all x2, starting transfers between devices: 21.8 us -> 15.4 us  [the longest x1 11.8 us: shards(): got = lax.all_to_all(sent, group, split_axis=0, concat_axis=0, tiled=True)]
    all_to_all x1, blocking collectives: 19.3 us -> 14 us  [shards(): lax.all_to_all(kept, 'z', split_axis=0, concat_axis=0, tiled=True)]
    ppermute x7, waiting for transfers between devices: 6.5 us -> 8.84 us  [hop(): lax.ppermute(chunk, axis, [(i, (i + by) % size) for i in range(size)])]
    another operation x2 -> x1, other arithmetic: 2.5 us -> 0.59 us  [shards(): jnp.stack([lax.axis_index(group), lax.axis_index('x'), lax.axis_index('pa...]
    pallas_call x2 -> x3, Pallas kernels: 6.64 us -> 8.28 us  [the longest x1 4.75 us: late_product(): pl.pallas_call(late_kernel, out_shape=(jax.ShapeDtypeStruct((PAIRS // 2,...]
  transfers between devices with their start and end apart: 9 -> 10, of which waited for: 2 -> 4; matrix products, arithmetic and copies ran while one was open for 9% -> 4% of each run, Pallas kernels for 6% -> 9%
where the time goes in v4:
time: 126 us; the launch traced here: 125 us
  starting transfers between devices  45.2 us (36%)
  blocking collectives  31.6 us (25%)
  Pallas kernels  18.5 us (15%)
  waiting for transfers between devices  14 us (11%)
  local copies, waits for them, and re-layouts  7.86 us (6%)
  between operations  6.05 us (5%)
  other arithmetic  1.56 us (1%)
    ppermute x7, starting transfers between devices, hop(): lax.ppermute(chunk, axis, [(i, (i + by) % size) for i in range(size)])  22.3 us
    all_gather x1, blocking collectives, shards(): a = lax.all_gather(compact(got), 'quad')  17.6 us
    all_to_all x1, blocking collectives, shards(): lax.all_to_all(kept, 'z', split_axis=0, concat_axis=0, tiled=True)  14 us
    all_to_all x1, starting transfers between devices, shards(): got = lax.all_to_all(sent, group, split_axis=0, concat_axis=0, tiled=True)  11.8 us
    ppermute x7, waiting for transfers between devices, hop(): lax.ppermute(chunk, axis, [(i, (i + by) % size) for i in range(size)])  8.84 us
    ppermute x1, starting transfers between devices, shards(): kept = kept + lax.ppermute(passed, 'core', [(0, 1), (1, 0)])  7.51 us
    pallas_call x1, Pallas kernels, late_product(): pl.pallas_call(late_kernel, out_shape=(jax.ShapeDtypeStruct((PAIRS // 2,...  4.75 us
    pallas_call x1, Pallas kernels, split_share(): pl.pallas_call(share_kernel, out_shape=jax.ShapeDtypeStruct((XS, 2, 512,...  4.66 us
  transfers between devices with their start and end apart: 10, of which 4 were waited for; matrix products, arithmetic and copies ran while one was open for 4% of the time, Pallas kernels for 9%

profile of v4, /device:TPU:1, one launch (start us, length us, event | category | flops | bytes accessed | tf_op | source)
XLA Modules:
  0.0 124.9 jit_solution(10190802733389359167)
XLA Ops:
  0.6 2.0 %encode.1 = (bf16[16,32,128]{2,1,0:T(8,128)(2,1)}, s32[16]{0:T(128)}) custom-call(s32[3]{0:T(128)} %pad_add_fusion.place, s32[19]{0:T(128)} %nodes.2, f32[512]{0:T(512)} %constant.38.clone.table, bf16[96,128]{1,0:T(8,128)(2,1)} %bitcast.33), custom_call_target="tpu_custom_call" | custom-call | tf_op jit(solution)/shard_map/encode/pallas_call | solution.py:155
  2.6 11.8 %all-to-all-start = ((bf16[16,32,128]{2,1,0:T(8,128)(2,1)}), bf16[16,32,128]{2,1,0:T(8,128)(2,1)S(1)}, u32[]{:S(2)}, u32[]{:S(2)}) async-start(bf16[16,32,128]{2,1,0:T(8,128)(2,1)} %get-tuple-element.15), calls=%async_computation | async-start | bytes 262144 | tf_op jit(solution)/shard_map/all_to_all | solution.py:401
  14.4 1.6 %slice-done = bf16[1,4096,2,128]{3,2,1,0:T(2,128)(2,1)S(1)} async-done(((bf16[2,4096,2,128]{3,2,1,0:T(2,128)(2,1)}), bf16[1,4096,2,128]{3,2,1,0:T(2,128)(2,1)S(1)}, s32[]{:S(2)}) %slice-start) | async-done | bytes 2097176 | tf_op jit(solution)/shard_map/slice | solution.py:403
  16.0 3.4 %copy.11 = bf16[32,16,8,2,128]{4,3,2,0,1:T(2,128)(2,1)} copy(bf16[32,16,8,2,128]{4,3,2,1,0:T(2,128)(2,1)S(1)} %bitcast.21) | data formatting | bytes 4194304 | tf_op jit(solution)/shard_map/reshape;squeeze | solution.py:403
  19.4 3.9 %all-to-all-done.got = bf16[16,32,128]{2,1,0:T(8,128)(2,1)S(1)} async-done(((bf16[16,32,128]{2,1,0:T(8,128)(2,1)}), bf16[16,32,128]{2,1,0:T(8,128)(2,1)S(1)}, u32[]{:S(2)}, u32[]{:S(2)}) %all-to-all-start) | async-done | bytes 131104 | tf_op jit(solution)/shard_map/all_to_all | solution.py:401
  24.0 3.6 %all-to-all-start.1 = ((bf16[16,32,8,2,128]{4,3,2,1,0:T(2,128)(2,1)}), bf16[16,32,8,2,128]{4,3,2,1,0:T(2,128)(2,1)S(1)}, u32[]{:S(2)}, u32[]{:S(2)}) async-start(bf16[16,32,8,2,128]{4,3,2,1,0:T(2,128)(2,1)} %bitcast.22), calls=%async_computation.1 | async-start | bytes 4194304 | tf_op jit(solution)/shard_map/all_to_all | solution.py:405
  27.6 1.6 %compact.1 = bf16[464,128]{1,0:T(8,128)(2,1)} custom-call(bf16[16,32,128]{2,1,0:T(8,128)(2,1)} %copy-done.3), custom_call_target="tpu_custom_call" | custom-call | tf_op jit(solution)/shard_map/compact/pallas_call | solution.py:197
  29.2 17.6 %all-gather = bf16[1856,128]{1,0:T(8,128)(2,1)S(1)} all-gather(bf16[464,128]{1,0:T(8,128)(2,1)} %compact.1), channel_id=2, replica_groups=mesh['z'=8,'core'=2,'x'=4,'quad'=4,'parity'=2] {'quad'}, dimensions={0}, use_global_device_ids=true | all-gather | bytes 593920 | tf_op jit(solution)/shard_map/all_gather | solution.py:406
  46.9 4.4 %collective-permute-start.2 = (bf16[4,464,128]{2,1,0:T(8,128)(2,1)S(1)}, bf16[4,464,128]{2,1,0:T(8,128)(2,1)S(1)}, u32[]{:S(2)}, u32[]{:S(2)}) collective-permute-start(bf16[4,464,128]{2,1,0:T(8,128)(2,1)S(1)} %bitcast.23), channel_id=1, source_target_pairs={{0,24},{8,0},{16,8},{24,16},{1,25},{9,1},{17,9},{25,17},{2,26},{10... | collective-permute-start | bytes 1425416 | tf_op jit(solution)/shard_map/ppermute | solution.py:409
  51.2 1.9 %collective-permute-start.1 = (bf16[4,464,128]{2,1,0:T(8,128)(2,1)S(1)}, bf16[4,464,128]{2,1,0:T(8,128)(2,1)S(1)}, u32[]{:S(2)}, u32[]{:S(2)}) collective-permute-start(bf16[4,464,128]{2,1,0:T(8,128)(2,1)S(1)} %bitcast.24), channel_id=1, source_target_pairs={{0,8},{8,16},{16,24},{24,0},{1,9},{9,17},{17,25},{25,1},{2,10},{10... | collective-permute-start | bytes 1425416 | tf_op jit(solution)/shard_map/ppermute | solution.py:409
  53.2 7.1 %collective-permute-done.2.c3 = bf16[4,464,128]{2,1,0:T(8,128)(2,1)S(1)} collective-permute-done((bf16[4,464,128]{2,1,0:T(8,128)(2,1)S(1)}, bf16[4,464,128]{2,1,0:T(8,128)(2,1)S(1)}, u32[]{:S(2)}, u32[]{:S(2)}) %collective-permute-start.2) | collective-permute-done | bytes 475168 | tf_op jit(solution)/shard_map/ppermute | solution.py:409
  60.3 1.9 %collective-permute-start.4 = (bf16[4,464,128]{2,1,0:T(8,128)(2,1)S(1)}, bf16[4,464,128]{2,1,0:T(8,128)(2,1)}, u32[]{:S(2)}, u32[]{:S(2)}) collective-permute-start(bf16[4,464,128]{2,1,0:T(8,128)(2,1)S(1)} %collective-permute-done.2.c3), channel_id=1, source_target_pairs={{0,7},{1,0},{2,1},{3,2},{4,3},{5,4},{6,5},{7,6},{8,15},{9,8},{10,9... | collective-permute-start | bytes 1425416 | tf_op jit(solution)/shard_map/ppermute | solution.py:409
  62.2 4.0 %collective-permute-start = (bf16[4,464,128]{2,1,0:T(8,128)(2,1)S(1)}, bf16[4,464,128]{2,1,0:T(8,128)(2,1)}, u32[]{:S(2)}, u32[]{:S(2)}) collective-permute-start(bf16[4,464,128]{2,1,0:T(8,128)(2,1)S(1)} %bitcast.25), channel_id=1, source_target_pairs={{0,7},{1,0},{2,1},{3,2},{4,3},{5,4},{6,5},{7,6},{8,15},{9,8},{10,9... | collective-permute-start | bytes 1425416 | tf_op jit(solution)/shard_map/ppermute | solution.py:409
  66.2 1.9 %collective-permute-start.3 = (bf16[4,464,128]{2,1,0:T(8,128)(2,1)S(1)}, bf16[4,464,128]{2,1,0:T(8,128)(2,1)}, u32[]{:S(2)}, u32[]{:S(2)}) collective-permute-start(bf16[4,464,128]{2,1,0:T(8,128)(2,1)S(1)} %collective-permute-done.1.c2), channel_id=1, source_target_pairs={{0,1},{1,2},{2,3},{3,4},{4,5},{5,6},{6,7},{7,0},{8,9},{9,10},{10,1... | collective-permute-start | bytes 1425416 | tf_op jit(solution)/shard_map/ppermute | solution.py:409
  68.2 2.8 %collective-permute-start.5 = (bf16[4,464,128]{2,1,0:T(8,128)(2,1)S(1)}, bf16[4,464,128]{2,1,0:T(8,128)(2,1)}, u32[]{:S(2)}, u32[]{:S(2)}) collective-permute-start(bf16[4,464,128]{2,1,0:T(8,128)(2,1)S(1)} %collective-permute-done.1.c2), channel_id=1, source_target_pairs={{0,8},{8,16},{16,24},{24,0},{1,9},{9,17},{17,25},{25,1},{2,10},{10... | collective-permute-start | bytes 1425416 | tf_op jit(solution)/shard_map/ppermute | solution.py:409
  71.0 1.7 %collective-permute-done.4.c5 = bf16[4,464,128]{2,1,0:T(8,128)(2,1)} collective-permute-done((bf16[4,464,128]{2,1,0:T(8,128)(2,1)S(1)}, bf16[4,464,128]{2,1,0:T(8,128)(2,1)}, u32[]{:S(2)}, u32[]{:S(2)}) %collective-permute-start.4) | collective-permute-done | bytes 475168 | tf_op jit(solution)/shard_map/ppermute | solution.py:409
  72.7 5.3 %collective-permute-start.6 = (bf16[4,464,128]{2,1,0:T(8,128)(2,1)}, bf16[4,464,128]{2,1,0:T(8,128)(2,1)}, u32[]{:S(2)}, u32[]{:S(2)}) collective-permute-start(bf16[4,464,128]{2,1,0:T(8,128)(2,1)} %collective-permute-done.4.c5), channel_id=1, source_target_pairs={{0,24},{8,0},{16,8},{24,16},{1,25},{9,1},{17,9},{25,17},{2,26},{10... | collective-permute-start | bytes 1425416 | tf_op jit(solution)/shard_map/ppermute | solution.py:409
  84.6 1.5 %weights.1 = f32[32,128]{1,0:T(8,128)} custom-call(s32[19]{0:T(128)} %nodes.2, s32[16]{0:T(128)} %get-tuple-element.14.picks, f32[64]{0:T(128)} %constant.39.clone.points, f32[16,128]{1,0:T(8,128)} %constant.40.clone.grid), custom_call_target="tpu_custom_call" | custom-call | tf_op jit(solution)/shard_map/weights/pallas_call | solution.py:90
  86.1 4.7 %split_share.1.share = bf16[4,2,512,256]{3,2,1,0:T(8,128)(2,1)} custom-call(s32[16]{0:T(128)} %get-tuple-element.14.picks, bf16[2,8192,128]{2,1,0:T(8,128)(2,1)} %bitcast.20), custom_call_target="tpu_custom_call" | custom-call | flops 400000000 | bytes 4200000 | tf_op jit(solution)/shard_map/split_share/pallas_call | solution.py:223
  90.8 4.0 %early_product.1.before = f32[384,256]{1,0:T(8,128)} custom-call(s32[16]{0:T(128)} %get-tuple-element.14.picks, bf16[4,2,512,256]{3,2,1,0:T(8,128)(2,1)} %split_share.1.share, bf16[4,464,128]{2,1,0:T(8,128)(2,1)} %bitcast.26, bf16[4,464,128]{2,1,0:T(8,128)(2,1)} %collective-permute-done.c1, bf16[4,464,128]{2,1,0:T(8,128)(2,1)} %copy-done.2, ...), custom_call_target="tpu_custom_call" | custom-call | flops 400000000 | bytes 4200000 | tf_op jit(solution)/shard_map/early_product/pallas_call | solution.py:268
  95.7 4.8 %late_product.1 = (f32[8,48,128]{2,1,0:T(8,128)}, f32[8,48,128]{2,1,0:T(8,128)}) custom-call(s32[16]{0:T(128)} %get-tuple-element.14.picks, f32[32,128]{1,0:T(8,128)} %weights.1, bf16[4,2,512,256]{3,2,1,0:T(8,128)(2,1)} %split_share.1.share, bf16[512,128]{1,0:T(8,128)(2,1)} %bitcast.30, bf16[512,128]{1,0:T(8,128)(2,1)} %bitcast.29, ...), custom_call_target="tpu_custom_call" | custom-call | tf_op jit(solution)/shard_map/late_product/pallas_call | solution.py:363
  100.5 7.5 %collective-permute-start.7 = (f32[8,48,128]{2,1,0:T(8,128)}, f32[8,48,128]{2,1,0:T(8,128)S(1)}, u32[]{:S(2)}, u32[]{:S(2)}) collective-permute-start(f32[8,48,128]{2,1,0:T(8,128)} %get-tuple-element.22), channel_id=1, source_target_pairs={{0,32},{32,0},{1,33},{33,1},{2,34},{34,2},{3,35},{35,3},{4,36},{36... | collective-permute-start | bytes 589832 | tf_op jit(solution)/shard_map/ppermute | solution.py:429
  108.0 1.3 %collective-permute-done.7 = f32[8,48,128]{2,1,0:T(8,128)S(1)} collective-permute-done((f32[8,48,128]{2,1,0:T(8,128)}, f32[8,48,128]{2,1,0:T(8,128)S(1)}, u32[]{:S(2)}, u32[]{:S(2)}) %collective-permute-start.7) | collective-permute-done | bytes 196640 | tf_op jit(solution)/shard_map/ppermute | solution.py:429
  110.2 14.0 %all_to_all.15 = f32[8,48,128]{2,1,0:T(8,128)S(1)} all-to-all(f32[8,48,128]{2,1,0:T(8,128)S(1)} %add.20), channel_id=1, replica_groups=mesh['z'=8,'core'=2,'x'=4,'quad'=4,'parity'=2] {'z'}, dimensions={0} | all-to-all | bytes 393216 | tf_op jit(solution)/shard_map/all_to_all | solution.py:430
  (26 shorter events, 4.5 us)
Async XLA Ops:
  2.6 20.7 %all-to-all-start = ((bf16[16,32,128]{2,1,0:T(8,128)(2,1)}), bf16[16,32,128]{2,1,0:T(8,128)(2,1)S(1)}, u32[]{:S(2)}, u32[]{:S(2)}) async-start(bf16[16,32,128]{2,1,0:T(8,128)(2,1)} %get-tuple-element.15), calls=%async_computation | async-start | bytes 262144 | tf_op jit(solution)/shard_map/all_to_all | solution.py:401
  14.4 1.6 %slice-start = ((bf16[2,4096,2,128]{3,2,1,0:T(2,128)(2,1)}), bf16[1,4096,2,128]{3,2,1,0:T(2,128)(2,1)S(1)}, s32[]{:S(2)}) async-start(bf16[2,4096,2,128]{3,2,1,0:T(2,128)(2,1)} %param.7), calls=%async_computation.3 | async-start | bytes 4194304 | tf_op jit(solution)/shard_map/slice | solution.py:403
  23.3 0.6 copy-start.3
  23.3 54.7 %copy-start.4 = (s32[16]{0:T(128)S(1)}, s32[16]{0:T(128)}, u32[]{:S(2)}) copy-start(s32[16]{0:T(128)} %get-tuple-element.14.picks) | copy-start | bytes 196
  24.0 70.8 %all-to-all-start.1 = ((bf16[16,32,8,2,128]{4,3,2,1,0:T(2,128)(2,1)}), bf16[16,32,8,2,128]{4,3,2,1,0:T(2,128)(2,1)S(1)}, u32[]{:S(2)}, u32[]{:S(2)}) async-start(bf16[16,32,8,2,128]{4,3,2,1,0:T(2,128)(2,1)} %bitcast.22), calls=%async_computation.1 | async-start | bytes 4194304 | tf_op jit(solution)/shard_map/all_to_all | solution.py:405
  46.9 43.9 %copy-start = (bf16[1856,128]{1,0:T(8,128)(2,1)}, bf16[1856,128]{1,0:T(8,128)(2,1)S(1)}, u32[]{:S(2)}) copy-start(bf16[1856,128]{1,0:T(8,128)(2,1)S(1)} %all-gather) | copy-start | bytes 1425412
  46.9 13.4 %collective-permute-start.2 = (bf16[4,464,128]{2,1,0:T(8,128)(2,1)S(1)}, bf16[4,464,128]{2,1,0:T(8,128)(2,1)S(1)}, u32[]{:S(2)}, u32[]{:S(2)}) collective-permute-start(bf16[4,464,128]{2,1,0:T(8,128)(2,1)S(1)} %bitcast.23), channel_id=1, source_target_pairs={{0,24},{8,0},{16,8},{24,16},{1,25},{9,1},{17,9},{25,17},{2,26},{10... | collective-permute-start | bytes 1425416 | tf_op jit(solution)/shard_map/ppermute | solution.py:409
  51.2 15.0 %collective-permute-start.1 = (bf16[4,464,128]{2,1,0:T(8,128)(2,1)S(1)}, bf16[4,464,128]{2,1,0:T(8,128)(2,1)S(1)}, u32[]{:S(2)}, u32[]{:S(2)}) collective-permute-start(bf16[4,464,128]{2,1,0:T(8,128)(2,1)S(1)} %bitcast.24), channel_id=1, source_target_pairs={{0,8},{8,16},{16,24},{24,0},{1,9},{9,17},{17,25},{25,1},{2,10},{10... | collective-permute-start | bytes 1425416 | tf_op jit(solution)/shard_map/ppermute | solution.py:409
  60.3 30.5 %copy-start.1 = (bf16[4,464,128]{2,1,0:T(8,128)(2,1)}, bf16[4,464,128]{2,1,0:T(8,128)(2,1)S(1)}, u32[]{:S(2)}) copy-start(bf16[4,464,128]{2,1,0:T(8,128)(2,1)S(1)} %collective-permute-done.2.c3) | copy-start | bytes 1425412
  60.3 12.4 %collective-permute-start.4 = (bf16[4,464,128]{2,1,0:T(8,128)(2,1)S(1)}, bf16[4,464,128]{2,1,0:T(8,128)(2,1)}, u32[]{:S(2)}, u32[]{:S(2)}) collective-permute-start(bf16[4,464,128]{2,1,0:T(8,128)(2,1)S(1)} %collective-permute-done.2.c3), channel_id=1, source_target_pairs={{0,7},{1,0},{2,1},{3,2},{4,3},{5,4},{6,5},{7,6},{8,15},{9,8},{10,9... | collective-permute-start | bytes 1425416 | tf_op jit(solution)/shard_map/ppermute | solution.py:409
  62.2 28.6 %collective-permute-start = (bf16[4,464,128]{2,1,0:T(8,128)(2,1)S(1)}, bf16[4,464,128]{2,1,0:T(8,128)(2,1)}, u32[]{:S(2)}, u32[]{:S(2)}) collective-permute-start(bf16[4,464,128]{2,1,0:T(8,128)(2,1)S(1)} %bitcast.25), channel_id=1, source_target_pairs={{0,7},{1,0},{2,1},{3,2},{4,3},{5,4},{6,5},{7,6},{8,15},{9,8},{10,9... | collective-permute-start | bytes 1425416 | tf_op jit(solution)/shard_map/ppermute | solution.py:409
  66.2 24.6 %copy-start.2 = (bf16[4,464,128]{2,1,0:T(8,128)(2,1)}, bf16[4,464,128]{2,1,0:T(8,128)(2,1)S(1)}, u32[]{:S(2)}) copy-start(bf16[4,464,128]{2,1,0:T(8,128)(2,1)S(1)} %collective-permute-done.1.c2) | copy-start | bytes 1425412
  66.2 24.6 %collective-permute-start.3 = (bf16[4,464,128]{2,1,0:T(8,128)(2,1)S(1)}, bf16[4,464,128]{2,1,0:T(8,128)(2,1)}, u32[]{:S(2)}, u32[]{:S(2)}) collective-permute-start(bf16[4,464,128]{2,1,0:T(8,128)(2,1)S(1)} %collective-permute-done.1.c2), channel_id=1, source_target_pairs={{0,1},{1,2},{2,3},{3,4},{4,5},{5,6},{6,7},{7,0},{8,9},{9,10},{10,1... | collective-permute-start | bytes 1425416 | tf_op jit(solution)/shard_map/ppermute | solution.py:409
  68.2 27.6 %collective-permute-start.5 = (bf16[4,464,128]{2,1,0:T(8,128)(2,1)S(1)}, bf16[4,464,128]{2,1,0:T(8,128)(2,1)}, u32[]{:S(2)}, u32[]{:S(2)}) collective-permute-start(bf16[4,464,128]{2,1,0:T(8,128)(2,1)S(1)} %collective-permute-done.1.c2), channel_id=1, source_target_pairs={{0,8},{8,16},{16,24},{24,0},{1,9},{9,17},{17,25},{25,1},{2,10},{10... | collective-permute-start | bytes 1425416 | tf_op jit(solution)/shard_map/ppermute | solution.py:409
  72.7 23.0 %collective-permute-start.6 = (bf16[4,464,128]{2,1,0:T(8,128)(2,1)}, bf16[4,464,128]{2,1,0:T(8,128)(2,1)}, u32[]{:S(2)}, u32[]{:S(2)}) collective-permute-start(bf16[4,464,128]{2,1,0:T(8,128)(2,1)} %collective-permute-done.4.c5), channel_id=1, source_target_pairs={{0,24},{8,0},{16,8},{24,16},{1,25},{9,1},{17,9},{25,17},{2,26},{10... | collective-permute-start | bytes 1425416 | tf_op jit(solution)/shard_map/ppermute | solution.py:409
  100.5 8.8 %collective-permute-start.7 = (f32[8,48,128]{2,1,0:T(8,128)}, f32[8,48,128]{2,1,0:T(8,128)S(1)}, u32[]{:S(2)}, u32[]{:S(2)}) collective-permute-start(f32[8,48,128]{2,1,0:T(8,128)} %get-tuple-element.22), channel_id=1, source_target_pairs={{0,32},{32,0},{1,33},{33,1},{2,34},{34,2},{3,35},{35,3},{4,36},{36... | collective-permute-start | bytes 589832 | tf_op jit(solution)/shard_map/ppermute | solution.py:429

commit v5 on v4

--- a/solution.py
+++ b/solution.py
@@ -97,7 +97,12 @@
     )(nodes, picks, jnp.asarray(points), jnp.asarray(grid))
 
 
-def encode_kernel(place, nodes, table, source, out, picks, flags, extra_points, rows, stack):
+def position():
+    group = 2 * lax.axis_index("z") + lax.axis_index("core")
+    return group, lax.axis_index("x"), lax.axis_index("parity")
+
+
+def encode_kernel(nodes, table, source, out, picks, flags, extra_points, rows, stack):
     for j in range(NODE_NUMBER):
         flags[j] = 0
     for s in range(nodes.shape[0]):
@@ -106,12 +111,13 @@
     for g in range(PAIRS):
         extra_points[found] = 2 * g + 1
         found = found + flags[2 * g] * flags[2 * g + 1]
-    second = 1 - flags[2 * place[0]]
+    group, x, parity = position()
+    second = 1 - flags[2 * group]
     picks[0] = second
-    picks[1] = place[1]
-    picks[2] = place[2]
-    picks[3] = place[0] % 2
-    picks[8] = 2 * place[0] + second
+    picks[1] = x
+    picks[2] = parity
+    picks[3] = group % 2
+    picks[8] = 2 * group + second
     for e in range(EXTRAS):
         picks[4 + e] = (extra_points[e] - 1) // 2
         picks[9 + e] = extra_points[e]
@@ -151,14 +157,14 @@
     lax.fori_loop(0, PAIRS, main, 0)
 
 
-def encode(place, nodes, table, source):
+def encode(nodes, table, source):
     return pl.pallas_call(
         encode_kernel,
         out_shape=(
             jax.ShapeDtypeStruct((PAIRS, 32, 128), jnp.bfloat16),
             jax.ShapeDtypeStruct((16,), jnp.int32),
         ),
-        in_specs=[pl.BlockSpec(memory_space=pltpu.SMEM)] * 3 + [pl.BlockSpec(memory_space=pltpu.VMEM)],
+        in_specs=[pl.BlockSpec(memory_space=pltpu.SMEM)] * 2 + [pl.BlockSpec(memory_space=pltpu.VMEM)],
         out_specs=(pl.BlockSpec(memory_space=pltpu.VMEM), pl.BlockSpec(memory_space=pltpu.SMEM)),
         scratch_shapes=[
             pltpu.SMEM((NODE_NUMBER,), jnp.int32),
@@ -168,7 +174,7 @@
         ],
         name="encode",
         interpret=INTERPRET,
-    )(place, nodes, table, source)
+    )(nodes, table, source)
 
 
 def compact_kernel(got, out, rows):
@@ -277,7 +283,7 @@
 
 
 def late_kernel(
-    picks, weights, share, s0, s1, s2, before, c0, c1, c2, c3, c4, c5, c6, c7, kept, sent,
+    picks, weights, share, spread, before, c0, c1, c2, c3, c4, c5, c6, c7, kept, sent,
     acc, blocks, small, ends, late, extra, acc_extra, scratch, sems,
 ):
     early = (c0, c1, c2, c3, c4, c5)
@@ -289,8 +295,8 @@
         copy.start()
         copies.append(copy)
 
-    for e, part in enumerate((s0, s1, s2)):
-        start(part, small.at[e])
+    for e in range(EXTRAS):
+        start(spread.at[picks[4 + e]], small.at[e])
     for n in range(6):
         start(early[n].at[:, pl.ds(ROWS, 80), :], ends.at[n])
     for n in range(2):
@@ -364,7 +370,7 @@
         late_kernel,
         out_shape=(jax.ShapeDtypeStruct((PAIRS // 2, 48, 128), jnp.float32),) * 2,
         in_specs=[pl.BlockSpec(memory_space=pltpu.SMEM), pl.BlockSpec(memory_space=pltpu.VMEM)]
-        + [pl.BlockSpec(memory_space=pl.ANY)] * 13,
+        + [pl.BlockSpec(memory_space=pl.ANY)] * 11,
         out_specs=(pl.BlockSpec(memory_space=pltpu.VMEM),) * 2,
         scratch_shapes=[
             pltpu.VMEM((ROWS, 256), jnp.float32),
@@ -379,7 +385,7 @@
         ],
         name="late_product",
         interpret=INTERPRET,
-    )(picks, weights, share, *spread, before, *early, *late)
+    )(picks, weights, share, spread, before, *early, *late)
 
 
 def summed(received):
@@ -391,9 +397,7 @@
 
 def shards(source_matrix_tiles, second_operand_encoded, responding_nodes):
     group = ("z", "core")
-    place = jnp.stack([lax.axis_index(group), lax.axis_index("x"), lax.axis_index("parity")])
     sent, picks = encode(
-        place.astype(jnp.int32),
         responding_nodes,
         jnp.asarray(trig_table().reshape(-1)),
         source_matrix_tiles.reshape(96, 128),
@@ -421,11 +425,9 @@
     weights = decode_weights(nodes, picks)
     early = (a, b, right_a, left_a, right_b, left_b)
     before = early_product(picks, share, early)
-    three = [
-        lax.dynamic_index_in_dim(spread, picks[4 + e], 0, keepdims=False).reshape(512, 128)
-        for e in range(EXTRAS)
-    ]
-    kept, passed = late_product(picks, weights, share, three, before, early, (far_a, far_b))
+    kept, passed = late_product(
+        picks, weights, share, spread.reshape(PAIRS, 512, 128), before, early, (far_a, far_b)
+    )
     kept = kept + lax.ppermute(passed, "core", [(0, 1), (1, 0)])
     received = lax.all_to_all(kept, "z", split_axis=0, concat_axis=0, tiled=True)
     return summed(received)

time: 126 us -> 119 us (0.944)
  between operations: 6.05 us -> 0.19 us
    unnamed x10, local copies, waits for them, and re-layouts: 0.66 us -> 2 us
  transfers between devices with their start and end apart: 10 -> 10, of which waited for: 4 -> 4; matrix products, arithmetic and copies ran while one was open for 4% -> 3% of each run, Pallas kernels for 9% -> 10%
where the time goes in v5:
time: 119 us; the launch traced here: 118 us
  starting transfers between devices  45.2 us (38%)
  blocking collectives  31.6 us (27%)
  Pallas kernels  18.5 us (16%)
  waiting for transfers between devices  14 us (12%)
  local copies, waits for them, and re-layouts  7.57 us (6%)
    ppermute x7, starting transfers between devices, hop(): lax.ppermute(chunk, axis, [(i, (i + by) % size) for i in range(size)])  22.3 us
    all_gather x1, blocking collectives, shards(): a = lax.all_gather(compact(got), 'quad')  17.6 us
    all_to_all x1, blocking collectives, shards(): lax.all_to_all(kept, 'z', split_axis=0, concat_axis=0, tiled=True)  14 us
    all_to_all x1, starting transfers between devices, shards(): got = lax.all_to_all(sent, group, split_axis=0, concat_axis=0, tiled=True)  11.8 us
    ppermute x7, waiting for transfers between devices, hop(): lax.ppermute(chunk, axis, [(i, (i + by) % size) for i in range(size)])  8.84 us
    ppermute x1, starting transfers between devices, shards(): kept = kept + lax.ppermute(passed, 'core', [(0, 1), (1, 0)])  7.51 us
    pallas_call x1, Pallas kernels, late_product(): pl.pallas_call(late_kernel, out_shape=(jax.ShapeDtypeStruct((PAIRS // 2,...  4.7 us
    pallas_call x1, Pallas kernels, split_share(): pl.pallas_call(share_kernel, out_shape=jax.ShapeDtypeStruct((XS, 2, 512,...  4.68 us
  transfers between devices with their start and end apart: 10, of which 4 were waited for; matrix products, arithmetic and copies ran while one was open for 3% of the time, Pallas kernels for 10%

profile of v5, /device:TPU:1, one launch (start us, length us, event | category | flops | bytes accessed | tf_op | source)
XLA Modules:
  0.0 118.1 jit_solution(18227855824756397680)
XLA Ops:
  0.0 2.0 %encode.1 = (bf16[16,32,128]{2,1,0:T(8,128)(2,1)}, s32[16]{0:T(128)}) custom-call(s32[19]{0:T(128)} %nodes.2, f32[512]{0:T(512)} %constant.8.clone.table, bf16[96,128]{1,0:T(8,128)(2,1)} %bitcast.23), custom_call_target="tpu_custom_call" | custom-call | tf_op jit(solution)/shard_map/encode/pallas_call | solution.py:161
  2.0 11.8 %all-to-all-start = ((bf16[16,32,128]{2,1,0:T(8,128)(2,1)}), bf16[16,32,128]{2,1,0:T(8,128)(2,1)S(1)}, u32[]{:S(2)}, u32[]{:S(2)}) async-start(bf16[16,32,128]{2,1,0:T(8,128)(2,1)} %get-tuple-element.15), calls=%async_computation | async-start | bytes 262144 | tf_op jit(solution)/shard_map/all_to_all | solution.py:405
  13.9 1.6 %slice-done = bf16[1,4096,2,128]{3,2,1,0:T(2,128)(2,1)S(1)} async-done(((bf16[2,4096,2,128]{3,2,1,0:T(2,128)(2,1)}), bf16[1,4096,2,128]{3,2,1,0:T(2,128)(2,1)S(1)}, s32[]{:S(2)}) %slice-start) | async-done | bytes 2097176 | tf_op jit(solution)/shard_map/slice | solution.py:407
  15.4 3.4 %copy.11 = bf16[32,16,8,2,128]{4,3,2,0,1:T(2,128)(2,1)} copy(bf16[32,16,8,2,128]{4,3,2,1,0:T(2,128)(2,1)S(1)} %bitcast.13) | data formatting | bytes 4194304 | tf_op jit(solution)/shard_map/reshape;squeeze | solution.py:407
  18.8 3.9 %all-to-all-done.got = bf16[16,32,128]{2,1,0:T(8,128)(2,1)S(1)} async-done(((bf16[16,32,128]{2,1,0:T(8,128)(2,1)}), bf16[16,32,128]{2,1,0:T(8,128)(2,1)S(1)}, u32[]{:S(2)}, u32[]{:S(2)}) %all-to-all-start) | async-done | bytes 131104 | tf_op jit(solution)/shard_map/all_to_all | solution.py:405
  23.4 3.6 %all-to-all-start.1 = ((bf16[16,32,8,2,128]{4,3,2,1,0:T(2,128)(2,1)}), bf16[16,32,8,2,128]{4,3,2,1,0:T(2,128)(2,1)S(1)}, u32[]{:S(2)}, u32[]{:S(2)}) async-start(bf16[16,32,8,2,128]{4,3,2,1,0:T(2,128)(2,1)} %bitcast.14), calls=%async_computation.1 | async-start | bytes 4194304 | tf_op jit(solution)/shard_map/all_to_all | solution.py:409
  27.0 1.7 %compact.1 = bf16[464,128]{1,0:T(8,128)(2,1)} custom-call(bf16[16,32,128]{2,1,0:T(8,128)(2,1)} %copy-done.4), custom_call_target="tpu_custom_call" | custom-call | tf_op jit(solution)/shard_map/compact/pallas_call | solution.py:203
  28.7 17.6 %all-gather = bf16[1856,128]{1,0:T(8,128)(2,1)S(1)} all-gather(bf16[464,128]{1,0:T(8,128)(2,1)} %compact.1), channel_id=2, replica_groups=mesh['z'=8,'core'=2,'x'=4,'quad'=4,'parity'=2] {'quad'}, dimensions={0}, use_global_device_ids=true | all-gather | bytes 593920 | tf_op jit(solution)/shard_map/all_gather | solution.py:410
  46.3 4.4 %collective-permute-start.2 = (bf16[4,464,128]{2,1,0:T(8,128)(2,1)S(1)}, bf16[4,464,128]{2,1,0:T(8,128)(2,1)S(1)}, u32[]{:S(2)}, u32[]{:S(2)}) collective-permute-start(bf16[4,464,128]{2,1,0:T(8,128)(2,1)S(1)} %bitcast.16), channel_id=1, source_target_pairs={{0,24},{8,0},{16,8},{24,16},{1,25},{9,1},{17,9},{25,17},{2,26},{10... | collective-permute-start | bytes 1425416 | tf_op jit(solution)/shard_map/ppermute | solution.py:413
  50.7 1.9 %collective-permute-start.1 = (bf16[4,464,128]{2,1,0:T(8,128)(2,1)S(1)}, bf16[4,464,128]{2,1,0:T(8,128)(2,1)S(1)}, u32[]{:S(2)}, u32[]{:S(2)}) collective-permute-start(bf16[4,464,128]{2,1,0:T(8,128)(2,1)S(1)} %bitcast.17), channel_id=1, source_target_pairs={{0,8},{8,16},{16,24},{24,0},{1,9},{9,17},{17,25},{25,1},{2,10},{10... | collective-permute-start | bytes 1425416 | tf_op jit(solution)/shard_map/ppermute | solution.py:413
  52.6 7.1 %collective-permute-done.2.c3 = bf16[4,464,128]{2,1,0:T(8,128)(2,1)S(1)} collective-permute-done((bf16[4,464,128]{2,1,0:T(8,128)(2,1)S(1)}, bf16[4,464,128]{2,1,0:T(8,128)(2,1)S(1)}, u32[]{:S(2)}, u32[]{:S(2)}) %collective-permute-start.2) | collective-permute-done | bytes 475168 | tf_op jit(solution)/shard_map/ppermute | solution.py:413
  59.8 1.9 %collective-permute-start.4 = (bf16[4,464,128]{2,1,0:T(8,128)(2,1)S(1)}, bf16[4,464,128]{2,1,0:T(8,128)(2,1)}, u32[]{:S(2)}, u32[]{:S(2)}) collective-permute-start(bf16[4,464,128]{2,1,0:T(8,128)(2,1)S(1)} %collective-permute-done.2.c3), channel_id=1, source_target_pairs={{0,7},{1,0},{2,1},{3,2},{4,3},{5,4},{6,5},{7,6},{8,15},{9,8},{10,9... | collective-permute-start | bytes 1425416 | tf_op jit(solution)/shard_map/ppermute | solution.py:413
  61.7 4.0 %collective-permute-start = (bf16[4,464,128]{2,1,0:T(8,128)(2,1)S(1)}, bf16[4,464,128]{2,1,0:T(8,128)(2,1)}, u32[]{:S(2)}, u32[]{:S(2)}) collective-permute-start(bf16[4,464,128]{2,1,0:T(8,128)(2,1)S(1)} %bitcast.18), channel_id=1, source_target_pairs={{0,7},{1,0},{2,1},{3,2},{4,3},{5,4},{6,5},{7,6},{8,15},{9,8},{10,9... | collective-permute-start | bytes 1425416 | tf_op jit(solution)/shard_map/ppermute | solution.py:413
  65.7 1.9 %collective-permute-start.3 = (bf16[4,464,128]{2,1,0:T(8,128)(2,1)S(1)}, bf16[4,464,128]{2,1,0:T(8,128)(2,1)}, u32[]{:S(2)}, u32[]{:S(2)}) collective-permute-start(bf16[4,464,128]{2,1,0:T(8,128)(2,1)S(1)} %collective-permute-done.1.c2), channel_id=1, source_target_pairs={{0,1},{1,2},{2,3},{3,4},{4,5},{5,6},{6,7},{7,0},{8,9},{9,10},{10,1... | collective-permute-start | bytes 1425416 | tf_op jit(solution)/shard_map/ppermute | solution.py:413
  67.6 2.8 %collective-permute-start.5 = (bf16[4,464,128]{2,1,0:T(8,128)(2,1)S(1)}, bf16[4,464,128]{2,1,0:T(8,128)(2,1)}, u32[]{:S(2)}, u32[]{:S(2)}) collective-permute-start(bf16[4,464,128]{2,1,0:T(8,128)(2,1)S(1)} %collective-permute-done.1.c2), channel_id=1, source_target_pairs={{0,8},{8,16},{16,24},{24,0},{1,9},{9,17},{17,25},{25,1},{2,10},{10... | collective-permute-start | bytes 1425416 | tf_op jit(solution)/shard_map/ppermute | solution.py:413
  70.5 1.7 %collective-permute-done.4.c5 = bf16[4,464,128]{2,1,0:T(8,128)(2,1)} collective-permute-done((bf16[4,464,128]{2,1,0:T(8,128)(2,1)S(1)}, bf16[4,464,128]{2,1,0:T(8,128)(2,1)}, u32[]{:S(2)}, u32[]{:S(2)}) %collective-permute-start.4) | collective-permute-done | bytes 475168 | tf_op jit(solution)/shard_map/ppermute | solution.py:413
  72.2 5.3 %collective-permute-start.6 = (bf16[4,464,128]{2,1,0:T(8,128)(2,1)}, bf16[4,464,128]{2,1,0:T(8,128)(2,1)}, u32[]{:S(2)}, u32[]{:S(2)}) collective-permute-start(bf16[4,464,128]{2,1,0:T(8,128)(2,1)} %collective-permute-done.4.c5), channel_id=1, source_target_pairs={{0,24},{8,0},{16,8},{24,16},{1,25},{9,1},{17,9},{25,17},{2,26},{10... | collective-permute-start | bytes 1425416 | tf_op jit(solution)/shard_map/ppermute | solution.py:413
  77.5 1.5 %weights.1 = f32[32,128]{1,0:T(8,128)} custom-call(s32[19]{0:T(128)} %nodes.2, s32[16]{0:T(128)} %get-tuple-element.14.picks, f32[64]{0:T(128)} %constant.9.clone.points, f32[16,128]{1,0:T(8,128)} %constant.10.clone.grid), custom_call_target="tpu_custom_call" | custom-call | tf_op jit(solution)/shard_map/weights/pallas_call | solution.py:90
  79.0 4.7 %split_share.1.share = bf16[4,2,512,256]{3,2,1,0:T(8,128)(2,1)} custom-call(s32[16]{0:T(128)} %get-tuple-element.14.picks, bf16[2,8192,128]{2,1,0:T(8,128)(2,1)} %bitcast.12), custom_call_target="tpu_custom_call" | custom-call | flops 400000000 | bytes 4200000 | tf_op jit(solution)/shard_map/split_share/pallas_call | solution.py:229
  83.7 4.0 %early_product.1.before = f32[384,256]{1,0:T(8,128)} custom-call(s32[16]{0:T(128)} %get-tuple-element.14.picks, bf16[4,2,512,256]{3,2,1,0:T(8,128)(2,1)} %split_share.1.share, bf16[4,464,128]{2,1,0:T(8,128)(2,1)} %bitcast.19, bf16[4,464,128]{2,1,0:T(8,128)(2,1)} %collective-permute-done.c1, bf16[4,464,128]{2,1,0:T(8,128)(2,1)} %copy-done.3, ...), custom_call_target="tpu_custom_call" | custom-call | flops 400000000 | bytes 4200000 | tf_op jit(solution)/shard_map/early_product/pallas_call | solution.py:274
  87.7 1.3 %copy-done = bf16[16,32,8,2,128]{4,3,2,1,0:T(2,128)(2,1)} copy-done((bf16[16,32,8,2,128]{4,3,2,1,0:T(2,128)(2,1)}, bf16[16,32,8,2,128]{4,3,2,1,0:T(2,128)(2,1)S(1)}, u32[]{:S(2)}) %copy-start) | copy-done | bytes 2097176
  89.0 4.7 %late_product.1 = (f32[8,48,128]{2,1,0:T(8,128)}, f32[8,48,128]{2,1,0:T(8,128)}) custom-call(s32[16]{0:T(128)} %get-tuple-element.14.picks, f32[32,128]{1,0:T(8,128)} %weights.1, bf16[4,2,512,256]{3,2,1,0:T(8,128)(2,1)} %split_share.1.share, bf16[16,512,128]{2,1,0:T(8,128)(2,1)} %bitcast.15, f32[384,256]{1,0:T(8,128)} %early_product.1.before, ...), custom_call_target="tpu_custom_call" | custom-call | tf_op jit(solution)/shard_map/late_product/pallas_call | solution.py:369
  93.8 7.5 %collective-permute-start.7 = (f32[8,48,128]{2,1,0:T(8,128)}, f32[8,48,128]{2,1,0:T(8,128)S(1)}, u32[]{:S(2)}, u32[]{:S(2)}) collective-permute-start(f32[8,48,128]{2,1,0:T(8,128)} %get-tuple-element.22), channel_id=1, source_target_pairs={{0,32},{32,0},{1,33},{33,1},{2,34},{34,2},{3,35},{35,3},{4,36},{36... | collective-permute-start | bytes 589832 | tf_op jit(solution)/shard_map/ppermute | solution.py:431
  103.5 14.0 %all_to_all.15 = f32[8,48,128]{2,1,0:T(8,128)S(1)} all-to-all(f32[8,48,128]{2,1,0:T(8,128)S(1)} %add.3), channel_id=1, replica_groups=mesh['z'=8,'core'=2,'x'=4,'quad'=4,'parity'=2] {'z'}, dimensions={0} | all-to-all | bytes 393216 | tf_op jit(solution)/shard_map/all_to_all | solution.py:432
  (23 shorter events, 3.5 us)
Async XLA Ops:
  2.0 20.7 %all-to-all-start = ((bf16[16,32,128]{2,1,0:T(8,128)(2,1)}), bf16[16,32,128]{2,1,0:T(8,128)(2,1)S(1)}, u32[]{:S(2)}, u32[]{:S(2)}) async-start(bf16[16,32,128]{2,1,0:T(8,128)(2,1)} %get-tuple-element.15), calls=%async_computation | async-start | bytes 262144 | tf_op jit(solution)/shard_map/all_to_all | solution.py:405
  13.8 1.6 %slice-start = ((bf16[2,4096,2,128]{3,2,1,0:T(2,128)(2,1)}), bf16[1,4096,2,128]{3,2,1,0:T(2,128)(2,1)S(1)}, s32[]{:S(2)}) async-start(bf16[2,4096,2,128]{3,2,1,0:T(2,128)(2,1)} %param.7), calls=%async_computation.3 | async-start | bytes 4194304 | tf_op jit(solution)/shard_map/slice | solution.py:407
  22.7 0.7 copy-start.4
  23.4 64.3 %all-to-all-start.1 = ((bf16[16,32,8,2,128]{4,3,2,1,0:T(2,128)(2,1)}), bf16[16,32,8,2,128]{4,3,2,1,0:T(2,128)(2,1)S(1)}, u32[]{:S(2)}, u32[]{:S(2)}) async-start(bf16[16,32,8,2,128]{4,3,2,1,0:T(2,128)(2,1)} %bitcast.14), calls=%async_computation.1 | async-start | bytes 4194304 | tf_op jit(solution)/shard_map/all_to_all | solution.py:409
  46.3 37.4 %copy-start.1 = (bf16[1856,128]{1,0:T(8,128)(2,1)}, bf16[1856,128]{1,0:T(8,128)(2,1)S(1)}, u32[]{:S(2)}) copy-start(bf16[1856,128]{1,0:T(8,128)(2,1)S(1)} %all-gather) | copy-start | bytes 1425412
  46.3 13.4 %collective-permute-start.2 = (bf16[4,464,128]{2,1,0:T(8,128)(2,1)S(1)}, bf16[4,464,128]{2,1,0:T(8,128)(2,1)S(1)}, u32[]{:S(2)}, u32[]{:S(2)}) collective-permute-start(bf16[4,464,128]{2,1,0:T(8,128)(2,1)S(1)} %bitcast.16), channel_id=1, source_target_pairs={{0,24},{8,0},{16,8},{24,16},{1,25},{9,1},{17,9},{25,17},{2,26},{10... | collective-permute-start | bytes 1425416 | tf_op jit(solution)/shard_map/ppermute | solution.py:413
  50.7 15.0 %collective-permute-start.1 = (bf16[4,464,128]{2,1,0:T(8,128)(2,1)S(1)}, bf16[4,464,128]{2,1,0:T(8,128)(2,1)S(1)}, u32[]{:S(2)}, u32[]{:S(2)}) collective-permute-start(bf16[4,464,128]{2,1,0:T(8,128)(2,1)S(1)} %bitcast.17), channel_id=1, source_target_pairs={{0,8},{8,16},{16,24},{24,0},{1,9},{9,17},{17,25},{25,1},{2,10},{10... | collective-permute-start | bytes 1425416 | tf_op jit(solution)/shard_map/ppermute | solution.py:413
  59.8 24.0 %copy-start.2 = (bf16[4,464,128]{2,1,0:T(8,128)(2,1)}, bf16[4,464,128]{2,1,0:T(8,128)(2,1)S(1)}, u32[]{:S(2)}) copy-start(bf16[4,464,128]{2,1,0:T(8,128)(2,1)S(1)} %collective-permute-done.2.c3) | copy-start | bytes 1425412
  59.8 12.4 %collective-permute-start.4 = (bf16[4,464,128]{2,1,0:T(8,128)(2,1)S(1)}, bf16[4,464,128]{2,1,0:T(8,128)(2,1)}, u32[]{:S(2)}, u32[]{:S(2)}) collective-permute-start(bf16[4,464,128]{2,1,0:T(8,128)(2,1)S(1)} %collective-permute-done.2.c3), channel_id=1, source_target_pairs={{0,7},{1,0},{2,1},{3,2},{4,3},{5,4},{6,5},{7,6},{8,15},{9,8},{10,9... | collective-permute-start | bytes 1425416 | tf_op jit(solution)/shard_map/ppermute | solution.py:413
  61.7 22.0 %collective-permute-start = (bf16[4,464,128]{2,1,0:T(8,128)(2,1)S(1)}, bf16[4,464,128]{2,1,0:T(8,128)(2,1)}, u32[]{:S(2)}, u32[]{:S(2)}) collective-permute-start(bf16[4,464,128]{2,1,0:T(8,128)(2,1)S(1)} %bitcast.18), channel_id=1, source_target_pairs={{0,7},{1,0},{2,1},{3,2},{4,3},{5,4},{6,5},{7,6},{8,15},{9,8},{10,9... | collective-permute-start | bytes 1425416 | tf_op jit(solution)/shard_map/ppermute | solution.py:413
  65.7 18.0 %copy-start.3 = (bf16[4,464,128]{2,1,0:T(8,128)(2,1)}, bf16[4,464,128]{2,1,0:T(8,128)(2,1)S(1)}, u32[]{:S(2)}) copy-start(bf16[4,464,128]{2,1,0:T(8,128)(2,1)S(1)} %collective-permute-done.1.c2) | copy-start | bytes 1425412
  65.7 18.0 %collective-permute-start.3 = (bf16[4,464,128]{2,1,0:T(8,128)(2,1)S(1)}, bf16[4,464,128]{2,1,0:T(8,128)(2,1)}, u32[]{:S(2)}, u32[]{:S(2)}) collective-permute-start(bf16[4,464,128]{2,1,0:T(8,128)(2,1)S(1)} %collective-permute-done.1.c2), channel_id=1, source_target_pairs={{0,1},{1,2},{2,3},{3,4},{4,5},{5,6},{6,7},{7,0},{8,9},{9,10},{10,1... | collective-permute-start | bytes 1425416 | tf_op jit(solution)/shard_map/ppermute | solution.py:413
  67.6 20.1 %collective-permute-start.5 = (bf16[4,464,128]{2,1,0:T(8,128)(2,1)S(1)}, bf16[4,464,128]{2,1,0:T(8,128)(2,1)}, u32[]{:S(2)}, u32[]{:S(2)}) collective-permute-start(bf16[4,464,128]{2,1,0:T(8,128)(2,1)S(1)} %collective-permute-done.1.c2), channel_id=1, source_target_pairs={{0,8},{8,16},{16,24},{24,0},{1,9},{9,17},{17,25},{25,1},{2,10},{10... | collective-permute-start | bytes 1425416 | tf_op jit(solution)/shard_map/ppermute | solution.py:413
  72.2 15.5 %collective-permute-start.6 = (bf16[4,464,128]{2,1,0:T(8,128)(2,1)}, bf16[4,464,128]{2,1,0:T(8,128)(2,1)}, u32[]{:S(2)}, u32[]{:S(2)}) collective-permute-start(bf16[4,464,128]{2,1,0:T(8,128)(2,1)} %collective-permute-done.4.c5), channel_id=1, source_target_pairs={{0,24},{8,0},{16,8},{24,16},{1,25},{9,1},{17,9},{25,17},{2,26},{10... | collective-permute-start | bytes 1425416 | tf_op jit(solution)/shard_map/ppermute | solution.py:413
  87.7 1.3 %copy-start = (bf16[16,32,8,2,128]{4,3,2,1,0:T(2,128)(2,1)}, bf16[16,32,8,2,128]{4,3,2,1,0:T(2,128)(2,1)S(1)}, u32[]{:S(2)}) copy-start(bf16[16,32,8,2,128]{4,3,2,1,0:T(2,128)(2,1)S(1)} %all-to-all-done.1) | copy-start | bytes 6291460
  93.8 8.8 %collective-permute-start.7 = (f32[8,48,128]{2,1,0:T(8,128)}, f32[8,48,128]{2,1,0:T(8,128)S(1)}, u32[]{:S(2)}, u32[]{:S(2)}) collective-permute-start(f32[8,48,128]{2,1,0:T(8,128)} %get-tuple-element.22), channel_id=1, source_target_pairs={{0,32},{32,0},{1,33},{33,1},{2,34},{34,2},{3,35},{35,3},{4,36},{36... | collective-permute-start | bytes 589832 | tf_op jit(solution)/shard_map/ppermute | solution.py:431

commit v6 on v5

--- a/solution.py
+++ b/solution.py
@@ -219,6 +219,33 @@
     return jnp.concatenate([real, imag], axis=1).astype(jnp.bfloat16)
 
 
+def slices_kernel(picks, spread, out, small, scratch, sems):
+    copies = [
+        pltpu.make_async_copy(spread.at[picks[4 + e]], small.at[e], sems.at[e]) for e in range(EXTRAS)
+    ]
+    for copy in copies:
+        copy.start()
+    for e in range(EXTRAS):
+        copies[e].wait()
+        out[e] = split_pairs(small[e], scratch)
+
+
+def split_slices(picks, spread):
+    return pl.pallas_call(
+        slices_kernel,
+        out_shape=jax.ShapeDtypeStruct((EXTRAS, 256, 256), jnp.bfloat16),
+        in_specs=[pl.BlockSpec(memory_space=pltpu.SMEM), pl.BlockSpec(memory_space=pl.ANY)],
+        out_specs=pl.BlockSpec(memory_space=pltpu.VMEM),
+        scratch_shapes=[
+            pltpu.VMEM((EXTRAS, 512, 128), jnp.bfloat16),
+            pltpu.VMEM((512, 128), jnp.float32),
+            pltpu.SemaphoreType.DMA((EXTRAS,)),
+        ],
+        name="split_slices",
+        interpret=INTERPRET,
+    )(picks, spread)
+
+
 def share_kernel(picks, share, out, scratch):
     for y in range(YS):
         piece = split_pairs(share[0, 256 * y : 256 * y + 256, :], scratch)
@@ -283,8 +310,8 @@
 
 
 def late_kernel(
-    picks, weights, share, spread, before, c0, c1, c2, c3, c4, c5, c6, c7, kept, sent,
-    acc, blocks, small, ends, late, extra, acc_extra, scratch, sems,
+    picks, weights, share, slices, before, c0, c1, c2, c3, c4, c5, c6, c7, kept, sent,
+    acc, blocks, small, ends, late, extra, acc_extra, sems,
 ):
     early = (c0, c1, c2, c3, c4, c5)
     chunks = (c6, c7)
@@ -295,8 +322,7 @@
         copy.start()
         copies.append(copy)
 
-    for e in range(EXTRAS):
-        start(spread.at[picks[4 + e]], small.at[e])
+    start(slices, small)
     for n in range(6):
         start(early[n].at[:, pl.ds(ROWS, 80), :], ends.at[n])
     for n in range(2):
@@ -313,22 +339,21 @@
             for v in range(9):
                 extra[pl.ds(at, 8), 128 * v : 128 * v + 128] = rows[8 * v : 8 * v + 8]
 
-    for copy in copies[:9]:
+    for copy in copies[:7]:
         copy.wait()
     for n in range(6):
         place(lambda q: ends[n, q].astype(jnp.float32), EARLY[n])
-    slices = [split_pairs(small[e], scratch) for e in range(EXTRAS)]
     for n in range(2):
-        copies[9 + 2 * n].wait()
+        copies[7 + 2 * n].wait()
         place(lambda q: late[n, q, ROWS:, :].astype(jnp.float32), LATE[n])
     for e in range(EXTRAS):
         turned = extra[:, ROWS * e : ROWS * e + ROWS].astype(jnp.bfloat16)
         acc_extra[e] = lax.dot_general(
-            turned, slices[e], (((0,), (0,)), ((), ())), preferred_element_type=jnp.float32
+            turned, small[e], (((0,), (0,)), ((), ())), preferred_element_type=jnp.float32
         )
-    copies[13].wait()
+    copies[11].wait()
     for n in range(2):
-        copies[10 + 2 * n].wait()
+        copies[8 + 2 * n].wait()
         acc[...] += dot(wide(late.at[n]), blocks[n])
 
     upper = lax.broadcasted_iota(jnp.int32, (8, 128), 0) < 4
@@ -365,7 +390,7 @@
     lax.fori_loop(0, PAIRS // 2, both, 0)
 
 
-def late_product(picks, weights, share, spread, before, early, late):
+def late_product(picks, weights, share, slices, before, early, late):
     return pl.pallas_call(
         late_kernel,
         out_shape=(jax.ShapeDtypeStruct((PAIRS // 2, 48, 128), jnp.float32),) * 2,
@@ -375,17 +400,16 @@
         scratch_shapes=[
             pltpu.VMEM((ROWS, 256), jnp.float32),
             pltpu.VMEM((2, 512, 256), jnp.bfloat16),
-            pltpu.VMEM((EXTRAS, 512, 128), jnp.bfloat16),
+            pltpu.VMEM((EXTRAS, 256, 256), jnp.bfloat16),
             pltpu.VMEM((6, QUADS, 80, 128), jnp.bfloat16),
             pltpu.VMEM((2, QUADS, CHUNK_ROWS, 128), jnp.bfloat16),
             pltpu.VMEM((256, 1152), jnp.float32),
             pltpu.VMEM((EXTRAS, ROWS, 256), jnp.float32),
-            pltpu.VMEM((512, 128), jnp.float32),
-            pltpu.SemaphoreType.DMA((14,)),
+            pltpu.SemaphoreType.DMA((12,)),
         ],
         name="late_product",
         interpret=INTERPRET,
-    )(picks, weights, share, spread, before, *early, *late)
+    )(picks, weights, share, slices, before, *early, *late)
 
 
 def summed(received):
@@ -416,7 +440,7 @@
     nodes, whole, a = lax.optimization_barrier((responding_nodes, second_operand_encoded, a))
     right_a = hop(a, "x", XS, 1)
     left_a = hop(a, "x", XS, -1)
-    b = hop(a, y_axes, YS, -1)
+    b = hop(a, y_axes, YS, 1)
     right_b = hop(right_a, y_axes, YS, 1)
     left_b = hop(left_a, y_axes, YS, -1)
     far_a = hop(right_a, "x", XS, 1)
@@ -425,8 +449,9 @@
     weights = decode_weights(nodes, picks)
     early = (a, b, right_a, left_a, right_b, left_b)
     before = early_product(picks, share, early)
+    slices = split_slices(picks, spread.reshape(PAIRS, 512, 128))
     kept, passed = late_product(
-        picks, weights, share, spread.reshape(PAIRS, 512, 128), before, early, (far_a, far_b)
+        picks, weights, share, slices, before, early, (far_a, far_b)
     )
     kept = kept + lax.ppermute(passed, "core", [(0, 1), (1, 0)])
     received = lax.all_to_all(kept, "z", split_axis=0, concat_axis=0, tiled=True)

time: 119 us -> 122 us (1.025)
  starting transfers between devices: 45.2 us -> 41.9 us
  Pallas kernels: 18.5 us -> 21 us
  waiting for transfers between devices: 14 us -> 16.4 us
    ppermute x1, starting transfers between devices: 7.51 us -> 4.77 us  [shards(): kept = kept + lax.ppermute(passed, 'core', [(0, 1), (1, 0)])]
    pallas_call x0 -> x1, Pallas kernels: none -> 2.52 us  [split_slices(): pl.pallas_call(slices_kernel, out_shape=jax.ShapeDtypeStruct((EXTRAS, 256...]
    ppermute x7, waiting for transfers between devices: 8.84 us -> 11.2 us  [hop(): lax.ppermute(chunk, axis, [(i, (i + by) % size) for i in range(size)])]
  transfers between devices with their start and end apart: 10 -> 10, of which waited for: 4 -> 5; matrix products, arithmetic and copies ran while one was open for 3% -> 3% of each run, Pallas kernels for 10% -> 12%
where the time goes in v6:
time: 122 us; the launch traced here: 120 us
  starting transfers between devices  41.9 us (34%)
  blocking collectives  32 us (26%)
  Pallas kernels  21 us (17%)
  waiting for transfers between devices  16.4 us (13%)
  local copies, waits for them, and re-layouts  7.56 us (6%)
    ppermute x7, starting transfers between devices, hop(): lax.ppermute(chunk, axis, [(i, (i + by) % size) for i in range(size)])  21.6 us
    all_gather x1, blocking collectives, shards(): a = lax.all_gather(compact(got), 'quad')  17.6 us
    all_to_all x1, blocking collectives, shards(): lax.all_to_all(kept, 'z', split_axis=0, concat_axis=0, tiled=True)  14.3 us
    all_to_all x1, starting transfers between devices, shards(): got = lax.all_to_all(sent, group, split_axis=0, concat_axis=0, tiled=True)  11.8 us
    ppermute x7, waiting for transfers between devices, hop(): lax.ppermute(chunk, axis, [(i, (i + by) % size) for i in range(size)])  11.2 us
    ppermute x1, starting transfers between devices, shards(): kept = kept + lax.ppermute(passed, 'core', [(0, 1), (1, 0)])  4.77 us
    pallas_call x1, Pallas kernels, split_share(): pl.pallas_call(share_kernel, out_shape=jax.ShapeDtypeStruct((XS, 2, 512,...  4.7 us
    pallas_call x1, Pallas kernels, late_product(): pl.pallas_call(late_kernel, out_shape=(jax.ShapeDtypeStruct((PAIRS // 2,...  4.58 us
  transfers between devices with their start and end apart: 10, of which 5 were waited for; matrix products, arithmetic and copies ran while one was open for 3% of the time, Pallas kernels for 12%

profile of v6, /device:TPU:1, one launch (start us, length us, event | category | flops | bytes accessed | tf_op | source)
XLA Modules:
  0.0 119.9 jit_solution(7618009704010345883)
XLA Ops:
  0.0 2.0 %encode.1 = (bf16[16,32,128]{2,1,0:T(8,128)(2,1)}, s32[16]{0:T(128)}) custom-call(s32[19]{0:T(128)} %nodes.2, f32[512]{0:T(512)} %constant.8.clone.table, bf16[96,128]{1,0:T(8,128)(2,1)} %bitcast.23), custom_call_target="tpu_custom_call" | custom-call | tf_op jit(solution)/shard_map/encode/pallas_call | solution.py:161
  2.0 11.8 %all-to-all-start = ((bf16[16,32,128]{2,1,0:T(8,128)(2,1)}), bf16[16,32,128]{2,1,0:T(8,128)(2,1)S(1)}, u32[]{:S(2)}, u32[]{:S(2)}) async-start(bf16[16,32,128]{2,1,0:T(8,128)(2,1)} %get-tuple-element.15), calls=%async_computation | async-start | bytes 262144 | tf_op jit(solution)/shard_map/all_to_all | solution.py:429
  13.9 1.6 %slice-done = bf16[1,4096,2,128]{3,2,1,0:T(2,128)(2,1)S(1)} async-done(((bf16[2,4096,2,128]{3,2,1,0:T(2,128)(2,1)}), bf16[1,4096,2,128]{3,2,1,0:T(2,128)(2,1)S(1)}, s32[]{:S(2)}) %slice-start) | async-done | bytes 2097176 | tf_op jit(solution)/shard_map/slice | solution.py:431
  15.5 3.3 %copy.11 = bf16[32,16,8,2,128]{4,3,2,0,1:T(2,128)(2,1)} copy(bf16[32,16,8,2,128]{4,3,2,1,0:T(2,128)(2,1)S(1)} %bitcast.13) | data formatting | bytes 4194304 | tf_op jit(solution)/shard_map/reshape;squeeze | solution.py:431
  18.8 4.0 %all-to-all-done.got = bf16[16,32,128]{2,1,0:T(8,128)(2,1)S(1)} async-done(((bf16[16,32,128]{2,1,0:T(8,128)(2,1)}), bf16[16,32,128]{2,1,0:T(8,128)(2,1)S(1)}, u32[]{:S(2)}, u32[]{:S(2)}) %all-to-all-start) | async-done | bytes 131104 | tf_op jit(solution)/shard_map/all_to_all | solution.py:429
  23.4 3.6 %all-to-all-start.1 = ((bf16[16,32,8,2,128]{4,3,2,1,0:T(2,128)(2,1)}), bf16[16,32,8,2,128]{4,3,2,1,0:T(2,128)(2,1)S(1)}, u32[]{:S(2)}, u32[]{:S(2)}) async-start(bf16[16,32,8,2,128]{4,3,2,1,0:T(2,128)(2,1)} %bitcast.14), calls=%async_computation.1 | async-start | bytes 4194304 | tf_op jit(solution)/shard_map/all_to_all | solution.py:433
  27.0 1.6 %compact.1 = bf16[464,128]{1,0:T(8,128)(2,1)} custom-call(bf16[16,32,128]{2,1,0:T(8,128)(2,1)} %copy-done.4), custom_call_target="tpu_custom_call" | custom-call | tf_op jit(solution)/shard_map/compact/pallas_call | solution.py:203
  28.7 17.6 %all-gather = bf16[1856,128]{1,0:T(8,128)(2,1)S(1)} all-gather(bf16[464,128]{1,0:T(8,128)(2,1)} %compact.1), channel_id=2, replica_groups=mesh['z'=8,'core'=2,'x'=4,'quad'=4,'parity'=2] {'quad'}, dimensions={0}, use_global_device_ids=true | all-gather | bytes 593920 | tf_op jit(solution)/shard_map/all_gather | solution.py:434
  46.3 4.4 %collective-permute-start.2 = (bf16[4,464,128]{2,1,0:T(8,128)(2,1)S(1)}, bf16[4,464,128]{2,1,0:T(8,128)(2,1)S(1)}, u32[]{:S(2)}, u32[]{:S(2)}) collective-permute-start(bf16[4,464,128]{2,1,0:T(8,128)(2,1)S(1)} %bitcast.16), channel_id=1, source_target_pairs={{0,24},{8,0},{16,8},{24,16},{1,25},{9,1},{17,9},{25,17},{2,26},{10... | collective-permute-start | bytes 1425416 | tf_op jit(solution)/shard_map/ppermute | solution.py:437
  50.7 1.9 %collective-permute-start.1 = (bf16[4,464,128]{2,1,0:T(8,128)(2,1)S(1)}, bf16[4,464,128]{2,1,0:T(8,128)(2,1)S(1)}, u32[]{:S(2)}, u32[]{:S(2)}) collective-permute-start(bf16[4,464,128]{2,1,0:T(8,128)(2,1)S(1)} %bitcast.17), channel_id=1, source_target_pairs={{0,8},{8,16},{16,24},{24,0},{1,9},{9,17},{17,25},{25,1},{2,10},{10... | collective-permute-start | bytes 1425416 | tf_op jit(solution)/shard_map/ppermute | solution.py:437
  52.7 7.1 %collective-permute-done.2.c3 = bf16[4,464,128]{2,1,0:T(8,128)(2,1)S(1)} collective-permute-done((bf16[4,464,128]{2,1,0:T(8,128)(2,1)S(1)}, bf16[4,464,128]{2,1,0:T(8,128)(2,1)S(1)}, u32[]{:S(2)}, u32[]{:S(2)}) %collective-permute-start.2) | collective-permute-done | bytes 475168 | tf_op jit(solution)/shard_map/ppermute | solution.py:437
  59.8 1.9 %collective-permute-start.4 = (bf16[4,464,128]{2,1,0:T(8,128)(2,1)S(1)}, bf16[4,464,128]{2,1,0:T(8,128)(2,1)}, u32[]{:S(2)}, u32[]{:S(2)}) collective-permute-start(bf16[4,464,128]{2,1,0:T(8,128)(2,1)S(1)} %collective-permute-done.2.c3), channel_id=1, source_target_pairs={{0,7},{1,0},{2,1},{3,2},{4,3},{5,4},{6,5},{7,6},{8,15},{9,8},{10,9... | collective-permute-start | bytes 1425416 | tf_op jit(solution)/shard_map/ppermute | solution.py:437
  61.7 3.4 %collective-permute-start = (bf16[4,464,128]{2,1,0:T(8,128)(2,1)S(1)}, bf16[4,464,128]{2,1,0:T(8,128)(2,1)}, u32[]{:S(2)}, u32[]{:S(2)}) collective-permute-start(bf16[4,464,128]{2,1,0:T(8,128)(2,1)S(1)} %bitcast.18), channel_id=1, source_target_pairs={{0,1},{1,2},{2,3},{3,4},{4,5},{5,6},{6,7},{7,0},{8,9},{9,10},{10,1... | collective-permute-start | bytes 1425416 | tf_op jit(solution)/shard_map/ppermute | solution.py:437
  65.1 1.9 %collective-permute-start.3 = (bf16[4,464,128]{2,1,0:T(8,128)(2,1)S(1)}, bf16[4,464,128]{2,1,0:T(8,128)(2,1)}, u32[]{:S(2)}, u32[]{:S(2)}) collective-permute-start(bf16[4,464,128]{2,1,0:T(8,128)(2,1)S(1)} %collective-permute-done.1.c2), channel_id=1, source_target_pairs={{0,1},{1,2},{2,3},{3,4},{4,5},{5,6},{6,7},{7,0},{8,9},{9,10},{10,1... | collective-permute-start | bytes 1425416 | tf_op jit(solution)/shard_map/ppermute | solution.py:437
  67.0 2.8 %collective-permute-start.5 = (bf16[4,464,128]{2,1,0:T(8,128)(2,1)S(1)}, bf16[4,464,128]{2,1,0:T(8,128)(2,1)}, u32[]{:S(2)}, u32[]{:S(2)}) collective-permute-start(bf16[4,464,128]{2,1,0:T(8,128)(2,1)S(1)} %collective-permute-done.1.c2), channel_id=1, source_target_pairs={{0,8},{8,16},{16,24},{24,0},{1,9},{9,17},{17,25},{25,1},{2,10},{10... | collective-permute-start | bytes 1425416 | tf_op jit(solution)/shard_map/ppermute | solution.py:437
  69.9 2.3 %collective-permute-done.4.c5 = bf16[4,464,128]{2,1,0:T(8,128)(2,1)} collective-permute-done((bf16[4,464,128]{2,1,0:T(8,128)(2,1)S(1)}, bf16[4,464,128]{2,1,0:T(8,128)(2,1)}, u32[]{:S(2)}, u32[]{:S(2)}) %collective-permute-start.4) | collective-permute-done | bytes 475168 | tf_op jit(solution)/shard_map/ppermute | solution.py:437
  72.2 5.3 %collective-permute-start.6 = (bf16[4,464,128]{2,1,0:T(8,128)(2,1)}, bf16[4,464,128]{2,1,0:T(8,128)(2,1)}, u32[]{:S(2)}, u32[]{:S(2)}) collective-permute-start(bf16[4,464,128]{2,1,0:T(8,128)(2,1)} %collective-permute-done.4.c5), channel_id=1, source_target_pairs={{0,24},{8,0},{16,8},{24,16},{1,25},{9,1},{17,9},{25,17},{2,26},{10... | collective-permute-start | bytes 1425416 | tf_op jit(solution)/shard_map/ppermute | solution.py:437
  79.0 4.7 %split_share.1.share = bf16[4,2,512,256]{3,2,1,0:T(8,128)(2,1)} custom-call(s32[16]{0:T(128)} %get-tuple-element.14.picks, bf16[2,8192,128]{2,1,0:T(8,128)(2,1)} %bitcast.12), custom_call_target="tpu_custom_call" | custom-call | flops 400000000 | bytes 4200000 | tf_op jit(solution)/shard_map/split_share/pallas_call | solution.py:256
  83.8 1.7 %collective-permute-done.3.c4 = bf16[4,464,128]{2,1,0:T(8,128)(2,1)} collective-permute-done((bf16[4,464,128]{2,1,0:T(8,128)(2,1)S(1)}, bf16[4,464,128]{2,1,0:T(8,128)(2,1)}, u32[]{:S(2)}, u32[]{:S(2)}) %collective-permute-start.3) | collective-permute-done | bytes 475168 | tf_op jit(solution)/shard_map/ppermute | solution.py:437
  85.5 4.0 %early_product.1.before = f32[384,256]{1,0:T(8,128)} custom-call(s32[16]{0:T(128)} %get-tuple-element.14.picks, bf16[4,2,512,256]{3,2,1,0:T(8,128)(2,1)} %split_share.1.share, bf16[4,464,128]{2,1,0:T(8,128)(2,1)} %bitcast.19, bf16[4,464,128]{2,1,0:T(8,128)(2,1)} %collective-permute-done.c1, bf16[4,464,128]{2,1,0:T(8,128)(2,1)} %copy-done.3, ...), custom_call_target="tpu_custom_call" | custom-call | flops 400000000 | bytes 4200000 | tf_op jit(solution)/shard_map/early_product/pallas_call | solution.py:301
  90.8 2.5 %split_slices.1.slices = bf16[3,256,256]{2,1,0:T(8,128)(2,1)} custom-call(s32[16]{0:T(128)} %get-tuple-element.14.picks, bf16[16,512,128]{2,1,0:T(8,128)(2,1)} %bitcast.15), custom_call_target="tpu_custom_call" | custom-call | tf_op jit(solution)/shard_map/split_slices/pallas_call | solution.py:234
  93.3 4.6 %late_product.1 = (f32[8,48,128]{2,1,0:T(8,128)}, f32[8,48,128]{2,1,0:T(8,128)}) custom-call(s32[16]{0:T(128)} %get-tuple-element.14.picks, f32[32,128]{1,0:T(8,128)} %weights.1, bf16[4,2,512,256]{3,2,1,0:T(8,128)(2,1)} %split_share.1.share, bf16[3,256,256]{2,1,0:T(8,128)(2,1)} %split_slices.1.slices, f32[384,256]{1,0:T(8,128)} %early_product.1.before, ...), custom_call_target="tpu_custom_call" | custom-call | tf_op jit(solution)/shard_map/late_product/pallas_call | solution.py:394
  97.9 4.8 %collective-permute-start.7 = (f32[8,48,128]{2,1,0:T(8,128)}, f32[8,48,128]{2,1,0:T(8,128)S(1)}, u32[]{:S(2)}, u32[]{:S(2)}) collective-permute-start(f32[8,48,128]{2,1,0:T(8,128)} %get-tuple-element.22), channel_id=1, source_target_pairs={{0,32},{32,0},{1,33},{33,1},{2,34},{34,2},{3,35},{35,3},{4,36},{36... | collective-permute-start | bytes 589832 | tf_op jit(solution)/shard_map/ppermute | solution.py:456
  104.9 14.3 %all_to_all.15 = f32[8,48,128]{2,1,0:T(8,128)S(1)} all-to-all(f32[8,48,128]{2,1,0:T(8,128)S(1)} %add.3), channel_id=1, replica_groups=mesh['z'=8,'core'=2,'x'=4,'quad'=4,'parity'=2] {'z'}, dimensions={0} | all-to-all | bytes 393216 | tf_op jit(solution)/shard_map/all_to_all | solution.py:457
  (24 shorter events, 6.4 us)
Async XLA Ops:
  2.0 20.7 %all-to-all-start = ((bf16[16,32,128]{2,1,0:T(8,128)(2,1)}), bf16[16,32,128]{2,1,0:T(8,128)(2,1)S(1)}, u32[]{:S(2)}, u32[]{:S(2)}) async-start(bf16[16,32,128]{2,1,0:T(8,128)(2,1)} %get-tuple-element.15), calls=%async_computation | async-start | bytes 262144 | tf_op jit(solution)/shard_map/all_to_all | solution.py:429
  13.9 1.6 %slice-start = ((bf16[2,4096,2,128]{3,2,1,0:T(2,128)(2,1)}), bf16[1,4096,2,128]{3,2,1,0:T(2,128)(2,1)S(1)}, s32[]{:S(2)}) async-start(bf16[2,4096,2,128]{3,2,1,0:T(2,128)(2,1)} %param.7), calls=%async_computation.3 | async-start | bytes 4194304 | tf_op jit(solution)/shard_map/slice | solution.py:431
  22.8 0.7 copy-start.4
  23.4 66.0 %all-to-all-start.1 = ((bf16[16,32,8,2,128]{4,3,2,1,0:T(2,128)(2,1)}), bf16[16,32,8,2,128]{4,3,2,1,0:T(2,128)(2,1)S(1)}, u32[]{:S(2)}, u32[]{:S(2)}) async-start(bf16[16,32,8,2,128]{4,3,2,1,0:T(2,128)(2,1)} %bitcast.14), calls=%async_computation.1 | async-start | bytes 4194304 | tf_op jit(solution)/shard_map/all_to_all | solution.py:433
  46.3 37.4 %copy-start.1 = (bf16[1856,128]{1,0:T(8,128)(2,1)}, bf16[1856,128]{1,0:T(8,128)(2,1)S(1)}, u32[]{:S(2)}) copy-start(bf16[1856,128]{1,0:T(8,128)(2,1)S(1)} %all-gather) | copy-start | bytes 1425412
  46.3 13.4 %collective-permute-start.2 = (bf16[4,464,128]{2,1,0:T(8,128)(2,1)S(1)}, bf16[4,464,128]{2,1,0:T(8,128)(2,1)S(1)}, u32[]{:S(2)}, u32[]{:S(2)}) collective-permute-start(bf16[4,464,128]{2,1,0:T(8,128)(2,1)S(1)} %bitcast.16), channel_id=1, source_target_pairs={{0,24},{8,0},{16,8},{24,16},{1,25},{9,1},{17,9},{25,17},{2,26},{10... | collective-permute-start | bytes 1425416 | tf_op jit(solution)/shard_map/ppermute | solution.py:437
  50.7 14.3 %collective-permute-start.1 = (bf16[4,464,128]{2,1,0:T(8,128)(2,1)S(1)}, bf16[4,464,128]{2,1,0:T(8,128)(2,1)S(1)}, u32[]{:S(2)}, u32[]{:S(2)}) collective-permute-start(bf16[4,464,128]{2,1,0:T(8,128)(2,1)S(1)} %bitcast.17), channel_id=1, source_target_pairs={{0,8},{8,16},{16,24},{24,0},{1,9},{9,17},{17,25},{25,1},{2,10},{10... | collective-permute-start | bytes 1425416 | tf_op jit(solution)/shard_map/ppermute | solution.py:437
  59.8 24.0 %copy-start.2 = (bf16[4,464,128]{2,1,0:T(8,128)(2,1)}, bf16[4,464,128]{2,1,0:T(8,128)(2,1)S(1)}, u32[]{:S(2)}) copy-start(bf16[4,464,128]{2,1,0:T(8,128)(2,1)S(1)} %collective-permute-done.2.c3) | copy-start | bytes 1425412
  59.8 12.4 %collective-permute-start.4 = (bf16[4,464,128]{2,1,0:T(8,128)(2,1)S(1)}, bf16[4,464,128]{2,1,0:T(8,128)(2,1)}, u32[]{:S(2)}, u32[]{:S(2)}) collective-permute-start(bf16[4,464,128]{2,1,0:T(8,128)(2,1)S(1)} %collective-permute-done.2.c3), channel_id=1, source_target_pairs={{0,7},{1,0},{2,1},{3,2},{4,3},{5,4},{6,5},{7,6},{8,15},{9,8},{10,9... | collective-permute-start | bytes 1425416 | tf_op jit(solution)/shard_map/ppermute | solution.py:437
  61.7 22.1 %collective-permute-start = (bf16[4,464,128]{2,1,0:T(8,128)(2,1)S(1)}, bf16[4,464,128]{2,1,0:T(8,128)(2,1)}, u32[]{:S(2)}, u32[]{:S(2)}) collective-permute-start(bf16[4,464,128]{2,1,0:T(8,128)(2,1)S(1)} %bitcast.18), channel_id=1, source_target_pairs={{0,1},{1,2},{2,3},{3,4},{4,5},{5,6},{6,7},{7,0},{8,9},{9,10},{10,1... | collective-permute-start | bytes 1425416 | tf_op jit(solution)/shard_map/ppermute | solution.py:437
  65.1 18.7 %copy-start.3 = (bf16[4,464,128]{2,1,0:T(8,128)(2,1)}, bf16[4,464,128]{2,1,0:T(8,128)(2,1)S(1)}, u32[]{:S(2)}) copy-start(bf16[4,464,128]{2,1,0:T(8,128)(2,1)S(1)} %collective-permute-done.1.c2) | copy-start | bytes 1425412
  65.1 20.4 %collective-permute-start.3 = (bf16[4,464,128]{2,1,0:T(8,128)(2,1)S(1)}, bf16[4,464,128]{2,1,0:T(8,128)(2,1)}, u32[]{:S(2)}, u32[]{:S(2)}) collective-permute-start(bf16[4,464,128]{2,1,0:T(8,128)(2,1)S(1)} %collective-permute-done.1.c2), channel_id=1, source_target_pairs={{0,1},{1,2},{2,3},{3,4},{4,5},{5,6},{6,7},{7,0},{8,9},{9,10},{10,1... | collective-permute-start | bytes 1425416 | tf_op jit(solution)/shard_map/ppermute | solution.py:437
  67.0 26.3 %collective-permute-start.5 = (bf16[4,464,128]{2,1,0:T(8,128)(2,1)S(1)}, bf16[4,464,128]{2,1,0:T(8,128)(2,1)}, u32[]{:S(2)}, u32[]{:S(2)}) collective-permute-start(bf16[4,464,128]{2,1,0:T(8,128)(2,1)S(1)} %collective-permute-done.1.c2), channel_id=1, source_target_pairs={{0,8},{8,16},{16,24},{24,0},{1,9},{9,17},{17,25},{25,1},{2,10},{10... | collective-permute-start | bytes 1425416 | tf_op jit(solution)/shard_map/ppermute | solution.py:437
  72.2 21.1 %collective-permute-start.6 = (bf16[4,464,128]{2,1,0:T(8,128)(2,1)}, bf16[4,464,128]{2,1,0:T(8,128)(2,1)}, u32[]{:S(2)}, u32[]{:S(2)}) collective-permute-start(bf16[4,464,128]{2,1,0:T(8,128)(2,1)} %collective-permute-done.4.c5), channel_id=1, source_target_pairs={{0,24},{8,0},{16,8},{24,16},{1,25},{9,1},{17,9},{25,17},{2,26},{10... | collective-permute-start | bytes 1425416 | tf_op jit(solution)/shard_map/ppermute | solution.py:437
  89.5 1.3 %copy-start = (bf16[16,32,8,2,128]{4,3,2,1,0:T(2,128)(2,1)}, bf16[16,32,8,2,128]{4,3,2,1,0:T(2,128)(2,1)S(1)}, u32[]{:S(2)}) copy-start(bf16[16,32,8,2,128]{4,3,2,1,0:T(2,128)(2,1)S(1)} %all-to-all-done.1) | copy-start | bytes 6291460
  97.9 6.0 %collective-permute-start.7 = (f32[8,48,128]{2,1,0:T(8,128)}, f32[8,48,128]{2,1,0:T(8,128)S(1)}, u32[]{:S(2)}, u32[]{:S(2)}) collective-permute-start(f32[8,48,128]{2,1,0:T(8,128)} %get-tuple-element.22), channel_id=1, source_target_pairs={{0,32},{32,0},{1,33},{33,1},{2,34},{34,2},{3,35},{35,3},{4,36},{36... | collective-permute-start | bytes 589832 | tf_op jit(solution)/shard_map/ppermute | solution.py:456

commit v7 on v5

--- a/solution.py
+++ b/solution.py
@@ -260,7 +260,7 @@
     return x, picks[2] if same else 1 - picks[2]
 
 
-def early_kernel(picks, share, c0, c1, c2, c3, c4, c5, acc):
+def early_kernel(picks, share, c0, c1, c2, c3, c4, c5, spread, acc):
     for n, (chunk, kind) in enumerate(zip((c0, c1, c2, c3, c4, c5), EARLY)):
         x, parity = block_of(picks, kind)
         term = dot(wide(chunk), share[x, parity])
@@ -270,16 +270,17 @@
             acc[...] += term
 
 
-def early_product(picks, share, chunks):
+def early_product(picks, share, chunks, spread):
     return pl.pallas_call(
         early_kernel,
         out_shape=jax.ShapeDtypeStruct((ROWS, 256), jnp.float32),
-        in_specs=[pl.BlockSpec(memory_space=pltpu.SMEM)] + [pl.BlockSpec(memory_space=pltpu.VMEM)] * 7,
+        in_specs=[pl.BlockSpec(memory_space=pltpu.SMEM)] + [pl.BlockSpec(memory_space=pltpu.VMEM)] * 7
+        + [pl.BlockSpec(memory_space=pl.ANY)],
         out_specs=pl.BlockSpec(memory_space=pltpu.VMEM),
         name="early_product",
         cost_estimate=pl.CostEstimate(flops=400_000_000, bytes_accessed=4_200_000, transcendentals=0),
         interpret=INTERPRET,
-    )(picks, share, *chunks)
+    )(picks, share, *chunks, spread)
 
 
 def late_kernel(
@@ -404,6 +405,8 @@
     )
     got = lax.all_to_all(sent, group, split_axis=0, concat_axis=0, tiled=True)
 
+    share = split_share(picks, second_operand_encoded.reshape(2, 8192, 128))
+
     odd = second_operand_encoded[1].reshape(PANELS, PAIRS, 8, 2, 128).transpose(1, 0, 2, 3, 4)
     odd, got = lax.optimization_barrier((odd, got))
     spread = lax.all_to_all(odd, group, split_axis=0, concat_axis=0, tiled=True)
@@ -413,7 +416,7 @@
         return lax.ppermute(chunk, axis, [(i, (i + by) % size) for i in range(size)])
 
     y_axes = ("quad", "parity")
-    nodes, whole, a = lax.optimization_barrier((responding_nodes, second_operand_encoded, a))
+    nodes, a = lax.optimization_barrier((responding_nodes, a))
     right_a = hop(a, "x", XS, 1)
     left_a = hop(a, "x", XS, -1)
     b = hop(a, y_axes, YS, -1)
@@ -421,12 +424,12 @@
     left_b = hop(left_a, y_axes, YS, -1)
     far_a = hop(right_a, "x", XS, 1)
     far_b = hop(left_b, "x", XS, -1)
-    share = split_share(picks, whole.reshape(2, 8192, 128))
     weights = decode_weights(nodes, picks)
     early = (a, b, right_a, left_a, right_b, left_b)
-    before = early_product(picks, share, early)
+    spread = spread.reshape(PAIRS, 512, 128)
+    before = early_product(picks, share, early, spread)
     kept, passed = late_product(
-        picks, weights, share, spread.reshape(PAIRS, 512, 128), before, early, (far_a, far_b)
+        picks, weights, share, spread, before, early, (far_a, far_b)
     )
     kept = kept + lax.ppermute(passed, "core", [(0, 1), (1, 0)])
     received = lax.all_to_all(kept, "z", split_axis=0, concat_axis=0, tiled=True)

time: 119 us -> 119 us (level)
  no operation moved by 1% of the time
where the time goes in v7:
time: 119 us; the launch traced here: 118 us
  starting transfers between devices  45.2 us (38%)
  blocking collectives  31.6 us (27%)
  Pallas kernels  18.6 us (16%)
  waiting for transfers between devices  14.1 us (12%)
  local copies, waits for them, and re-layouts  7.55 us (6%)
    ppermute x7, starting transfers between devices, hop(): lax.ppermute(chunk, axis, [(i, (i + by) % size) for i in range(size)])  22.3 us
    all_gather x1, blocking collectives, shards(): a = lax.all_gather(compact(got), 'quad')  17.6 us
    all_to_all x1, blocking collectives, shards(): lax.all_to_all(kept, 'z', split_axis=0, concat_axis=0, tiled=True)  14 us
    all_to_all x1, starting transfers between devices, shards(): got = lax.all_to_all(sent, group, split_axis=0, concat_axis=0, tiled=True)  11.8 us
    ppermute x7, waiting for transfers between devices, hop(): lax.ppermute(chunk, axis, [(i, (i + by) % size) for i in range(size)])  8.84 us
    ppermute x1, starting transfers between devices, shards(): kept = kept + lax.ppermute(passed, 'core', [(0, 1), (1, 0)])  7.51 us
    pallas_call x1, Pallas kernels, late_product(): pl.pallas_call(late_kernel, out_shape=(jax.ShapeDtypeStruct((PAIRS // 2,...  4.7 us
    pallas_call x1, Pallas kernels, split_share(): pl.pallas_call(share_kernel, out_shape=jax.ShapeDtypeStruct((XS, 2, 512,...  4.7 us
  transfers between devices with their start and end apart: 10, of which 4 were waited for; matrix products, arithmetic and copies ran while one was open for 3% of the time, Pallas kernels for 10%

profile of v7, /device:TPU:1, one launch (start us, length us, event | category | flops | bytes accessed | tf_op | source)
XLA Modules:
  0.0 118.1 jit_solution(5323965560750008026)
XLA Ops:
  0.0 2.0 %encode.1 = (bf16[16,32,128]{2,1,0:T(8,128)(2,1)}, s32[16]{0:T(128)}) custom-call(s32[19]{0:T(128)} %nodes.2, f32[512]{0:T(512)} %constant.8.clone.table, bf16[96,128]{1,0:T(8,128)(2,1)} %bitcast.24), custom_call_target="tpu_custom_call" | custom-call | tf_op jit(solution)/shard_map/encode/pallas_call | solution.py:161
  2.0 11.8 %all-to-all-start = ((bf16[16,32,128]{2,1,0:T(8,128)(2,1)}), bf16[16,32,128]{2,1,0:T(8,128)(2,1)S(1)}, u32[]{:S(2)}, u32[]{:S(2)}) async-start(bf16[16,32,128]{2,1,0:T(8,128)(2,1)} %get-tuple-element.14), calls=%async_computation | async-start | bytes 262144 | tf_op jit(solution)/shard_map/all_to_all | solution.py:406
  13.9 1.6 %slice-done = bf16[1,4096,2,128]{3,2,1,0:T(2,128)(2,1)S(1)} async-done(((bf16[2,4096,2,128]{3,2,1,0:T(2,128)(2,1)}), bf16[1,4096,2,128]{3,2,1,0:T(2,128)(2,1)S(1)}, s32[]{:S(2)}) %slice-start) | async-done | bytes 2097176 | tf_op jit(solution)/shard_map/slice | solution.py:410
  15.5 3.3 %copy.11 = bf16[32,16,8,2,128]{4,3,2,0,1:T(2,128)(2,1)} copy(bf16[32,16,8,2,128]{4,3,2,1,0:T(2,128)(2,1)S(1)} %bitcast.15) | data formatting | bytes 4194304 | tf_op jit(solution)/shard_map/reshape;squeeze | solution.py:410
  18.8 4.0 %all-to-all-done.got = bf16[16,32,128]{2,1,0:T(8,128)(2,1)S(1)} async-done(((bf16[16,32,128]{2,1,0:T(8,128)(2,1)}), bf16[16,32,128]{2,1,0:T(8,128)(2,1)S(1)}, u32[]{:S(2)}, u32[]{:S(2)}) %all-to-all-start) | async-done | bytes 131104 | tf_op jit(solution)/shard_map/all_to_all | solution.py:406
  23.4 3.6 %all-to-all-start.1 = ((bf16[16,32,8,2,128]{4,3,2,1,0:T(2,128)(2,1)}), bf16[16,32,8,2,128]{4,3,2,1,0:T(2,128)(2,1)S(1)}, u32[]{:S(2)}, u32[]{:S(2)}) async-start(bf16[16,32,8,2,128]{4,3,2,1,0:T(2,128)(2,1)} %bitcast.16), calls=%async_computation.1 | async-start | bytes 4194304 | tf_op jit(solution)/shard_map/all_to_all | solution.py:412
  27.0 1.6 %compact.1 = bf16[464,128]{1,0:T(8,128)(2,1)} custom-call(bf16[16,32,128]{2,1,0:T(8,128)(2,1)} %copy-done.4), custom_call_target="tpu_custom_call" | custom-call | tf_op jit(solution)/shard_map/compact/pallas_call | solution.py:203
  28.7 17.6 %all-gather = bf16[1856,128]{1,0:T(8,128)(2,1)S(1)} all-gather(bf16[464,128]{1,0:T(8,128)(2,1)} %compact.1), channel_id=2, replica_groups=mesh['z'=8,'core'=2,'x'=4,'quad'=4,'parity'=2] {'quad'}, dimensions={0}, use_global_device_ids=true | all-gather | bytes 593920 | tf_op jit(solution)/shard_map/all_gather | solution.py:413
  46.3 4.4 %collective-permute-start.2 = (bf16[4,464,128]{2,1,0:T(8,128)(2,1)S(1)}, bf16[4,464,128]{2,1,0:T(8,128)(2,1)S(1)}, u32[]{:S(2)}, u32[]{:S(2)}) collective-permute-start(bf16[4,464,128]{2,1,0:T(8,128)(2,1)S(1)} %bitcast.17), channel_id=1, source_target_pairs={{0,24},{8,0},{16,8},{24,16},{1,25},{9,1},{17,9},{25,17},{2,26},{10... | collective-permute-start | bytes 1425416 | tf_op jit(solution)/shard_map/ppermute | solution.py:416
  50.7 1.9 %collective-permute-start.1 = (bf16[4,464,128]{2,1,0:T(8,128)(2,1)S(1)}, bf16[4,464,128]{2,1,0:T(8,128)(2,1)S(1)}, u32[]{:S(2)}, u32[]{:S(2)}) collective-permute-start(bf16[4,464,128]{2,1,0:T(8,128)(2,1)S(1)} %bitcast.18), channel_id=1, source_target_pairs={{0,8},{8,16},{16,24},{24,0},{1,9},{9,17},{17,25},{25,1},{2,10},{10... | collective-permute-start | bytes 1425416 | tf_op jit(solution)/shard_map/ppermute | solution.py:416
  52.7 7.1 %collective-permute-done.2.c3 = bf16[4,464,128]{2,1,0:T(8,128)(2,1)S(1)} collective-permute-done((bf16[4,464,128]{2,1,0:T(8,128)(2,1)S(1)}, bf16[4,464,128]{2,1,0:T(8,128)(2,1)S(1)}, u32[]{:S(2)}, u32[]{:S(2)}) %collective-permute-start.2) | collective-permute-done | bytes 475168 | tf_op jit(solution)/shard_map/ppermute | solution.py:416
  59.8 1.9 %collective-permute-start.4 = (bf16[4,464,128]{2,1,0:T(8,128)(2,1)S(1)}, bf16[4,464,128]{2,1,0:T(8,128)(2,1)}, u32[]{:S(2)}, u32[]{:S(2)}) collective-permute-start(bf16[4,464,128]{2,1,0:T(8,128)(2,1)S(1)} %collective-permute-done.2.c3), channel_id=1, source_target_pairs={{0,7},{1,0},{2,1},{3,2},{4,3},{5,4},{6,5},{7,6},{8,15},{9,8},{10,9... | collective-permute-start | bytes 1425416 | tf_op jit(solution)/shard_map/ppermute | solution.py:416
  61.7 4.0 %collective-permute-start = (bf16[4,464,128]{2,1,0:T(8,128)(2,1)S(1)}, bf16[4,464,128]{2,1,0:T(8,128)(2,1)}, u32[]{:S(2)}, u32[]{:S(2)}) collective-permute-start(bf16[4,464,128]{2,1,0:T(8,128)(2,1)S(1)} %bitcast.19), channel_id=1, source_target_pairs={{0,7},{1,0},{2,1},{3,2},{4,3},{5,4},{6,5},{7,6},{8,15},{9,8},{10,9... | collective-permute-start | bytes 1425416 | tf_op jit(solution)/shard_map/ppermute | solution.py:416
  65.7 1.9 %collective-permute-start.3 = (bf16[4,464,128]{2,1,0:T(8,128)(2,1)S(1)}, bf16[4,464,128]{2,1,0:T(8,128)(2,1)}, u32[]{:S(2)}, u32[]{:S(2)}) collective-permute-start(bf16[4,464,128]{2,1,0:T(8,128)(2,1)S(1)} %collective-permute-done.1.c2), channel_id=1, source_target_pairs={{0,1},{1,2},{2,3},{3,4},{4,5},{5,6},{6,7},{7,0},{8,9},{9,10},{10,1... | collective-permute-start | bytes 1425416 | tf_op jit(solution)/shard_map/ppermute | solution.py:416
  67.6 2.8 %collective-permute-start.5 = (bf16[4,464,128]{2,1,0:T(8,128)(2,1)S(1)}, bf16[4,464,128]{2,1,0:T(8,128)(2,1)}, u32[]{:S(2)}, u32[]{:S(2)}) collective-permute-start(bf16[4,464,128]{2,1,0:T(8,128)(2,1)S(1)} %collective-permute-done.1.c2), channel_id=1, source_target_pairs={{0,8},{8,16},{16,24},{24,0},{1,9},{9,17},{17,25},{25,1},{2,10},{10... | collective-permute-start | bytes 1425416 | tf_op jit(solution)/shard_map/ppermute | solution.py:416
  70.5 1.7 %collective-permute-done.4.c5 = bf16[4,464,128]{2,1,0:T(8,128)(2,1)} collective-permute-done((bf16[4,464,128]{2,1,0:T(8,128)(2,1)S(1)}, bf16[4,464,128]{2,1,0:T(8,128)(2,1)}, u32[]{:S(2)}, u32[]{:S(2)}) %collective-permute-start.4) | collective-permute-done | bytes 475168 | tf_op jit(solution)/shard_map/ppermute | solution.py:416
  72.2 5.3 %collective-permute-start.6 = (bf16[4,464,128]{2,1,0:T(8,128)(2,1)}, bf16[4,464,128]{2,1,0:T(8,128)(2,1)}, u32[]{:S(2)}, u32[]{:S(2)}) collective-permute-start(bf16[4,464,128]{2,1,0:T(8,128)(2,1)} %collective-permute-done.4.c5), channel_id=1, source_target_pairs={{0,24},{8,0},{16,8},{24,16},{1,25},{9,1},{17,9},{25,17},{2,26},{10... | collective-permute-start | bytes 1425416 | tf_op jit(solution)/shard_map/ppermute | solution.py:416
  77.5 4.7 %split_share.1.share = bf16[4,2,512,256]{3,2,1,0:T(8,128)(2,1)} custom-call(s32[16]{0:T(128)} %get-tuple-element.13.picks, bf16[2,8192,128]{2,1,0:T(8,128)(2,1)} %bitcast.14), custom_call_target="tpu_custom_call" | custom-call | flops 400000000 | bytes 4200000 | tf_op jit(solution)/shard_map/split_share/pallas_call | solution.py:229
  82.2 1.5 %weights.1 = f32[32,128]{1,0:T(8,128)} custom-call(s32[19]{0:T(128)} %nodes.2, s32[16]{0:T(128)} %get-tuple-element.13.picks, f32[64]{0:T(128)} %constant.9.clone.points, f32[16,128]{1,0:T(8,128)} %constant.10.clone.grid), custom_call_target="tpu_custom_call" | custom-call | tf_op jit(solution)/shard_map/weights/pallas_call | solution.py:90
  83.8 1.3 %copy-done = bf16[16,32,8,2,128]{4,3,2,1,0:T(2,128)(2,1)} copy-done((bf16[16,32,8,2,128]{4,3,2,1,0:T(2,128)(2,1)}, bf16[16,32,8,2,128]{4,3,2,1,0:T(2,128)(2,1)S(1)}, u32[]{:S(2)}) %copy-start) | copy-done | bytes 2097176
  85.1 4.0 %early_product.1.before = f32[384,256]{1,0:T(8,128)} custom-call(s32[16]{0:T(128)} %get-tuple-element.13.picks, bf16[4,2,512,256]{3,2,1,0:T(8,128)(2,1)} %split_share.1.share, bf16[4,464,128]{2,1,0:T(8,128)(2,1)} %bitcast.20, bf16[4,464,128]{2,1,0:T(8,128)(2,1)} %collective-permute-done.c1, bf16[4,464,128]{2,1,0:T(8,128)(2,1)} %copy-done.3, ...), custom_call_target="tpu_custom_call" | custom-call | flops 400000000 | bytes 4200000 | tf_op jit(solution)/shard_map/early_product/pallas_call | solution.py:274
  89.1 4.7 %late_product.1 = (f32[8,48,128]{2,1,0:T(8,128)}, f32[8,48,128]{2,1,0:T(8,128)}) custom-call(s32[16]{0:T(128)} %get-tuple-element.13.picks, f32[32,128]{1,0:T(8,128)} %weights.1, bf16[4,2,512,256]{3,2,1,0:T(8,128)(2,1)} %split_share.1.share, bf16[16,512,128]{2,1,0:T(8,128)(2,1)} %bitcast.13, f32[384,256]{1,0:T(8,128)} %early_product.1.before, ...), custom_call_target="tpu_custom_call" | custom-call | tf_op jit(solution)/shard_map/late_product/pallas_call | solution.py:370
  93.8 7.5 %collective-permute-start.7 = (f32[8,48,128]{2,1,0:T(8,128)}, f32[8,48,128]{2,1,0:T(8,128)S(1)}, u32[]{:S(2)}, u32[]{:S(2)}) collective-permute-start(f32[8,48,128]{2,1,0:T(8,128)} %get-tuple-element.20), channel_id=1, source_target_pairs={{0,32},{32,0},{1,33},{33,1},{2,34},{34,2},{3,35},{35,3},{4,36},{36... | collective-permute-start | bytes 589832 | tf_op jit(solution)/shard_map/ppermute | solution.py:434
  103.5 14.0 %all_to_all.15 = f32[8,48,128]{2,1,0:T(8,128)S(1)} all-to-all(f32[8,48,128]{2,1,0:T(8,128)S(1)} %add.3), channel_id=1, replica_groups=mesh['z'=8,'core'=2,'x'=4,'quad'=4,'parity'=2] {'z'}, dimensions={0} | all-to-all | bytes 393216 | tf_op jit(solution)/shard_map/all_to_all | solution.py:435
  (23 shorter events, 3.6 us)
Async XLA Ops:
  2.0 20.7 %all-to-all-start = ((bf16[16,32,128]{2,1,0:T(8,128)(2,1)}), bf16[16,32,128]{2,1,0:T(8,128)(2,1)S(1)}, u32[]{:S(2)}, u32[]{:S(2)}) async-start(bf16[16,32,128]{2,1,0:T(8,128)(2,1)} %get-tuple-element.14), calls=%async_computation | async-start | bytes 262144 | tf_op jit(solution)/shard_map/all_to_all | solution.py:406
  13.9 1.6 %slice-start = ((bf16[2,4096,2,128]{3,2,1,0:T(2,128)(2,1)}), bf16[1,4096,2,128]{3,2,1,0:T(2,128)(2,1)S(1)}, s32[]{:S(2)}) async-start(bf16[2,4096,2,128]{3,2,1,0:T(2,128)(2,1)} %param.7), calls=%async_computation.3 | async-start | bytes 4194304 | tf_op jit(solution)/shard_map/slice | solution.py:410
  22.8 0.7 copy-start.4
  23.4 60.3 %all-to-all-start.1 = ((bf16[16,32,8,2,128]{4,3,2,1,0:T(2,128)(2,1)}), bf16[16,32,8,2,128]{4,3,2,1,0:T(2,128)(2,1)S(1)}, u32[]{:S(2)}, u32[]{:S(2)}) async-start(bf16[16,32,8,2,128]{4,3,2,1,0:T(2,128)(2,1)} %bitcast.16), calls=%async_computation.1 | async-start | bytes 4194304 | tf_op jit(solution)/shard_map/all_to_all | solution.py:412
  46.3 35.9 %copy-start.1 = (bf16[1856,128]{1,0:T(8,128)(2,1)}, bf16[1856,128]{1,0:T(8,128)(2,1)S(1)}, u32[]{:S(2)}) copy-start(bf16[1856,128]{1,0:T(8,128)(2,1)S(1)} %all-gather) | copy-start | bytes 1425412
  46.3 13.4 %collective-permute-start.2 = (bf16[4,464,128]{2,1,0:T(8,128)(2,1)S(1)}, bf16[4,464,128]{2,1,0:T(8,128)(2,1)S(1)}, u32[]{:S(2)}, u32[]{:S(2)}) collective-permute-start(bf16[4,464,128]{2,1,0:T(8,128)(2,1)S(1)} %bitcast.17), channel_id=1, source_target_pairs={{0,24},{8,0},{16,8},{24,16},{1,25},{9,1},{17,9},{25,17},{2,26},{10... | collective-permute-start | bytes 1425416 | tf_op jit(solution)/shard_map/ppermute | solution.py:416
  50.7 15.0 %collective-permute-start.1 = (bf16[4,464,128]{2,1,0:T(8,128)(2,1)S(1)}, bf16[4,464,128]{2,1,0:T(8,128)(2,1)S(1)}, u32[]{:S(2)}, u32[]{:S(2)}) collective-permute-start(bf16[4,464,128]{2,1,0:T(8,128)(2,1)S(1)} %bitcast.18), channel_id=1, source_target_pairs={{0,8},{8,16},{16,24},{24,0},{1,9},{9,17},{17,25},{25,1},{2,10},{10... | collective-permute-start | bytes 1425416 | tf_op jit(solution)/shard_map/ppermute | solution.py:416
  59.8 22.4 %copy-start.2 = (bf16[4,464,128]{2,1,0:T(8,128)(2,1)}, bf16[4,464,128]{2,1,0:T(8,128)(2,1)S(1)}, u32[]{:S(2)}) copy-start(bf16[4,464,128]{2,1,0:T(8,128)(2,1)S(1)} %collective-permute-done.2.c3) | copy-start | bytes 1425412
  59.8 12.4 %collective-permute-start.4 = (bf16[4,464,128]{2,1,0:T(8,128)(2,1)S(1)}, bf16[4,464,128]{2,1,0:T(8,128)(2,1)}, u32[]{:S(2)}, u32[]{:S(2)}) collective-permute-start(bf16[4,464,128]{2,1,0:T(8,128)(2,1)S(1)} %collective-permute-done.2.c3), channel_id=1, source_target_pairs={{0,7},{1,0},{2,1},{3,2},{4,3},{5,4},{6,5},{7,6},{8,15},{9,8},{10,9... | collective-permute-start | bytes 1425416 | tf_op jit(solution)/shard_map/ppermute | solution.py:416
  61.7 22.1 %collective-permute-start = (bf16[4,464,128]{2,1,0:T(8,128)(2,1)S(1)}, bf16[4,464,128]{2,1,0:T(8,128)(2,1)}, u32[]{:S(2)}, u32[]{:S(2)}) collective-permute-start(bf16[4,464,128]{2,1,0:T(8,128)(2,1)S(1)} %bitcast.19), channel_id=1, source_target_pairs={{0,7},{1,0},{2,1},{3,2},{4,3},{5,4},{6,5},{7,6},{8,15},{9,8},{10,9... | collective-permute-start | bytes 1425416 | tf_op jit(solution)/shard_map/ppermute | solution.py:416
  65.7 16.5 %copy-start.3 = (bf16[4,464,128]{2,1,0:T(8,128)(2,1)}, bf16[4,464,128]{2,1,0:T(8,128)(2,1)S(1)}, u32[]{:S(2)}) copy-start(bf16[4,464,128]{2,1,0:T(8,128)(2,1)S(1)} %collective-permute-done.1.c2) | copy-start | bytes 1425412
  65.7 18.1 %collective-permute-start.3 = (bf16[4,464,128]{2,1,0:T(8,128)(2,1)S(1)}, bf16[4,464,128]{2,1,0:T(8,128)(2,1)}, u32[]{:S(2)}, u32[]{:S(2)}) collective-permute-start(bf16[4,464,128]{2,1,0:T(8,128)(2,1)S(1)} %collective-permute-done.1.c2), channel_id=1, source_target_pairs={{0,1},{1,2},{2,3},{3,4},{4,5},{5,6},{6,7},{7,0},{8,9},{9,10},{10,1... | collective-permute-start | bytes 1425416 | tf_op jit(solution)/shard_map/ppermute | solution.py:416
  67.6 21.4 %collective-permute-start.5 = (bf16[4,464,128]{2,1,0:T(8,128)(2,1)S(1)}, bf16[4,464,128]{2,1,0:T(8,128)(2,1)}, u32[]{:S(2)}, u32[]{:S(2)}) collective-permute-start(bf16[4,464,128]{2,1,0:T(8,128)(2,1)S(1)} %collective-permute-done.1.c2), channel_id=1, source_target_pairs={{0,8},{8,16},{16,24},{24,0},{1,9},{9,17},{17,25},{25,1},{2,10},{10... | collective-permute-start | bytes 1425416 | tf_op jit(solution)/shard_map/ppermute | solution.py:416
  72.2 16.9 %collective-permute-start.6 = (bf16[4,464,128]{2,1,0:T(8,128)(2,1)}, bf16[4,464,128]{2,1,0:T(8,128)(2,1)}, u32[]{:S(2)}, u32[]{:S(2)}) collective-permute-start(bf16[4,464,128]{2,1,0:T(8,128)(2,1)} %collective-permute-done.4.c5), channel_id=1, source_target_pairs={{0,24},{8,0},{16,8},{24,16},{1,25},{9,1},{17,9},{25,17},{2,26},{10... | collective-permute-start | bytes 1425416 | tf_op jit(solution)/shard_map/ppermute | solution.py:416
  83.8 1.3 %copy-start = (bf16[16,32,8,2,128]{4,3,2,1,0:T(2,128)(2,1)}, bf16[16,32,8,2,128]{4,3,2,1,0:T(2,128)(2,1)S(1)}, u32[]{:S(2)}) copy-start(bf16[16,32,8,2,128]{4,3,2,1,0:T(2,128)(2,1)S(1)} %all-to-all-done.1) | copy-start | bytes 6291460
  93.8 8.8 %collective-permute-start.7 = (f32[8,48,128]{2,1,0:T(8,128)}, f32[8,48,128]{2,1,0:T(8,128)S(1)}, u32[]{:S(2)}, u32[]{:S(2)}) collective-permute-start(f32[8,48,128]{2,1,0:T(8,128)} %get-tuple-element.20), channel_id=1, source_target_pairs={{0,32},{32,0},{1,33},{33,1},{2,34},{34,2},{3,35},{35,3},{4,36},{36... | collective-permute-start | bytes 589832 | tf_op jit(solution)/shard_map/ppermute | solution.py:434

commit v8 on v5

--- a/solution.py
+++ b/solution.py
@@ -250,8 +250,8 @@
     return jnp.dot(a, b, preferred_element_type=jnp.float32)
 
 
-EARLY = ((0, True), (0, False), (-1, True), (1, True), (-1, False), (1, False))
-LATE = ((2, True), (2, False))
+EARLY = ((0, True), (0, False), (-1, True), (1, True), (1, False), (2, False))
+LATE = ((2, True), (-1, False))
 
 
 def block_of(picks, kind):
@@ -416,17 +416,18 @@
     nodes, whole, a = lax.optimization_barrier((responding_nodes, second_operand_encoded, a))
     right_a = hop(a, "x", XS, 1)
     left_a = hop(a, "x", XS, -1)
-    b = hop(a, y_axes, YS, -1)
-    right_b = hop(right_a, y_axes, YS, 1)
+    b = hop(a, y_axes, YS, 1)
+    right_b = hop(right_a, y_axes, YS, -1)
     left_b = hop(left_a, y_axes, YS, -1)
     far_a = hop(right_a, "x", XS, 1)
-    far_b = hop(left_b, "x", XS, -1)
+    slant = [(YS * x + y, YS * ((x - 1) % XS) + (y + 1) % YS) for x in range(XS) for y in range(YS)]
+    far_b = lax.ppermute(left_a, ("x",) + y_axes, slant)
     share = split_share(picks, whole.reshape(2, 8192, 128))
     weights = decode_weights(nodes, picks)
-    early = (a, b, right_a, left_a, right_b, left_b)
+    early = (a, b, right_a, left_a, left_b, far_b)
     before = early_product(picks, share, early)
     kept, passed = late_product(
-        picks, weights, share, spread.reshape(PAIRS, 512, 128), before, early, (far_a, far_b)
+        picks, weights, share, spread.reshape(PAIRS, 512, 128), before, early, (far_a, right_b)
     )
     kept = kept + lax.ppermute(passed, "core", [(0, 1), (1, 0)])
     received = lax.all_to_all(kept, "z", split_axis=0, concat_axis=0, tiled=True)

time: 119 us -> 117 us (0.983); the launches traced: 118 us -> 115 us
  starting transfers between devices: 45.2 us -> 42.2 us
    ppermute x7 -> x6, starting transfers between devices: 22.3 us -> 19.5 us  [hop(): lax.ppermute(chunk, axis, [(i, (i + by) % size) for i in range(size)])]
    ppermute x1, starting transfers between devices: 7.51 us -> 5.05 us  [shards(): kept = kept + lax.ppermute(passed, 'core', [(0, 1), (1, 0)])]
    ppermute x0 -> x1, starting transfers between devices: none -> 2.21 us  [shards(): far_b = lax.ppermute(left_a, ('x',) + y_axes, slant)]
    ppermute x7 -> x6, waiting for transfers between devices: 8.84 us -> 9.21 us  [hop(): lax.ppermute(chunk, axis, [(i, (i + by) % size) for i in range(size)])]
where the time goes in v8:
time: 117 us; the launch traced here: 115 us
  starting transfers between devices  42.2 us (36%)
  blocking collectives  31 us (26%)
  Pallas kernels  18.5 us (16%)
  waiting for transfers between devices  14.4 us (12%)
  local copies, waits for them, and re-layouts  7.58 us (6%)
    ppermute x6, starting transfers between devices, hop(): lax.ppermute(chunk, axis, [(i, (i + by) % size) for i in range(size)])  19.5 us
    all_gather x1, blocking collectives, shards(): a = lax.all_gather(compact(got), 'quad')  17.6 us
    all_to_all x1, blocking collectives, shards(): lax.all_to_all(kept, 'z', split_axis=0, concat_axis=0, tiled=True)  13.3 us
    all_to_all x1, starting transfers between devices, shards(): got = lax.all_to_all(sent, group, split_axis=0, concat_axis=0, tiled=True)  11.8 us
    ppermute x6, waiting for transfers between devices, hop(): lax.ppermute(chunk, axis, [(i, (i + by) % size) for i in range(size)])  9.21 us
    ppermute x1, starting transfers between devices, shards(): kept = kept + lax.ppermute(passed, 'core', [(0, 1), (1, 0)])  5.05 us
    pallas_call x1, Pallas kernels, late_product(): pl.pallas_call(late_kernel, out_shape=(jax.ShapeDtypeStruct((PAIRS // 2,...  4.7 us
    pallas_call x1, Pallas kernels, split_share(): pl.pallas_call(share_kernel, out_shape=jax.ShapeDtypeStruct((XS, 2, 512,...  4.68 us
  transfers between devices with their start and end apart: 10, of which 4 were waited for; matrix products, arithmetic and copies ran while one was open for 3% of the time, Pallas kernels for 10%

profile of v8, /device:TPU:1, one launch (start us, length us, event | category | flops | bytes accessed | tf_op | source)
XLA Modules:
  0.0 114.8 jit_solution(3386232371128120130)
XLA Ops:
  0.0 2.0 %encode.1 = (bf16[16,32,128]{2,1,0:T(8,128)(2,1)}, s32[16]{0:T(128)}) custom-call(s32[19]{0:T(128)} %nodes.2, f32[512]{0:T(512)} %constant.8.clone.table, bf16[96,128]{1,0:T(8,128)(2,1)} %bitcast.23), custom_call_target="tpu_custom_call" | custom-call | tf_op jit(solution)/shard_map/encode/pallas_call | solution.py:161
  2.0 11.8 %all-to-all-start = ((bf16[16,32,128]{2,1,0:T(8,128)(2,1)}), bf16[16,32,128]{2,1,0:T(8,128)(2,1)S(1)}, u32[]{:S(2)}, u32[]{:S(2)}) async-start(bf16[16,32,128]{2,1,0:T(8,128)(2,1)} %get-tuple-element.15), calls=%async_computation | async-start | bytes 262144 | tf_op jit(solution)/shard_map/all_to_all | solution.py:405
  13.9 1.6 %slice-done = bf16[1,4096,2,128]{3,2,1,0:T(2,128)(2,1)S(1)} async-done(((bf16[2,4096,2,128]{3,2,1,0:T(2,128)(2,1)}), bf16[1,4096,2,128]{3,2,1,0:T(2,128)(2,1)S(1)}, s32[]{:S(2)}) %slice-start) | async-done | bytes 2097176 | tf_op jit(solution)/shard_map/slice | solution.py:407
  15.4 3.4 %copy.11 = bf16[32,16,8,2,128]{4,3,2,0,1:T(2,128)(2,1)} copy(bf16[32,16,8,2,128]{4,3,2,1,0:T(2,128)(2,1)S(1)} %bitcast.13) | data formatting | bytes 4194304 | tf_op jit(solution)/shard_map/reshape;squeeze | solution.py:407
  18.8 3.9 %all-to-all-done.got = bf16[16,32,128]{2,1,0:T(8,128)(2,1)S(1)} async-done(((bf16[16,32,128]{2,1,0:T(8,128)(2,1)}), bf16[16,32,128]{2,1,0:T(8,128)(2,1)S(1)}, u32[]{:S(2)}, u32[]{:S(2)}) %all-to-all-start) | async-done | bytes 131104 | tf_op jit(solution)/shard_map/all_to_all | solution.py:405
  23.4 3.6 %all-to-all-start.1 = ((bf16[16,32,8,2,128]{4,3,2,1,0:T(2,128)(2,1)}), bf16[16,32,8,2,128]{4,3,2,1,0:T(2,128)(2,1)S(1)}, u32[]{:S(2)}, u32[]{:S(2)}) async-start(bf16[16,32,8,2,128]{4,3,2,1,0:T(2,128)(2,1)} %bitcast.14), calls=%async_computation.1 | async-start | bytes 4194304 | tf_op jit(solution)/shard_map/all_to_all | solution.py:409
  27.0 1.7 %compact.1 = bf16[464,128]{1,0:T(8,128)(2,1)} custom-call(bf16[16,32,128]{2,1,0:T(8,128)(2,1)} %copy-done.4), custom_call_target="tpu_custom_call" | custom-call | tf_op jit(solution)/shard_map/compact/pallas_call | solution.py:203
  28.7 17.6 %all-gather = bf16[1856,128]{1,0:T(8,128)(2,1)S(1)} all-gather(bf16[464,128]{1,0:T(8,128)(2,1)} %compact.1), channel_id=2, replica_groups=mesh['z'=8,'core'=2,'x'=4,'quad'=4,'parity'=2] {'quad'}, dimensions={0}, use_global_device_ids=true | all-gather | bytes 593920 | tf_op jit(solution)/shard_map/all_gather | solution.py:410
  46.3 4.4 %collective-permute-start.2 = (bf16[4,464,128]{2,1,0:T(8,128)(2,1)S(1)}, bf16[4,464,128]{2,1,0:T(8,128)(2,1)S(1)}, u32[]{:S(2)}, u32[]{:S(2)}) collective-permute-start(bf16[4,464,128]{2,1,0:T(8,128)(2,1)S(1)} %bitcast.16), channel_id=1, source_target_pairs={{0,24},{8,0},{16,8},{24,16},{1,25},{9,1},{17,9},{25,17},{2,26},{10... | collective-permute-start | bytes 1425416 | tf_op jit(solution)/shard_map/ppermute | solution.py:413
  50.7 1.9 %collective-permute-start.1 = (bf16[4,464,128]{2,1,0:T(8,128)(2,1)S(1)}, bf16[4,464,128]{2,1,0:T(8,128)(2,1)S(1)}, u32[]{:S(2)}, u32[]{:S(2)}) collective-permute-start(bf16[4,464,128]{2,1,0:T(8,128)(2,1)S(1)} %bitcast.17), channel_id=1, source_target_pairs={{0,8},{8,16},{16,24},{24,0},{1,9},{9,17},{17,25},{25,1},{2,10},{10... | collective-permute-start | bytes 1425416 | tf_op jit(solution)/shard_map/ppermute | solution.py:413
  52.6 1.9 %collective-permute-start = (bf16[4,464,128]{2,1,0:T(8,128)(2,1)S(1)}, bf16[4,464,128]{2,1,0:T(8,128)(2,1)}, u32[]{:S(2)}, u32[]{:S(2)}) collective-permute-start(bf16[4,464,128]{2,1,0:T(8,128)(2,1)S(1)} %bitcast.18), channel_id=1, source_target_pairs={{0,1},{1,2},{2,3},{3,4},{4,5},{5,6},{6,7},{7,0},{8,9},{9,10},{10,1... | collective-permute-start | bytes 1425416 | tf_op jit(solution)/shard_map/ppermute | solution.py:413
  54.6 5.2 %collective-permute-done.2.c3 = bf16[4,464,128]{2,1,0:T(8,128)(2,1)S(1)} collective-permute-done((bf16[4,464,128]{2,1,0:T(8,128)(2,1)S(1)}, bf16[4,464,128]{2,1,0:T(8,128)(2,1)S(1)}, u32[]{:S(2)}, u32[]{:S(2)}) %collective-permute-start.2) | collective-permute-done | bytes 475168 | tf_op jit(solution)/shard_map/ppermute | solution.py:413
  59.8 2.2 %collective-permute-start.4 = (bf16[4,464,128]{2,1,0:T(8,128)(2,1)S(1)}, bf16[4,464,128]{2,1,0:T(8,128)(2,1)}, u32[]{:S(2)}, u32[]{:S(2)}) collective-permute-start(bf16[4,464,128]{2,1,0:T(8,128)(2,1)S(1)} %collective-permute-done.2.c3), channel_id=1, source_target_pairs={{0,25},{1,26},{2,27},{3,28},{4,29},{5,30},{6,31},{7,24},{8,1},{9,2... | collective-permute-start | bytes 1425416 | tf_op jit(solution)/shard_map/ppermute | solution.py:424
  62.0 7.4 %collective-permute-start.3 = (bf16[4,464,128]{2,1,0:T(8,128)(2,1)S(1)}, bf16[4,464,128]{2,1,0:T(8,128)(2,1)}, u32[]{:S(2)}, u32[]{:S(2)}) collective-permute-start(bf16[4,464,128]{2,1,0:T(8,128)(2,1)S(1)} %collective-permute-done.2.c3), channel_id=1, source_target_pairs={{0,7},{1,0},{2,1},{3,2},{4,3},{5,4},{6,5},{7,6},{8,15},{9,8},{10,9... | collective-permute-start | bytes 1425416 | tf_op jit(solution)/shard_map/ppermute | solution.py:413
  69.4 1.9 %collective-permute-start.6 = (bf16[4,464,128]{2,1,0:T(8,128)(2,1)S(1)}, bf16[4,464,128]{2,1,0:T(8,128)(2,1)}, u32[]{:S(2)}, u32[]{:S(2)}) collective-permute-start(bf16[4,464,128]{2,1,0:T(8,128)(2,1)S(1)} %collective-permute-done.1.c2), channel_id=1, source_target_pairs={{0,7},{1,0},{2,1},{3,2},{4,3},{5,4},{6,5},{7,6},{8,15},{9,8},{10,9... | collective-permute-start | bytes 1425416 | tf_op jit(solution)/shard_map/ppermute | solution.py:413
  71.3 1.9 %collective-permute-start.5 = (bf16[4,464,128]{2,1,0:T(8,128)(2,1)S(1)}, bf16[4,464,128]{2,1,0:T(8,128)(2,1)}, u32[]{:S(2)}, u32[]{:S(2)}) collective-permute-start(bf16[4,464,128]{2,1,0:T(8,128)(2,1)S(1)} %collective-permute-done.1.c2), channel_id=1, source_target_pairs={{0,8},{8,16},{16,24},{24,0},{1,9},{9,17},{17,25},{25,1},{2,10},{10... | collective-permute-start | bytes 1425416 | tf_op jit(solution)/shard_map/ppermute | solution.py:413
  73.3 1.5 %weights.1 = f32[32,128]{1,0:T(8,128)} custom-call(s32[19]{0:T(128)} %nodes.2, s32[16]{0:T(128)} %get-tuple-element.14.picks, f32[64]{0:T(128)} %constant.9.clone.points, f32[16,128]{1,0:T(8,128)} %constant.10.clone.grid), custom_call_target="tpu_custom_call" | custom-call | tf_op jit(solution)/shard_map/weights/pallas_call | solution.py:90
  74.8 4.7 %split_share.1.share = bf16[4,2,512,256]{3,2,1,0:T(8,128)(2,1)} custom-call(s32[16]{0:T(128)} %get-tuple-element.14.picks, bf16[2,8192,128]{2,1,0:T(8,128)(2,1)} %bitcast.12), custom_call_target="tpu_custom_call" | custom-call | flops 400000000 | bytes 4200000 | tf_op jit(solution)/shard_map/split_share/pallas_call | solution.py:229
  79.5 4.0 %early_product.1.before = f32[384,256]{1,0:T(8,128)} custom-call(s32[16]{0:T(128)} %get-tuple-element.14.picks, bf16[4,2,512,256]{3,2,1,0:T(8,128)(2,1)} %split_share.1.share, bf16[4,464,128]{2,1,0:T(8,128)(2,1)} %bitcast.19, bf16[4,464,128]{2,1,0:T(8,128)(2,1)} %collective-permute-done.c1, bf16[4,464,128]{2,1,0:T(8,128)(2,1)} %copy-done.3, ...), custom_call_target="tpu_custom_call" | custom-call | flops 400000000 | bytes 4200000 | tf_op jit(solution)/shard_map/early_product/pallas_call | solution.py:274
  83.5 4.0 %collective-permute-done.6.c7 = bf16[4,464,128]{2,1,0:T(8,128)(2,1)} collective-permute-done((bf16[4,464,128]{2,1,0:T(8,128)(2,1)S(1)}, bf16[4,464,128]{2,1,0:T(8,128)(2,1)}, u32[]{:S(2)}, u32[]{:S(2)}) %collective-permute-start.6) | collective-permute-done | bytes 475168 | tf_op jit(solution)/shard_map/ppermute | solution.py:413
  87.5 1.3 %copy-done = bf16[16,32,8,2,128]{4,3,2,1,0:T(2,128)(2,1)} copy-done((bf16[16,32,8,2,128]{4,3,2,1,0:T(2,128)(2,1)}, bf16[16,32,8,2,128]{4,3,2,1,0:T(2,128)(2,1)S(1)}, u32[]{:S(2)}) %copy-start) | copy-done | bytes 2097176
  88.8 4.7 %late_product.1 = (f32[8,48,128]{2,1,0:T(8,128)}, f32[8,48,128]{2,1,0:T(8,128)}) custom-call(s32[16]{0:T(128)} %get-tuple-element.14.picks, f32[32,128]{1,0:T(8,128)} %weights.1, bf16[4,2,512,256]{3,2,1,0:T(8,128)(2,1)} %split_share.1.share, bf16[16,512,128]{2,1,0:T(8,128)(2,1)} %bitcast.15, f32[384,256]{1,0:T(8,128)} %early_product.1.before, ...), custom_call_target="tpu_custom_call" | custom-call | tf_op jit(solution)/shard_map/late_product/pallas_call | solution.py:369
  93.5 5.0 %collective-permute-start.7 = (f32[8,48,128]{2,1,0:T(8,128)}, f32[8,48,128]{2,1,0:T(8,128)S(1)}, u32[]{:S(2)}, u32[]{:S(2)}) collective-permute-start(f32[8,48,128]{2,1,0:T(8,128)} %get-tuple-element.22), channel_id=1, source_target_pairs={{0,32},{32,0},{1,33},{33,1},{2,34},{34,2},{3,35},{35,3},{4,36},{36... | collective-permute-start | bytes 589832 | tf_op jit(solution)/shard_map/ppermute | solution.py:432
  100.8 13.3 %all_to_all.15 = f32[8,48,128]{2,1,0:T(8,128)S(1)} all-to-all(f32[8,48,128]{2,1,0:T(8,128)S(1)} %add.3), channel_id=1, replica_groups=mesh['z'=8,'core'=2,'x'=4,'quad'=4,'parity'=2] {'z'}, dimensions={0} | all-to-all | bytes 393216 | tf_op jit(solution)/shard_map/all_to_all | solution.py:433
  (23 shorter events, 3.5 us)
Async XLA Ops:
  2.0 20.7 %all-to-all-start = ((bf16[16,32,128]{2,1,0:T(8,128)(2,1)}), bf16[16,32,128]{2,1,0:T(8,128)(2,1)S(1)}, u32[]{:S(2)}, u32[]{:S(2)}) async-start(bf16[16,32,128]{2,1,0:T(8,128)(2,1)} %get-tuple-element.15), calls=%async_computation | async-start | bytes 262144 | tf_op jit(solution)/shard_map/all_to_all | solution.py:405
  13.8 1.6 %slice-start = ((bf16[2,4096,2,128]{3,2,1,0:T(2,128)(2,1)}), bf16[1,4096,2,128]{3,2,1,0:T(2,128)(2,1)S(1)}, s32[]{:S(2)}) async-start(bf16[2,4096,2,128]{3,2,1,0:T(2,128)(2,1)} %param.7), calls=%async_computation.3 | async-start | bytes 4194304 | tf_op jit(solution)/shard_map/slice | solution.py:407
  22.7 0.7 copy-start.4
  23.4 64.1 %all-to-all-start.1 = ((bf16[16,32,8,2,128]{4,3,2,1,0:T(2,128)(2,1)}), bf16[16,32,8,2,128]{4,3,2,1,0:T(2,128)(2,1)S(1)}, u32[]{:S(2)}, u32[]{:S(2)}) async-start(bf16[16,32,8,2,128]{4,3,2,1,0:T(2,128)(2,1)} %bitcast.14), calls=%async_computation.1 | async-start | bytes 4194304 | tf_op jit(solution)/shard_map/all_to_all | solution.py:409
  46.3 33.2 %copy-start.1 = (bf16[1856,128]{1,0:T(8,128)(2,1)}, bf16[1856,128]{1,0:T(8,128)(2,1)S(1)}, u32[]{:S(2)}) copy-start(bf16[1856,128]{1,0:T(8,128)(2,1)S(1)} %all-gather) | copy-start | bytes 1425412
  46.3 13.4 %collective-permute-start.2 = (bf16[4,464,128]{2,1,0:T(8,128)(2,1)S(1)}, bf16[4,464,128]{2,1,0:T(8,128)(2,1)S(1)}, u32[]{:S(2)}, u32[]{:S(2)}) collective-permute-start(bf16[4,464,128]{2,1,0:T(8,128)(2,1)S(1)} %bitcast.16), channel_id=1, source_target_pairs={{0,24},{8,0},{16,8},{24,16},{1,25},{9,1},{17,9},{25,17},{2,26},{10... | collective-permute-start | bytes 1425416 | tf_op jit(solution)/shard_map/ppermute | solution.py:413
  50.7 18.7 %collective-permute-start.1 = (bf16[4,464,128]{2,1,0:T(8,128)(2,1)S(1)}, bf16[4,464,128]{2,1,0:T(8,128)(2,1)S(1)}, u32[]{:S(2)}, u32[]{:S(2)}) collective-permute-start(bf16[4,464,128]{2,1,0:T(8,128)(2,1)S(1)} %bitcast.17), channel_id=1, source_target_pairs={{0,8},{8,16},{16,24},{24,0},{1,9},{9,17},{17,25},{25,1},{2,10},{10... | collective-permute-start | bytes 1425416 | tf_op jit(solution)/shard_map/ppermute | solution.py:413
  52.6 26.9 %collective-permute-start = (bf16[4,464,128]{2,1,0:T(8,128)(2,1)S(1)}, bf16[4,464,128]{2,1,0:T(8,128)(2,1)}, u32[]{:S(2)}, u32[]{:S(2)}) collective-permute-start(bf16[4,464,128]{2,1,0:T(8,128)(2,1)S(1)} %bitcast.18), channel_id=1, source_target_pairs={{0,1},{1,2},{2,3},{3,4},{4,5},{5,6},{6,7},{7,0},{8,9},{9,10},{10,1... | collective-permute-start | bytes 1425416 | tf_op jit(solution)/shard_map/ppermute | solution.py:413
  59.8 19.7 %copy-start.2 = (bf16[4,464,128]{2,1,0:T(8,128)(2,1)}, bf16[4,464,128]{2,1,0:T(8,128)(2,1)S(1)}, u32[]{:S(2)}) copy-start(bf16[4,464,128]{2,1,0:T(8,128)(2,1)S(1)} %collective-permute-done.2.c3) | copy-start | bytes 1425412
  59.8 19.7 %collective-permute-start.4 = (bf16[4,464,128]{2,1,0:T(8,128)(2,1)S(1)}, bf16[4,464,128]{2,1,0:T(8,128)(2,1)}, u32[]{:S(2)}, u32[]{:S(2)}) collective-permute-start(bf16[4,464,128]{2,1,0:T(8,128)(2,1)S(1)} %collective-permute-done.2.c3), channel_id=1, source_target_pairs={{0,25},{1,26},{2,27},{3,28},{4,29},{5,30},{6,31},{7,24},{8,1},{9,2... | collective-permute-start | bytes 1425416 | tf_op jit(solution)/shard_map/ppermute | solution.py:424
  62.0 17.5 %collective-permute-start.3 = (bf16[4,464,128]{2,1,0:T(8,128)(2,1)S(1)}, bf16[4,464,128]{2,1,0:T(8,128)(2,1)}, u32[]{:S(2)}, u32[]{:S(2)}) collective-permute-start(bf16[4,464,128]{2,1,0:T(8,128)(2,1)S(1)} %collective-permute-done.2.c3), channel_id=1, source_target_pairs={{0,7},{1,0},{2,1},{3,2},{4,3},{5,4},{6,5},{7,6},{8,15},{9,8},{10,9... | collective-permute-start | bytes 1425416 | tf_op jit(solution)/shard_map/ppermute | solution.py:413
  69.4 10.1 %copy-start.3 = (bf16[4,464,128]{2,1,0:T(8,128)(2,1)}, bf16[4,464,128]{2,1,0:T(8,128)(2,1)S(1)}, u32[]{:S(2)}) copy-start(bf16[4,464,128]{2,1,0:T(8,128)(2,1)S(1)} %collective-permute-done.1.c2) | copy-start | bytes 1425412
  69.4 18.1 %collective-permute-start.6 = (bf16[4,464,128]{2,1,0:T(8,128)(2,1)S(1)}, bf16[4,464,128]{2,1,0:T(8,128)(2,1)}, u32[]{:S(2)}, u32[]{:S(2)}) collective-permute-start(bf16[4,464,128]{2,1,0:T(8,128)(2,1)S(1)} %collective-permute-done.1.c2), channel_id=1, source_target_pairs={{0,7},{1,0},{2,1},{3,2},{4,3},{5,4},{6,5},{7,6},{8,15},{9,8},{10,9... | collective-permute-start | bytes 1425416 | tf_op jit(solution)/shard_map/ppermute | solution.py:413
  71.3 16.2 %collective-permute-start.5 = (bf16[4,464,128]{2,1,0:T(8,128)(2,1)S(1)}, bf16[4,464,128]{2,1,0:T(8,128)(2,1)}, u32[]{:S(2)}, u32[]{:S(2)}) collective-permute-start(bf16[4,464,128]{2,1,0:T(8,128)(2,1)S(1)} %collective-permute-done.1.c2), channel_id=1, source_target_pairs={{0,8},{8,16},{16,24},{24,0},{1,9},{9,17},{17,25},{25,1},{2,10},{10... | collective-permute-start | bytes 1425416 | tf_op jit(solution)/shard_map/ppermute | solution.py:413
  87.5 1.3 %copy-start = (bf16[16,32,8,2,128]{4,3,2,1,0:T(2,128)(2,1)}, bf16[16,32,8,2,128]{4,3,2,1,0:T(2,128)(2,1)S(1)}, u32[]{:S(2)}) copy-start(bf16[16,32,8,2,128]{4,3,2,1,0:T(2,128)(2,1)S(1)} %all-to-all-done.1) | copy-start | bytes 6291460
  93.5 6.3 %collective-permute-start.7 = (f32[8,48,128]{2,1,0:T(8,128)}, f32[8,48,128]{2,1,0:T(8,128)S(1)}, u32[]{:S(2)}, u32[]{:S(2)}) collective-permute-start(f32[8,48,128]{2,1,0:T(8,128)} %get-tuple-element.22), channel_id=1, source_target_pairs={{0,32},{32,0},{1,33},{33,1},{2,34},{34,2},{3,35},{35,3},{4,36},{36... | collective-permute-start | bytes 589832 | tf_op jit(solution)/shard_map/ppermute | solution.py:432

commit v9 on v7

--- a/solution.py
+++ b/solution.py
@@ -250,8 +250,8 @@
     return jnp.dot(a, b, preferred_element_type=jnp.float32)
 
 
-EARLY = ((0, True), (0, False), (-1, True), (1, True), (-1, False), (1, False))
-LATE = ((2, True), (2, False))
+EARLY = ((0, True), (0, False), (-1, True), (1, True), (1, False), (2, False))
+LATE = ((2, True), (-1, False))
 
 
 def block_of(picks, kind):
@@ -405,8 +405,6 @@
     )
     got = lax.all_to_all(sent, group, split_axis=0, concat_axis=0, tiled=True)
 
-    share = split_share(picks, second_operand_encoded.reshape(2, 8192, 128))
-
     odd = second_operand_encoded[1].reshape(PANELS, PAIRS, 8, 2, 128).transpose(1, 0, 2, 3, 4)
     odd, got = lax.optimization_barrier((odd, got))
     spread = lax.all_to_all(odd, group, split_axis=0, concat_axis=0, tiled=True)
@@ -416,20 +414,22 @@
         return lax.ppermute(chunk, axis, [(i, (i + by) % size) for i in range(size)])
 
     y_axes = ("quad", "parity")
-    nodes, a = lax.optimization_barrier((responding_nodes, a))
+    nodes, whole, a = lax.optimization_barrier((responding_nodes, second_operand_encoded, a))
     right_a = hop(a, "x", XS, 1)
     left_a = hop(a, "x", XS, -1)
     b = hop(a, y_axes, YS, -1)
     right_b = hop(right_a, y_axes, YS, 1)
     left_b = hop(left_a, y_axes, YS, -1)
     far_a = hop(right_a, "x", XS, 1)
-    far_b = hop(left_b, "x", XS, -1)
+    slant = [(YS * x + y, YS * ((x - 1) % XS) + (y + 1) % YS) for x in range(XS) for y in range(YS)]
+    far_b = lax.ppermute(left_a, ("x",) + y_axes, slant)
+    share = split_share(picks, whole.reshape(2, 8192, 128))
     weights = decode_weights(nodes, picks)
-    early = (a, b, right_a, left_a, right_b, left_b)
+    early = (a, b, right_a, left_a, left_b, far_b)
     spread = spread.reshape(PAIRS, 512, 128)
     before = early_product(picks, share, early, spread)
     kept, passed = late_product(
-        picks, weights, share, spread, before, early, (far_a, far_b)
+        picks, weights, share, spread, before, early, (far_a, right_b)
     )
     kept = kept + lax.ppermute(passed, "core", [(0, 1), (1, 0)])
     received = lax.all_to_all(kept, "z", split_axis=0, concat_axis=0, tiled=True)

time: 119 us -> 113 us (0.950)
  starting transfers between devices: 45.2 us -> 41.9 us
  blocking collectives: 31.6 us -> 29.5 us
  waiting for transfers between devices: 14.1 us -> 12.3 us
    ppermute x7 -> x6, starting transfers between devices: 22.3 us -> 19.5 us  [hop(): lax.ppermute(chunk, axis, [(i, (i + by) % size) for i in range(size)])]
    ppermute x1, starting transfers between devices: 7.51 us -> 4.77 us  [shards(): kept = kept + lax.ppermute(passed, 'core', [(0, 1), (1, 0)])]
    ppermute x0 -> x1, starting transfers between devices: none -> 2.21 us  [shards(): far_b = lax.ppermute(left_a, ('x',) + y_axes, slant)]
    all_to_all x1, blocking collectives: 14 us -> 11.9 us  [shards(): lax.all_to_all(kept, 'z', split_axis=0, concat_axis=0, tiled=True)]
    ppermute x7 -> x6, waiting for transfers between devices: 8.84 us -> 7.07 us  [hop(): lax.ppermute(chunk, axis, [(i, (i + by) % size) for i in range(size)])]
  transfers between devices with their start and end apart: 10 -> 10, of which waited for: 4 -> 4; matrix products, arithmetic and copies ran while one was open for 3% -> 3% of each run, Pallas kernels for 10% -> 11%
where the time goes in v9:
time: 113 us; the launch traced here: 111 us
  starting transfers between devices  41.9 us (37%)
  blocking collectives  29.5 us (26%)
  Pallas kernels  18.6 us (16%)
  waiting for transfers between devices  12.3 us (11%)
  local copies, waits for them, and re-layouts  7.55 us (7%)
    ppermute x6, starting transfers between devices, hop(): lax.ppermute(chunk, axis, [(i, (i + by) % size) for i in range(size)])  19.5 us
    all_gather x1, blocking collectives, shards(): a = lax.all_gather(compact(got), 'quad')  17.6 us
    all_to_all x1, blocking collectives, shards(): lax.all_to_all(kept, 'z', split_axis=0, concat_axis=0, tiled=True)  11.9 us
    all_to_all x1, starting transfers between devices, shards(): got = lax.all_to_all(sent, group, split_axis=0, concat_axis=0, tiled=True)  11.8 us
    ppermute x6, waiting for transfers between devices, hop(): lax.ppermute(chunk, axis, [(i, (i + by) % size) for i in range(size)])  7.07 us
    ppermute x1, starting transfers between devices, shards(): kept = kept + lax.ppermute(passed, 'core', [(0, 1), (1, 0)])  4.77 us
    pallas_call x1, Pallas kernels, split_share(): pl.pallas_call(share_kernel, out_shape=jax.ShapeDtypeStruct((XS, 2, 512,...  4.7 us
    pallas_call x1, Pallas kernels, late_product(): pl.pallas_call(late_kernel, out_shape=(jax.ShapeDtypeStruct((PAIRS // 2,...  4.7 us
  transfers between devices with their start and end apart: 10, of which 4 were waited for; matrix products, arithmetic and copies ran while one was open for 3% of the time, Pallas kernels for 11%

profile of v9, /device:TPU:1, one launch (start us, length us, event | category | flops | bytes accessed | tf_op | source)
XLA Modules:
  0.0 111.0 jit_solution(597743746300444672)
XLA Ops:
  0.0 2.0 %encode.1 = (bf16[16,32,128]{2,1,0:T(8,128)(2,1)}, s32[16]{0:T(128)}) custom-call(s32[19]{0:T(128)} %nodes.2, f32[512]{0:T(512)} %constant.8.clone.table, bf16[96,128]{1,0:T(8,128)(2,1)} %bitcast.24), custom_call_target="tpu_custom_call" | custom-call | tf_op jit(solution)/shard_map/encode/pallas_call | solution.py:161
  2.0 11.8 %all-to-all-start = ((bf16[16,32,128]{2,1,0:T(8,128)(2,1)}), bf16[16,32,128]{2,1,0:T(8,128)(2,1)S(1)}, u32[]{:S(2)}, u32[]{:S(2)}) async-start(bf16[16,32,128]{2,1,0:T(8,128)(2,1)} %get-tuple-element.15), calls=%async_computation | async-start | bytes 262144 | tf_op jit(solution)/shard_map/all_to_all | solution.py:406
  13.9 1.6 %slice-done = bf16[1,4096,2,128]{3,2,1,0:T(2,128)(2,1)S(1)} async-done(((bf16[2,4096,2,128]{3,2,1,0:T(2,128)(2,1)}), bf16[1,4096,2,128]{3,2,1,0:T(2,128)(2,1)S(1)}, s32[]{:S(2)}) %slice-start) | async-done | bytes 2097176 | tf_op jit(solution)/shard_map/slice | solution.py:408
  15.5 3.3 %copy.11 = bf16[32,16,8,2,128]{4,3,2,0,1:T(2,128)(2,1)} copy(bf16[32,16,8,2,128]{4,3,2,1,0:T(2,128)(2,1)S(1)} %bitcast.15) | data formatting | bytes 4194304 | tf_op jit(solution)/shard_map/reshape;squeeze | solution.py:408
  18.8 4.0 %all-to-all-done.got = bf16[16,32,128]{2,1,0:T(8,128)(2,1)S(1)} async-done(((bf16[16,32,128]{2,1,0:T(8,128)(2,1)}), bf16[16,32,128]{2,1,0:T(8,128)(2,1)S(1)}, u32[]{:S(2)}, u32[]{:S(2)}) %all-to-all-start) | async-done | bytes 131104 | tf_op jit(solution)/shard_map/all_to_all | solution.py:406
  23.4 3.6 %all-to-all-start.1 = ((bf16[16,32,8,2,128]{4,3,2,1,0:T(2,128)(2,1)}), bf16[16,32,8,2,128]{4,3,2,1,0:T(2,128)(2,1)S(1)}, u32[]{:S(2)}, u32[]{:S(2)}) async-start(bf16[16,32,8,2,128]{4,3,2,1,0:T(2,128)(2,1)} %bitcast.16), calls=%async_computation.1 | async-start | bytes 4194304 | tf_op jit(solution)/shard_map/all_to_all | solution.py:410
  27.0 1.6 %compact.1 = bf16[464,128]{1,0:T(8,128)(2,1)} custom-call(bf16[16,32,128]{2,1,0:T(8,128)(2,1)} %copy-done.4), custom_call_target="tpu_custom_call" | custom-call | tf_op jit(solution)/shard_map/compact/pallas_call | solution.py:203
  28.7 17.6 %all-gather = bf16[1856,128]{1,0:T(8,128)(2,1)S(1)} all-gather(bf16[464,128]{1,0:T(8,128)(2,1)} %compact.1), channel_id=2, replica_groups=mesh['z'=8,'core'=2,'x'=4,'quad'=4,'parity'=2] {'quad'}, dimensions={0}, use_global_device_ids=true | all-gather | bytes 593920 | tf_op jit(solution)/shard_map/all_gather | solution.py:411
  46.3 4.4 %collective-permute-start.2 = (bf16[4,464,128]{2,1,0:T(8,128)(2,1)S(1)}, bf16[4,464,128]{2,1,0:T(8,128)(2,1)S(1)}, u32[]{:S(2)}, u32[]{:S(2)}) collective-permute-start(bf16[4,464,128]{2,1,0:T(8,128)(2,1)S(1)} %bitcast.17), channel_id=1, source_target_pairs={{0,24},{8,0},{16,8},{24,16},{1,25},{9,1},{17,9},{25,17},{2,26},{10... | collective-permute-start | bytes 1425416 | tf_op jit(solution)/shard_map/ppermute | solution.py:414
  50.7 1.9 %collective-permute-start.1 = (bf16[4,464,128]{2,1,0:T(8,128)(2,1)S(1)}, bf16[4,464,128]{2,1,0:T(8,128)(2,1)S(1)}, u32[]{:S(2)}, u32[]{:S(2)}) collective-permute-start(bf16[4,464,128]{2,1,0:T(8,128)(2,1)S(1)} %bitcast.18), channel_id=1, source_target_pairs={{0,8},{8,16},{16,24},{24,0},{1,9},{9,17},{17,25},{25,1},{2,10},{10... | collective-permute-start | bytes 1425416 | tf_op jit(solution)/shard_map/ppermute | solution.py:414
  52.7 1.9 %collective-permute-start = (bf16[4,464,128]{2,1,0:T(8,128)(2,1)S(1)}, bf16[4,464,128]{2,1,0:T(8,128)(2,1)}, u32[]{:S(2)}, u32[]{:S(2)}) collective-permute-start(bf16[4,464,128]{2,1,0:T(8,128)(2,1)S(1)} %bitcast.19), channel_id=1, source_target_pairs={{0,7},{1,0},{2,1},{3,2},{4,3},{5,4},{6,5},{7,6},{8,15},{9,8},{10,9... | collective-permute-start | bytes 1425416 | tf_op jit(solution)/shard_map/ppermute | solution.py:414
  54.6 5.2 %collective-permute-done.2.c3 = bf16[4,464,128]{2,1,0:T(8,128)(2,1)S(1)} collective-permute-done((bf16[4,464,128]{2,1,0:T(8,128)(2,1)S(1)}, bf16[4,464,128]{2,1,0:T(8,128)(2,1)S(1)}, u32[]{:S(2)}, u32[]{:S(2)}) %collective-permute-start.2) | collective-permute-done | bytes 475168 | tf_op jit(solution)/shard_map/ppermute | solution.py:414
  59.8 2.2 %collective-permute-start.4 = (bf16[4,464,128]{2,1,0:T(8,128)(2,1)S(1)}, bf16[4,464,128]{2,1,0:T(8,128)(2,1)}, u32[]{:S(2)}, u32[]{:S(2)}) collective-permute-start(bf16[4,464,128]{2,1,0:T(8,128)(2,1)S(1)} %collective-permute-done.2.c3), channel_id=1, source_target_pairs={{0,25},{1,26},{2,27},{3,28},{4,29},{5,30},{6,31},{7,24},{8,1},{9,2... | collective-permute-start | bytes 1425416 | tf_op jit(solution)/shard_map/ppermute | solution.py:425
  62.0 7.4 %collective-permute-start.3 = (bf16[4,464,128]{2,1,0:T(8,128)(2,1)S(1)}, bf16[4,464,128]{2,1,0:T(8,128)(2,1)}, u32[]{:S(2)}, u32[]{:S(2)}) collective-permute-start(bf16[4,464,128]{2,1,0:T(8,128)(2,1)S(1)} %collective-permute-done.2.c3), channel_id=1, source_target_pairs={{0,7},{1,0},{2,1},{3,2},{4,3},{5,4},{6,5},{7,6},{8,15},{9,8},{10,9... | collective-permute-start | bytes 1425416 | tf_op jit(solution)/shard_map/ppermute | solution.py:414
  69.4 1.9 %collective-permute-start.6 = (bf16[4,464,128]{2,1,0:T(8,128)(2,1)S(1)}, bf16[4,464,128]{2,1,0:T(8,128)(2,1)}, u32[]{:S(2)}, u32[]{:S(2)}) collective-permute-start(bf16[4,464,128]{2,1,0:T(8,128)(2,1)S(1)} %collective-permute-done.1.c2), channel_id=1, source_target_pairs={{0,1},{1,2},{2,3},{3,4},{4,5},{5,6},{6,7},{7,0},{8,9},{9,10},{10,1... | collective-permute-start | bytes 1425416 | tf_op jit(solution)/shard_map/ppermute | solution.py:414
  71.4 1.9 %collective-permute-start.5 = (bf16[4,464,128]{2,1,0:T(8,128)(2,1)S(1)}, bf16[4,464,128]{2,1,0:T(8,128)(2,1)}, u32[]{:S(2)}, u32[]{:S(2)}) collective-permute-start(bf16[4,464,128]{2,1,0:T(8,128)(2,1)S(1)} %collective-permute-done.1.c2), channel_id=1, source_target_pairs={{0,8},{8,16},{16,24},{24,0},{1,9},{9,17},{17,25},{25,1},{2,10},{10... | collective-permute-start | bytes 1425416 | tf_op jit(solution)/shard_map/ppermute | solution.py:414
  73.3 1.5 %weights.1 = f32[32,128]{1,0:T(8,128)} custom-call(s32[19]{0:T(128)} %nodes.2, s32[16]{0:T(128)} %get-tuple-element.14.picks, f32[64]{0:T(128)} %constant.9.clone.points, f32[16,128]{1,0:T(8,128)} %constant.10.clone.grid), custom_call_target="tpu_custom_call" | custom-call | tf_op jit(solution)/shard_map/weights/pallas_call | solution.py:90
  74.8 4.7 %split_share.1.share = bf16[4,2,512,256]{3,2,1,0:T(8,128)(2,1)} custom-call(s32[16]{0:T(128)} %get-tuple-element.14.picks, bf16[2,8192,128]{2,1,0:T(8,128)(2,1)} %bitcast.14), custom_call_target="tpu_custom_call" | custom-call | flops 400000000 | bytes 4200000 | tf_op jit(solution)/shard_map/split_share/pallas_call | solution.py:229
  79.6 1.3 %copy-done = bf16[16,32,8,2,128]{4,3,2,1,0:T(2,128)(2,1)} copy-done((bf16[16,32,8,2,128]{4,3,2,1,0:T(2,128)(2,1)}, bf16[16,32,8,2,128]{4,3,2,1,0:T(2,128)(2,1)S(1)}, u32[]{:S(2)}) %copy-start) | copy-done | bytes 2097176
  80.9 4.0 %early_product.1.before = f32[384,256]{1,0:T(8,128)} custom-call(s32[16]{0:T(128)} %get-tuple-element.14.picks, bf16[4,2,512,256]{3,2,1,0:T(8,128)(2,1)} %split_share.1.share, bf16[4,464,128]{2,1,0:T(8,128)(2,1)} %bitcast.20, bf16[4,464,128]{2,1,0:T(8,128)(2,1)} %collective-permute-done.c1, bf16[4,464,128]{2,1,0:T(8,128)(2,1)} %copy-done.3, ...), custom_call_target="tpu_custom_call" | custom-call | flops 400000000 | bytes 4200000 | tf_op jit(solution)/shard_map/early_product/pallas_call | solution.py:274
  84.9 1.9 %collective-permute-done.6.c7 = bf16[4,464,128]{2,1,0:T(8,128)(2,1)} collective-permute-done((bf16[4,464,128]{2,1,0:T(8,128)(2,1)S(1)}, bf16[4,464,128]{2,1,0:T(8,128)(2,1)}, u32[]{:S(2)}, u32[]{:S(2)}) %collective-permute-start.6) | collective-permute-done | bytes 475168 | tf_op jit(solution)/shard_map/ppermute | solution.py:414
  86.7 4.7 %late_product.1 = (f32[8,48,128]{2,1,0:T(8,128)}, f32[8,48,128]{2,1,0:T(8,128)}) custom-call(s32[16]{0:T(128)} %get-tuple-element.14.picks, f32[32,128]{1,0:T(8,128)} %weights.1, bf16[4,2,512,256]{3,2,1,0:T(8,128)(2,1)} %split_share.1.share, bf16[16,512,128]{2,1,0:T(8,128)(2,1)} %bitcast.13, f32[384,256]{1,0:T(8,128)} %early_product.1.before, ...), custom_call_target="tpu_custom_call" | custom-call | tf_op jit(solution)/shard_map/late_product/pallas_call | solution.py:370
  91.4 4.8 %collective-permute-start.7 = (f32[8,48,128]{2,1,0:T(8,128)}, f32[8,48,128]{2,1,0:T(8,128)S(1)}, u32[]{:S(2)}, u32[]{:S(2)}) collective-permute-start(f32[8,48,128]{2,1,0:T(8,128)} %get-tuple-element.22), channel_id=1, source_target_pairs={{0,32},{32,0},{1,33},{33,1},{2,34},{34,2},{3,35},{35,3},{4,36},{36... | collective-permute-start | bytes 589832 | tf_op jit(solution)/shard_map/ppermute | solution.py:434
  98.4 11.9 %all_to_all.15 = f32[8,48,128]{2,1,0:T(8,128)S(1)} all-to-all(f32[8,48,128]{2,1,0:T(8,128)S(1)} %add.3), channel_id=1, replica_groups=mesh['z'=8,'core'=2,'x'=4,'quad'=4,'parity'=2] {'z'}, dimensions={0} | all-to-all | bytes 393216 | tf_op jit(solution)/shard_map/all_to_all | solution.py:435
  (23 shorter events, 3.6 us)
Async XLA Ops:
  2.0 20.7 %all-to-all-start = ((bf16[16,32,128]{2,1,0:T(8,128)(2,1)}), bf16[16,32,128]{2,1,0:T(8,128)(2,1)S(1)}, u32[]{:S(2)}, u32[]{:S(2)}) async-start(bf16[16,32,128]{2,1,0:T(8,128)(2,1)} %get-tuple-element.15), calls=%async_computation | async-start | bytes 262144 | tf_op jit(solution)/shard_map/all_to_all | solution.py:406
  13.9 1.6 %slice-start = ((bf16[2,4096,2,128]{3,2,1,0:T(2,128)(2,1)}), bf16[1,4096,2,128]{3,2,1,0:T(2,128)(2,1)S(1)}, s32[]{:S(2)}) async-start(bf16[2,4096,2,128]{3,2,1,0:T(2,128)(2,1)} %param.7), calls=%async_computation.3 | async-start | bytes 4194304 | tf_op jit(solution)/shard_map/slice | solution.py:408
  22.8 0.7 copy-start.4
  23.4 56.1 %all-to-all-start.1 = ((bf16[16,32,8,2,128]{4,3,2,1,0:T(2,128)(2,1)}), bf16[16,32,8,2,128]{4,3,2,1,0:T(2,128)(2,1)S(1)}, u32[]{:S(2)}, u32[]{:S(2)}) async-start(bf16[16,32,8,2,128]{4,3,2,1,0:T(2,128)(2,1)} %bitcast.16), calls=%async_computation.1 | async-start | bytes 4194304 | tf_op jit(solution)/shard_map/all_to_all | solution.py:410
  46.3 33.2 %copy-start.1 = (bf16[1856,128]{1,0:T(8,128)(2,1)}, bf16[1856,128]{1,0:T(8,128)(2,1)S(1)}, u32[]{:S(2)}) copy-start(bf16[1856,128]{1,0:T(8,128)(2,1)S(1)} %all-gather) | copy-start | bytes 1425412
  46.3 13.4 %collective-permute-start.2 = (bf16[4,464,128]{2,1,0:T(8,128)(2,1)S(1)}, bf16[4,464,128]{2,1,0:T(8,128)(2,1)S(1)}, u32[]{:S(2)}, u32[]{:S(2)}) collective-permute-start(bf16[4,464,128]{2,1,0:T(8,128)(2,1)S(1)} %bitcast.17), channel_id=1, source_target_pairs={{0,24},{8,0},{16,8},{24,16},{1,25},{9,1},{17,9},{25,17},{2,26},{10... | collective-permute-start | bytes 1425416 | tf_op jit(solution)/shard_map/ppermute | solution.py:414
  50.7 18.7 %collective-permute-start.1 = (bf16[4,464,128]{2,1,0:T(8,128)(2,1)S(1)}, bf16[4,464,128]{2,1,0:T(8,128)(2,1)S(1)}, u32[]{:S(2)}, u32[]{:S(2)}) collective-permute-start(bf16[4,464,128]{2,1,0:T(8,128)(2,1)S(1)} %bitcast.18), channel_id=1, source_target_pairs={{0,8},{8,16},{16,24},{24,0},{1,9},{9,17},{17,25},{25,1},{2,10},{10... | collective-permute-start | bytes 1425416 | tf_op jit(solution)/shard_map/ppermute | solution.py:414
  52.7 26.9 %collective-permute-start = (bf16[4,464,128]{2,1,0:T(8,128)(2,1)S(1)}, bf16[4,464,128]{2,1,0:T(8,128)(2,1)}, u32[]{:S(2)}, u32[]{:S(2)}) collective-permute-start(bf16[4,464,128]{2,1,0:T(8,128)(2,1)S(1)} %bitcast.19), channel_id=1, source_target_pairs={{0,7},{1,0},{2,1},{3,2},{4,3},{5,4},{6,5},{7,6},{8,15},{9,8},{10,9... | collective-permute-start | bytes 1425416 | tf_op jit(solution)/shard_map/ppermute | solution.py:414
  59.8 19.8 %copy-start.2 = (bf16[4,464,128]{2,1,0:T(8,128)(2,1)}, bf16[4,464,128]{2,1,0:T(8,128)(2,1)S(1)}, u32[]{:S(2)}) copy-start(bf16[4,464,128]{2,1,0:T(8,128)(2,1)S(1)} %collective-permute-done.2.c3) | copy-start | bytes 1425412
  59.8 19.8 %collective-permute-start.4 = (bf16[4,464,128]{2,1,0:T(8,128)(2,1)S(1)}, bf16[4,464,128]{2,1,0:T(8,128)(2,1)}, u32[]{:S(2)}, u32[]{:S(2)}) collective-permute-start(bf16[4,464,128]{2,1,0:T(8,128)(2,1)S(1)} %collective-permute-done.2.c3), channel_id=1, source_target_pairs={{0,25},{1,26},{2,27},{3,28},{4,29},{5,30},{6,31},{7,24},{8,1},{9,2... | collective-permute-start | bytes 1425416 | tf_op jit(solution)/shard_map/ppermute | solution.py:425
  62.0 17.6 %collective-permute-start.3 = (bf16[4,464,128]{2,1,0:T(8,128)(2,1)S(1)}, bf16[4,464,128]{2,1,0:T(8,128)(2,1)}, u32[]{:S(2)}, u32[]{:S(2)}) collective-permute-start(bf16[4,464,128]{2,1,0:T(8,128)(2,1)S(1)} %collective-permute-done.2.c3), channel_id=1, source_target_pairs={{0,7},{1,0},{2,1},{3,2},{4,3},{5,4},{6,5},{7,6},{8,15},{9,8},{10,9... | collective-permute-start | bytes 1425416 | tf_op jit(solution)/shard_map/ppermute | solution.py:414
  69.4 10.1 %copy-start.3 = (bf16[4,464,128]{2,1,0:T(8,128)(2,1)}, bf16[4,464,128]{2,1,0:T(8,128)(2,1)S(1)}, u32[]{:S(2)}) copy-start(bf16[4,464,128]{2,1,0:T(8,128)(2,1)S(1)} %collective-permute-done.1.c2) | copy-start | bytes 1425412
  69.4 17.3 %collective-permute-start.6 = (bf16[4,464,128]{2,1,0:T(8,128)(2,1)S(1)}, bf16[4,464,128]{2,1,0:T(8,128)(2,1)}, u32[]{:S(2)}, u32[]{:S(2)}) collective-permute-start(bf16[4,464,128]{2,1,0:T(8,128)(2,1)S(1)} %collective-permute-done.1.c2), channel_id=1, source_target_pairs={{0,1},{1,2},{2,3},{3,4},{4,5},{5,6},{6,7},{7,0},{8,9},{9,10},{10,1... | collective-permute-start | bytes 1425416 | tf_op jit(solution)/shard_map/ppermute | solution.py:414
  71.4 15.4 %collective-permute-start.5 = (bf16[4,464,128]{2,1,0:T(8,128)(2,1)S(1)}, bf16[4,464,128]{2,1,0:T(8,128)(2,1)}, u32[]{:S(2)}, u32[]{:S(2)}) collective-permute-start(bf16[4,464,128]{2,1,0:T(8,128)(2,1)S(1)} %collective-permute-done.1.c2), channel_id=1, source_target_pairs={{0,8},{8,16},{16,24},{24,0},{1,9},{9,17},{17,25},{25,1},{2,10},{10... | collective-permute-start | bytes 1425416 | tf_op jit(solution)/shard_map/ppermute | solution.py:414
  79.6 1.3 %copy-start = (bf16[16,32,8,2,128]{4,3,2,1,0:T(2,128)(2,1)}, bf16[16,32,8,2,128]{4,3,2,1,0:T(2,128)(2,1)S(1)}, u32[]{:S(2)}) copy-start(bf16[16,32,8,2,128]{4,3,2,1,0:T(2,128)(2,1)S(1)} %all-to-all-done.1) | copy-start | bytes 6291460
  91.4 6.0 %collective-permute-start.7 = (f32[8,48,128]{2,1,0:T(8,128)}, f32[8,48,128]{2,1,0:T(8,128)S(1)}, u32[]{:S(2)}, u32[]{:S(2)}) collective-permute-start(f32[8,48,128]{2,1,0:T(8,128)} %get-tuple-element.22), channel_id=1, source_target_pairs={{0,32},{32,0},{1,33},{33,1},{2,34},{34,2},{3,35},{35,3},{4,36},{36... | collective-permute-start | bytes 589832 | tf_op jit(solution)/shard_map/ppermute | solution.py:434
